TPU v7x, 512 devices: a whole 4x8x8 slice. The times are simulated.
512 devices in a mesh: seq: 64 (over x, z, core), tensor: 8 (over y).
Axes of the slice: x: 4, y: 8, z: 8, core: 2. Of those that a mesh axis runs over, the one named last changes fastest.
Arguments:
- layer_input: bfloat16 [16384, 2048], P('seq', 'tensor'), may hold values from -4 to 4
- queries: bfloat16 [16384, 4096], P('seq', 'tensor'), may hold values from -160 to 160
- key_values: bfloat16 [2, 16384, 1024], P(None, 'seq', 'tensor'), may hold values from -4.5 to 4.5
- attention_out: bfloat16 [16384, 4096], P('seq', 'tensor'), may hold values from -6 to 6
- output_grad: bfloat16 [16384, 4096], P('seq', 'tensor'), may hold values from -24 to 24
- document_start: int32 [16384], P('seq'), may hold values from 0 to 16383, as said below
Outputs:
- query_grad: bfloat16 [16384, 4096], P('seq', 'tensor')
- key_value_grad: bfloat16 [2, 16384, 1024], P(None, 'seq', 'tensor')
- query_weight_grad: float32 [2048, 4096], P('seq', 'tensor')
Inputs may be any that keep to these rules, and one draw needn't show every extreme that they name: Non-decreasing; entry i is the position of the first token of token i's document, so i - 512 < document_start[i] <= i and document_start[document_start[i]] = document_start[i]; some token lies exactly 511 positions after its document's first token.
All inputs are finite; a program needn't handle non-finite values.
Results may differ from a plain program's by a relative error of at most 0.008.
Values may be sent and summed in bfloat16 or wider, within the bound.
No kernel may reach another device: no remote copies, remote signals or barrier semaphores. Data moves between devices by JAX's collectives and lax.ppermute only.
A program may use at most 64 MiB of HBM per device.

v0:
```python
import math

import jax
import jax.numpy as jnp
from jax import lax
from jax.sharding import PartitionSpec as P

HEADS = 32
KV_HEADS = 8
HD = 128
REACH = 2


def joined_along(parts, dim):
    parts = jnp.moveaxis(parts, 0, dim)
    shape = parts.shape
    return parts.reshape(*shape[:dim], shape[dim] * shape[dim + 1], *shape[dim + 2 :])


def from_everyone(shard, axis):
    copies = jnp.broadcast_to(shard, (lax.axis_size(axis), *shard.shape))
    return lax.all_to_all(copies, axis, split_axis=0, concat_axis=0, tiled=True)


def collect(shard, axis, dim):
    return joined_along(from_everyone(shard, axis), dim)


def passed_along(shard, axis, by):
    size = lax.axis_size(axis)
    pairs = [(i, i + by) for i in range(size) if 0 <= i + by < size]
    return lax.ppermute(shard, axis, pairs)


def cut_along(shard, dim, size):
    shape = shard.shape
    parts = shard.reshape(*shape[:dim], size, shape[dim] // size, *shape[dim + 1 :])
    return jnp.moveaxis(parts, dim, 0)


def sent_and_summed(shard, axis, dim):
    parts = cut_along(shard, dim, lax.axis_size(axis))
    arrived = lax.all_to_all(parts, axis, split_axis=0, concat_axis=0, tiled=True)
    return arrived.astype(jnp.float32).sum(axis=0)


def block_scores(query_heads, key_heads, query_pos, key_pos, starts, scaling):
    scores = (
        jnp.einsum("igrd,jgd->grij", query_heads, key_heads, preferred_element_type=jnp.float32)
        * scaling
    )
    allowed = (key_pos[None, :] >= starts[:, None]) & (key_pos[None, :] <= query_pos[:, None])
    return jnp.where(allowed, scores, -jnp.inf)


def shards(layer_input, queries, key_values, attention_out, output_grad, document_start):
    tok_rows = queries.shape[0]
    groups = key_values.shape[2] // HD
    repeat = HEADS // KV_HEADS
    scaling = 1.0 / math.sqrt(HD)
    shard_index = lax.axis_index("seq")
    features = collect(layer_input, "tensor", 1)
    offsets = jnp.arange(tok_rows, dtype=jnp.int32)
    query_pos = shard_index * tok_rows + offsets
    query_heads = queries.reshape(tok_rows, groups, repeat, HD)
    grad_heads = output_grad.reshape(tok_rows, groups, repeat, HD)
    output_heads = attention_out.reshape(tok_rows, groups, repeat, HD)
    row_delta = jnp.sum(
        grad_heads.astype(jnp.float32) * output_heads.astype(jnp.float32), axis=3
    ).transpose(1, 2, 0)
    fetched = [key_values]
    for distance in range(1, REACH + 1):
        fetched.append(passed_along(key_values, "seq", distance))

    def key_positions(distance):
        return (shard_index - distance) * tok_rows + offsets

    def statistics(distance, running):
        row_max, row_sum = running
        key_heads = fetched[distance][0].reshape(tok_rows, groups, HD)
        scores = block_scores(
            query_heads, key_heads, query_pos, key_positions(distance), document_start, scaling
        )
        new_max = jnp.maximum(row_max, jnp.max(scores, axis=3))
        row_sum = row_sum * jnp.exp(row_max - new_max) + jnp.sum(
            jnp.exp(scores - new_max[..., None]), axis=3
        )
        return (new_max, row_sum)

    running = (
        jnp.full((groups, repeat, tok_rows), -jnp.inf, jnp.float32),
        jnp.zeros((groups, repeat, tok_rows), jnp.float32),
    )
    running = statistics(0, running)
    for distance in range(1, REACH + 1):
        running = statistics(distance, running)
    log_total = running[0] + jnp.log(running[1])

    def block_grads(distance):
        key_heads = fetched[distance][0].reshape(tok_rows, groups, HD)
        value_heads = fetched[distance][1].reshape(tok_rows, groups, HD)
        scores = block_scores(
            query_heads, key_heads, query_pos, key_positions(distance), document_start, scaling
        )
        weights = jnp.exp(scores - log_total[..., None])
        weights_half = weights.astype(jnp.bfloat16)
        value_part = jnp.einsum(
            "grij,igrd->jgd", weights_half, grad_heads, preferred_element_type=jnp.float32
        )
        dot_grad = jnp.einsum(
            "igrd,jgd->grij", grad_heads, value_heads, preferred_element_type=jnp.float32
        )
        score_grad = (weights * (dot_grad - row_delta[..., None]) * scaling).astype(jnp.bfloat16)
        query_part = jnp.einsum(
            "grij,jgd->igrd", score_grad, key_heads, preferred_element_type=jnp.float32
        )
        key_part = jnp.einsum(
            "grij,igrd->jgd", score_grad, query_heads, preferred_element_type=jnp.float32
        )
        stacked = jnp.stack(
            (key_part.reshape(tok_rows, groups * HD), value_part.reshape(tok_rows, groups * HD))
        )
        return (query_part.reshape(tok_rows, groups * repeat * HD), stacked)

    query_total, local_part = block_grads(0)
    partials = [local_part]
    for distance in range(1, REACH + 1):
        query_piece, pair_piece = block_grads(distance)
        query_total = query_total + query_piece
        partials.append(pair_piece)
    pair_total = partials[0]
    for distance in range(1, REACH + 1):
        pair_total = pair_total + passed_along(
            partials[distance].astype(jnp.bfloat16), "seq", -distance
        ).astype(jnp.float32)
    query_half = query_total.astype(jnp.bfloat16)
    weight_grad = sent_and_summed(
        jnp.einsum("tf,tc->fc", features, query_half, preferred_element_type=jnp.float32).astype(
            jnp.bfloat16
        ),
        "seq",
        0,
    )
    return (query_half, pair_total.astype(jnp.bfloat16), weight_grad)


def solution(mesh):
    placed = (
        P("seq", "tensor"),
        P("seq", "tensor"),
        P(None, "seq", "tensor"),
        P("seq", "tensor"),
        P("seq", "tensor"),
        P("seq"),
    )
    return jax.shard_map(
        shards,
        mesh=mesh,
        in_specs=placed,
        out_specs=(P("seq", "tensor"), P(None, "seq", "tensor"), P("seq", "tensor")),
        check_vma=False,
    )
```

profile of v0, /device:TPU:1, one launch (start us, length us, event | category | flops | bytes accessed | tf_op | source)
XLA Modules:
  0.0 122.5 jit_solution(15754587663549069127)
XLA Ops:
  0.6 0.0 copy-start
  0.6 0.0 copy-start.1
  0.7 0.0 copy-start.14
  0.7 5.5 %collective-permute-start = (bf16[2,256,128]{2,1,0:T(8,128)(2,1)}, bf16[2,256,128]{2,1,0:T(8,128)(2,1)S(1)}, u32[]{:S(2)}, u32[]{:S(2)}) collective-permute-start(bf16[2,256,128]{2,1,0:T(8,128)(2,1)} %param.8), channel_id=1, source_target_pairs={{0,8},{8,16},{16,24},{24,32},{32,40},{40,48},{48,56},{56,64},{64,7... | collective-permute-start | bytes 393224 | tf_op jit(solution)/shard_map/ppermute | solution.py:32
  6.2 4.0 %collective-permute-start.1 = (bf16[2,256,128]{2,1,0:T(8,128)(2,1)}, bf16[2,256,128]{2,1,0:T(8,128)(2,1)S(1)}, u32[]{:S(2)}, u32[]{:S(2)}) collective-permute-start(bf16[2,256,128]{2,1,0:T(8,128)(2,1)} %param.8), channel_id=1, source_target_pairs={{0,16},{8,24},{16,32},{24,40},{32,48},{40,56},{48,64},{56,72},{64,... | collective-permute-start | bytes 393224 | tf_op jit(solution)/shard_map/ppermute | solution.py:32
  10.2 1.0 copy.68
  11.2 1.1 broadcast_in_dim.34
  12.3 7.0 %all-to-all-start = ((bf16[8,256,256]{1,2,0:T(8,128)(2,1)}), bf16[8,256,256]{1,2,0:T(8,128)(2,1)}, u32[]{:S(2)}, u32[]{:S(2)}) async-start(bf16[8,256,256]{1,2,0:T(8,128)(2,1)} %broadcast_in_dim.34), calls=%async_computation | async-start | bytes 2097152 | tf_op jit(solution)/shard_map/all_to_all | solution.py:22
  19.3 0.0 copy-done.1
  19.3 0.0 copy-done.14
  19.3 0.1 convert_multiply_fusion
  19.4 0.2 mul.108
  19.6 0.3 reduce_sum.50
  19.9 0.1 copy.53
  20.0 0.0 copy-done.15
  20.0 0.2 compare_and_fusion.1
  20.2 0.0 copy-done
  20.2 0.0 copy-done.9
  20.3 0.3 fusion.78
  20.6 0.2 exponential_reduce_fusion.2
  20.7 0.0 collective-permute-done
  20.7 0.0 copy-start.10
  20.8 0.3 fusion.79
  21.1 0.0 copy-start.2
  21.1 0.0 collective-permute-done.1
  21.1 0.3 copy-done.10
  21.4 0.7 copy-done.12
  22.1 1.2 fusion.77
  23.2 0.0 copy-start.11
  23.2 0.2 exponential_reduce_fusion
  23.4 0.2 exponential_reduce_fusion.1
  23.6 0.0 copy-start.13
  23.6 0.0 copy-done.2
  23.6 0.3 fusion.19
  24.0 0.2 copy-done.11
  24.1 0.3 fusion.20
  24.5 0.0 copy-done.13
  24.5 0.3 fusion.21
  24.8 0.0 copy-start.8
  24.9 0.3 fusion.70
  25.1 0.0 copy-done.4
  25.1 0.3 convolution_add_fusion.1
  25.4 0.0 copy-done.6
  25.4 0.2 copy-done.8
  25.7 1.0 fusion.22
  26.6 21.0 %all-to-all-done = bf16[8,256,256]{1,2,0:T(8,128)(2,1)} async-done(((bf16[8,256,256]{1,2,0:T(8,128)(2,1)}), bf16[8,256,256]{1,2,0:T(8,128)(2,1)}, u32[]{:S(2)}, u32[]{:S(2)}) %all-to-all-start) | async-done | bytes 1048608 | tf_op jit(solution)/shard_map/all_to_all | solution.py:22
  47.6 3.4 %fusion = bf16[2048,512]{0,1:T(8,128)(2,1)} fusion(bf16[256,512]{0,1:T(8,128)(2,1)} %bitcast.288, bf16[256,2048]{0,1:T(8,128)(2,1)} %bitcast.74), kind=kOutput, calls=%fused_computation.2 | convolution fusion | flops 537919488 | bytes 3407872 | tf_op jit(solution)/shard_map/tf,tc->fc/dot_general | solution.py:138
  51.0 3.9 %copy.69 = bf16[2048,512]{1,0:T(8,128)(2,1)} copy(bf16[2048,512]{0,1:T(8,128)(2,1)} %fusion) | data formatting | bytes 4194304 | tf_op jit(solution)/shard_map/convert_element_type | solution.py:138
  54.9 13.2 %all-to-all-start.1 = ((bf16[64,32,512]{2,1,0:T(8,128)(2,1)}), bf16[64,32,512]{2,1,0:T(8,128)(2,1)}, u32[]{:S(2)}, u32[]{:S(2)}) async-start(bf16[64,32,512]{2,1,0:T(8,128)(2,1)} %bitcast.287), calls=%async_computation.1 | async-start | bytes 4194304 | tf_op jit(solution)/shard_map/all_to_all | solution.py:43
  68.2 1.8 %copy.70 = bf16[256,512]{1,0:T(8,128)(2,1)} copy(bf16[256,512]{0,1:T(8,128)(2,1)} %bitcast.289) | data formatting | bytes 524288
  70.0 1.4 %fusion.28 = bf16[1,256,128]{2,1,0:T(8,128)(2,1)S(1)} fusion(bf16[4,256,256]{1,2,0:T(8,128)(2,1)} %copy-done.8, bf16[256,512]{1,0:T(8,128)(2,1)S(1)} %copy-done), kind=kOutput, calls=%fused_computation.44 | convolution fusion | flops 67141632 | bytes 851968 | tf_op jit(solution)/shard_map/grij,igrd->jgd/dot_general | solution.py:117
  71.4 1.2 %fusion.27 = bf16[1,256,128]{2,1,0:T(8,128)(2,1)S(1)} fusion(f32[1,4,256,256]{2,3,1,0:T(8,128)S(1)} %get-tuple-element.18, f32[4,256]{1,0:T(4,128)S(1)} %log_add_fusion, bf16[256,512]{1,0:T(8,128)(2,1)} %param.10), kind=kOutput, calls=%fused_computation.43 | convolution fusion | flops 67665920 | bytes 1380352 | tf_op jit(solution)/shard_map/grij,igrd->jgd/dot_general | solution.py:107
  72.6 1.4 %collective-permute-start.3 = (bf16[2,256,128]{2,1,0:T(8,128)(2,1)S(1)}, bf16[2,256,128]{2,1,0:T(8,128)(2,1)S(1)}, u32[]{:S(2)}, u32[]{:S(2)}) collective-permute-start(bf16[2,256,128]{2,1,0:T(8,128)(2,1)S(1)} %pad_maximum_fusion.1), channel_id=1, source_target_pairs={{16,0},{24,8},{32,16},{40,24},{48,32},{56,40},{64,48},{72,56},{80,... | collective-permute-start | bytes 393224 | tf_op jit(solution)/shard_map/ppermute | solution.py:32
  74.1 0.0 copy-done.7
  74.1 0.3 fusion.30
  74.4 0.3 fusion.29
  74.7 2.4 %collective-permute-start.2 = (bf16[2,256,128]{2,1,0:T(8,128)(2,1)S(1)}, bf16[2,256,128]{2,1,0:T(8,128)(2,1)S(1)}, u32[]{:S(2)}, u32[]{:S(2)}) collective-permute-start(bf16[2,256,128]{2,1,0:T(8,128)(2,1)S(1)} %pad_maximum_fusion), channel_id=1, source_target_pairs={{8,0},{16,8},{24,16},{32,24},{40,32},{48,40},{56,48},{64,56},{72,6... | collective-permute-start | bytes 393224 | tf_op jit(solution)/shard_map/ppermute | solution.py:32
  77.2 0.3 convolution_bitcast_fusion.7
  77.5 0.3 convolution_bitcast_fusion.8
  77.8 39.9 %collective-permute-done.3 = bf16[2,256,128]{2,1,0:T(8,128)(2,1)S(1)} collective-permute-done((bf16[2,256,128]{2,1,0:T(8,128)(2,1)S(1)}, bf16[2,256,128]{2,1,0:T(8,128)(2,1)S(1)}, u32[]{:S(2)}, u32[]{:S(2)}) %collective-permute-start.3) | collective-permute-done | bytes 131104 | tf_op jit(solution)/shard_map/ppermute | solution.py:32
  117.7 1.6 %collective-permute-done.2 = bf16[2,256,128]{2,1,0:T(8,128)(2,1)S(1)} collective-permute-done((bf16[2,256,128]{2,1,0:T(8,128)(2,1)S(1)}, bf16[2,256,128]{2,1,0:T(8,128)(2,1)S(1)}, u32[]{:S(2)}, u32[]{:S(2)}) %collective-permute-start.2) | collective-permute-done | bytes 131104 | tf_op jit(solution)/shard_map/ppermute | solution.py:32
  119.3 0.7 fusion.56
  120.0 0.0 all-to-all-done.1
  120.0 2.5 %convert_reduce_fusion = f32[32,512]{1,0:T(8,128)} fusion(bf16[64,32,512]{2,1,0:T(8,128)(2,1)} %all-to-all-done.1), kind=kLoop, calls=%fused_computation | loop fusion | flops 2080768 | bytes 2162688 | tf_op jit(solution)/shard_map/reduce_sum | solution.py:44
  (16 shorter events, 0.1 us)
Async XLA Ops:
  0.6 19.6 %copy-start = (bf16[256,512]{1,0:T(8,128)(2,1)S(1)}, bf16[256,512]{1,0:T(8,128)(2,1)}, u32[]{:S(2)}) copy-start(bf16[256,512]{1,0:T(8,128)(2,1)} %param.7) | copy-start | bytes 786436
  0.6 18.6 %copy-start.1 = (bf16[256,512]{1,0:T(8,128)(2,1)S(1)}, bf16[256,512]{1,0:T(8,128)(2,1)}, u32[]{:S(2)}) copy-start(bf16[256,512]{1,0:T(8,128)(2,1)} %param.10) | copy-start | bytes 786436
  0.7 18.6 %copy-start.14 = (bf16[256,512]{1,0:T(8,128)(2,1)S(1)}, bf16[256,512]{1,0:T(8,128)(2,1)}, u32[]{:S(2)}) copy-start(bf16[256,512]{1,0:T(8,128)(2,1)} %param.9) | copy-start | bytes 786436
  0.7 20.1 %collective-permute-start = (bf16[2,256,128]{2,1,0:T(8,128)(2,1)}, bf16[2,256,128]{2,1,0:T(8,128)(2,1)S(1)}, u32[]{:S(2)}, u32[]{:S(2)}) collective-permute-start(bf16[2,256,128]{2,1,0:T(8,128)(2,1)} %param.8), channel_id=1, source_target_pairs={{0,8},{8,16},{16,24},{24,32},{32,40},{40,48},{48,56},{56,64},{64,7... | collective-permute-start | bytes 393224 | tf_op jit(solution)/shard_map/ppermute | solution.py:32
  6.2 14.9 %collective-permute-start.1 = (bf16[2,256,128]{2,1,0:T(8,128)(2,1)}, bf16[2,256,128]{2,1,0:T(8,128)(2,1)S(1)}, u32[]{:S(2)}, u32[]{:S(2)}) collective-permute-start(bf16[2,256,128]{2,1,0:T(8,128)(2,1)} %param.8), channel_id=1, source_target_pairs={{0,16},{8,24},{16,32},{24,40},{32,48},{40,56},{48,64},{56,72},{64,... | collective-permute-start | bytes 393224 | tf_op jit(solution)/shard_map/ppermute | solution.py:32
  12.3 7.7 %copy-start.15 = (s32[256]{0:T(256)S(1)}, s32[256]{0:T(256)}, u32[]{:S(2)}) copy-start(s32[256]{0:T(256)} %param.11) | copy-start | bytes 3076
  12.3 7.9 %copy-start.9 = (bf16[2,256,128]{2,1,0:T(8,128)(2,1)S(1)}, bf16[2,256,128]{2,1,0:T(8,128)(2,1)}, u32[]{:S(2)}) copy-start(bf16[2,256,128]{2,1,0:T(8,128)(2,1)} %param.8) | copy-start | bytes 393220
  12.3 35.3 %all-to-all-start = ((bf16[8,256,256]{1,2,0:T(8,128)(2,1)}), bf16[8,256,256]{1,2,0:T(8,128)(2,1)}, u32[]{:S(2)}, u32[]{:S(2)}) async-start(bf16[8,256,256]{1,2,0:T(8,128)(2,1)} %broadcast_in_dim.34), calls=%async_computation | async-start | bytes 2097152 | tf_op jit(solution)/shard_map/all_to_all | solution.py:22
  20.7 0.7 copy-start.10
  21.1 2.5 %copy-start.2 = (bf16[256,512]{1,0:T(8,128)(2,1)S(1)}, bf16[256,512]{1,0:T(8,128)(2,1)}, u32[]{:S(2)}) copy-start(bf16[256,512]{1,0:T(8,128)(2,1)} %param.10) | copy-start | bytes 786436
  21.4 0.7 copy-start.12
  23.2 0.9 copy-start.11
  23.6 0.9 copy-start.13
  24.1 1.0 copy-start.4
  24.5 0.9 copy-start.6
  24.8 0.8 copy-start.8
  54.9 65.1 %all-to-all-start.1 = ((bf16[64,32,512]{2,1,0:T(8,128)(2,1)}), bf16[64,32,512]{2,1,0:T(8,128)(2,1)}, u32[]{:S(2)}, u32[]{:S(2)}) async-start(bf16[64,32,512]{2,1,0:T(8,128)(2,1)} %bitcast.287), calls=%async_computation.1 | async-start | bytes 4194304 | tf_op jit(solution)/shard_map/all_to_all | solution.py:43
  69.9 4.1 %copy-start.7 = (bf16[4,256,256]{1,2,0:T(8,128)(2,1)S(1)}, bf16[4,256,256]{1,2,0:T(8,128)(2,1)}, u32[]{:S(2)}) copy-start(bf16[4,256,256]{1,2,0:T(8,128)(2,1)} %copy-done.6) | copy-start | bytes 1572868
  70.0 4.4 %copy-start.3 = (bf16[256,512]{1,0:T(8,128)(2,1)S(1)}, bf16[256,512]{1,0:T(8,128)(2,1)}, u32[]{:S(2)}) copy-start(bf16[256,512]{1,0:T(8,128)(2,1)} %param.10) | copy-start | bytes 786436
  72.6 4.9 %copy-start.5 = (bf16[4,256,256]{1,2,0:T(8,128)(2,1)S(1)}, bf16[4,256,256]{1,2,0:T(8,128)(2,1)}, u32[]{:S(2)}) copy-start(bf16[4,256,256]{1,2,0:T(8,128)(2,1)} %copy-done.4) | copy-start | bytes 1572868
  72.6 45.0 %collective-permute-start.3 = (bf16[2,256,128]{2,1,0:T(8,128)(2,1)S(1)}, bf16[2,256,128]{2,1,0:T(8,128)(2,1)S(1)}, u32[]{:S(2)}, u32[]{:S(2)}) collective-permute-start(bf16[2,256,128]{2,1,0:T(8,128)(2,1)S(1)} %pad_maximum_fusion.1), channel_id=1, source_target_pairs={{16,0},{24,8},{32,16},{40,24},{48,32},{56,40},{64,48},{72,56},{80,... | collective-permute-start | bytes 393224 | tf_op jit(solution)/shard_map/ppermute | solution.py:32
  74.7 44.6 %collective-permute-start.2 = (bf16[2,256,128]{2,1,0:T(8,128)(2,1)S(1)}, bf16[2,256,128]{2,1,0:T(8,128)(2,1)S(1)}, u32[]{:S(2)}, u32[]{:S(2)}) collective-permute-start(bf16[2,256,128]{2,1,0:T(8,128)(2,1)S(1)} %pad_maximum_fusion), channel_id=1, source_target_pairs={{8,0},{16,8},{24,16},{32,24},{40,32},{48,40},{56,48},{64,56},{72,6... | collective-permute-start | bytes 393224 | tf_op jit(solution)/shard_map/ppermute | solution.py:32
where the time goes:
time: 123 us
  waiting for transfers between devices  62.5 us (51%)
  starting transfers between devices  33.5 us (27%)
  matrix products  11.5 us (9%)
  local copies, waits for them, and re-layouts  9.52 us (8%)
  other arithmetic  4.45 us (4%)
    ppermute x4, waiting for transfers between devices, passed_along(): return lax.ppermute(shard, axis, pairs)  41.5 us
    all_to_all x1, waiting for transfers between devices, from_everyone(): return lax.all_to_all(copies, axis, split_axis=0, concat_axis=0, tiled=True)  21 us
    ppermute x4, starting transfers between devices, passed_along(): return lax.ppermute(shard, axis, pairs)  13.4 us
    all_to_all x1, starting transfers between devices, sent_and_summed(): lax.all_to_all(parts, axis, split_axis=0, concat_axis=0, tiled=True)  13.2 us
    all_to_all x1, starting transfers between devices, from_everyone(): return lax.all_to_all(copies, axis, split_axis=0, concat_axis=0, tiled=True)  6.95 us
    unnamed x34, local copies, waits for them, and re-layouts  4.23 us
    convert_element_type x1, local copies, waits for them, and re-layouts, shards(): jnp.einsum('tf,tc->fc', features, query_half, preferred_element_type=jnp....  3.92 us
    dot_general x1, matrix products, shards(): jnp.einsum('tf,tc->fc', features, query_half, preferred_element_type=jnp....  3.37 us
  transfers between devices with their start and end apart: 6, of which 3 were waited for; matrix products, arithmetic and copies ran while one was open for 12% of the time, Pallas kernels for 0%

commit v1 on v0

v1 whole, which is shorter than its diff:
```python
import math

import jax
import jax.numpy as jnp
from jax import lax
from jax.experimental import pallas as pl
from jax.experimental.pallas import tpu as pltpu
from jax.sharding import Mesh, PartitionSpec as P

HD = 128
REACH = 2
SEQ = ("x", "z", "c")
XS, ZS, CS, YS = 4, 8, 2, 8


def moved(shard, axis, size, by, wrap):
    pairs = [(i, (i + by) % size) for i in range(size) if wrap or 0 <= i + by < size]
    return lax.ppermute(shard, axis, pairs)


def dot(a, b, ca, cb):
    return lax.dot_general(a, b, (((ca,), (cb,)), ((), ())), preferred_element_type=jnp.float32)


def attention_backward(queries, attention_out, output_grad, document_start, near, one, two):
    rows = queries.shape[0]
    heads = queries.shape[1] // HD
    span = rows * (REACH + 1)
    scaling = 1.0 / math.sqrt(HD)

    def body(starts, q_ref, o_ref, g_ref, near_ref, one_ref, two_ref, dq_ref, own_ref, d1_ref, d2_ref, acc):
        head = pl.program_id(0)
        first = lax.axis_index(SEQ) * rows - REACH * rows
        q = q_ref[...]
        g = g_ref[...]
        keys = jnp.concatenate([two_ref[0], one_ref[0], near_ref[0]], axis=0)
        values = jnp.concatenate([two_ref[1], one_ref[1], near_ref[1]], axis=0)
        key_at = lax.broadcasted_iota(jnp.int32, (span, rows), 0)
        query_at = lax.broadcasted_iota(jnp.int32, (1, rows), 1) + REACH * rows
        allowed = (key_at >= starts[...] - first) & (key_at <= query_at)
        scores = jnp.where(allowed, dot(keys, q, 1, 1) * scaling, -jnp.inf)
        row_max = jnp.max(scores, axis=0, keepdims=True)
        powers = jnp.exp(scores - row_max)
        weights = powers * (1.0 / jnp.sum(powers, axis=0, keepdims=True))
        product = g.astype(jnp.float32) * o_ref[...].astype(jnp.float32)
        delta = jnp.sum(product.T, axis=0, keepdims=True)
        dot_grad = dot(values, g, 1, 1)
        score_grad = (weights * (dot_grad - delta) * scaling).astype(jnp.bfloat16)
        value_part = dot(weights.astype(jnp.bfloat16), g, 1, 0)
        key_part = dot(score_grad, q, 1, 0)
        dq_ref[...] = dot(keys, score_grad, 0, 0).T.astype(jnp.bfloat16)

        @pl.when(head == 0)
        def _():
            acc[0] = key_part
            acc[1] = value_part

        @pl.when(head > 0)
        def _():
            acc[0] += key_part
            acc[1] += value_part

        @pl.when(head == heads - 1)
        def _():
            d2_ref[...] = acc[:, :rows].astype(jnp.bfloat16)
            d1_ref[...] = acc[:, rows : 2 * rows].astype(jnp.bfloat16)
            own_ref[...] = acc[:, 2 * rows :]

    by_head = pl.BlockSpec((rows, HD), lambda h: (0, h))
    pair = pl.BlockSpec((2, rows, HD), lambda h: (0, 0, 0))
    return pl.pallas_call(
        body,
        grid=(heads,),
        in_specs=[pl.BlockSpec((1, rows), lambda h: (0, 0)), by_head, by_head, by_head, pair, pair, pair],
        out_specs=[by_head, pair, pair, pair],
        out_shape=[
            jax.ShapeDtypeStruct(queries.shape, jnp.bfloat16),
            jax.ShapeDtypeStruct((2, rows, HD), jnp.float32),
            jax.ShapeDtypeStruct((2, rows, HD), jnp.bfloat16),
            jax.ShapeDtypeStruct((2, rows, HD), jnp.bfloat16),
        ],
        scratch_shapes=[pltpu.VMEM((2, span, HD), jnp.float32)],
        name="attention_backward",
    )(document_start.reshape(1, rows), queries, attention_out, output_grad, near, one, two)


def weight_parts(pieces, query_grad):
    tokens, width = pieces[0].shape
    columns = query_grad.shape[1]
    owners = width // 64

    def body(*refs):
        shards, dq_ref, keep_ref, send_ref = refs[:YS], refs[YS], refs[YS + 1], refs[YS + 2]
        y = lax.axis_index("y")
        first_core = lax.axis_index("c") == 0
        dq = dq_ref[...]
        for d in range(YS):
            term = dot(shards[d][...], dq, 0, 0).astype(jnp.bfloat16).reshape(owners, 2, 32, columns)
            at = lax.rem(y + YS - d, YS) * owners
            keep_ref[pl.ds(at, owners)] = jnp.where(first_core, term[:, 0], term[:, 1])
            send_ref[pl.ds(at, owners)] = jnp.where(first_core, term[:, 1], term[:, 0])

    shape = jax.ShapeDtypeStruct((YS * owners, 32, columns), jnp.bfloat16)
    return pl.pallas_call(body, out_shape=[shape, shape], name="weight_parts")(*pieces, query_grad)


def shards(layer_input, queries, key_values, attention_out, output_grad, document_start):
    pieces = [layer_input] + [None] * (YS - 1)
    forward = backward = layer_input
    one = two = None
    for step in range(1, YS // 2 + 1):
        forward = moved(forward, "y", YS, 1, True)
        pieces[step] = forward
        if step < YS // 2:
            backward = moved(backward, "y", YS, -1, True)
            pieces[YS - step] = backward
        if step == 1:
            one = moved(key_values, SEQ, XS * ZS * CS, 1, False)
            two = moved(key_values, SEQ, XS * ZS * CS, 2, False)
    query_grad, own, part_one, part_two = attention_backward(
        queries, attention_out, output_grad, document_start, key_values, one, two
    )
    keep, send = weight_parts(pieces, query_grad)
    summed = keep + lax.ppermute(send, "c", [(0, 1), (1, 0)])
    arrived = lax.all_to_all(summed, ("x", "z"), split_axis=0, concat_axis=0, tiled=True)
    back_one = moved(part_one, SEQ, XS * ZS * CS, -1, False)
    back_two = moved(part_two, SEQ, XS * ZS * CS, -2, False)
    pair_total = own + back_one.astype(jnp.float32) + back_two.astype(jnp.float32)
    weight_grad = arrived.astype(jnp.float32).sum(axis=0)
    return query_grad, pair_total.astype(jnp.bfloat16), weight_grad


def solution(mesh):
    split = Mesh(mesh.devices.reshape(XS, ZS, CS, YS), SEQ + ("y",))
    placed = (
        P(SEQ, "y"),
        P(SEQ, "y"),
        P(None, SEQ, "y"),
        P(SEQ, "y"),
        P(SEQ, "y"),
        P(SEQ),
    )
    return jax.shard_map(
        shards,
        mesh=split,
        in_specs=placed,
        out_specs=(P(SEQ, "y"), P(None, SEQ, "y"), P(SEQ, "y")),
        check_vma=False,
    )
```

time: 123 us -> 98.7 us (0.80)
  the two profiles are of different devices: /device:TPU:1 before, /device:TPU:24 now
where the time goes in v1:
time: 98.7 us; the launch traced here: 98.1 us
  starting transfers between devices  50.4 us (51%)
  waiting for transfers between devices  30.8 us (31%)
  Pallas kernels  10.5 us (11%)
  other arithmetic  4.07 us (4%)
  local copies, waits for them, and re-layouts  1.31 us (1%)
    ppermute x11, starting transfers between devices, moved(): return lax.ppermute(shard, axis, pairs)  35.4 us
    ppermute x11, waiting for transfers between devices, moved(): return lax.ppermute(shard, axis, pairs)  28.3 us
    all_to_all x1, starting transfers between devices, shards(): lax.all_to_all(summed, ('x', 'z'), split_axis=0, concat_axis=0, tiled=True)  11.5 us
    pallas_call x1, Pallas kernels, attention_backward(): pl.pallas_call(body, grid=(heads,), in_specs=[pl.BlockSpec((1, rows), lam...  7.07 us
    ppermute x1, starting transfers between devices, shards(): summed = keep + lax.ppermute(send, 'c', [(0, 1), (1, 0)])  3.53 us
    pallas_call x1, Pallas kernels, weight_parts(): pl.pallas_call(body, out_shape=[shape, shape], name='weight_parts')  3.44 us
    add x1, other arithmetic, shards(): summed = keep + lax.ppermute(send, 'c', [(0, 1), (1, 0)])  2.58 us
    ppermute x1, waiting for transfers between devices, shards(): summed = keep + lax.ppermute(send, 'c', [(0, 1), (1, 0)])  2.48 us
  transfers between devices with their start and end apart: 13, of which 5 were waited for; matrix products, arithmetic and copies ran while one was open for 1% of the time, Pallas kernels for 7%

profile of v1, /device:TPU:24, one launch (start us, length us, event | category | flops | bytes accessed | tf_op | source)
XLA Modules:
  0.0 98.1 jit_solution(7888984745084943721)
XLA Ops:
  0.6 4.7 %collective-permute-start.4 = (bf16[256,256]{1,0:T(8,128)(2,1)}, bf16[256,256]{1,0:T(8,128)(2,1)S(1)}, u32[]{:S(2)}, u32[]{:S(2)}) collective-permute-start(bf16[256,256]{1,0:T(8,128)(2,1)} %refs_0_.1), channel_id=1, source_target_pairs={{0,1},{1,2},{2,3},{3,4},{4,5},{5,6},{6,7},{7,0},{8,9},{9,10},{10,1... | collective-permute-start | bytes 393224 | tf_op jit(solution)/shard_map/ppermute | solution.py:18
  5.3 1.9 %collective-permute-start.8 = (bf16[256,256]{1,0:T(8,128)(2,1)}, bf16[256,256]{1,0:T(8,128)(2,1)S(1)}, u32[]{:S(2)}, u32[]{:S(2)}) collective-permute-start(bf16[256,256]{1,0:T(8,128)(2,1)} %refs_0_.1), channel_id=1, source_target_pairs={{0,7},{1,0},{2,1},{3,2},{4,3},{5,4},{6,5},{7,6},{8,15},{9,8},{10,9... | collective-permute-start | bytes 393224 | tf_op jit(solution)/shard_map/ppermute | solution.py:18
  7.3 1.1 %collective-permute-done.4.refs_1_ = bf16[256,256]{1,0:T(8,128)(2,1)S(1)} collective-permute-done((bf16[256,256]{1,0:T(8,128)(2,1)}, bf16[256,256]{1,0:T(8,128)(2,1)S(1)}, u32[]{:S(2)}, u32[]{:S(2)}) %collective-permute-start.4) | collective-permute-done | bytes 131104 | tf_op jit(solution)/shard_map/ppermute | solution.py:18
  8.4 0.0 copy-start.1
  8.4 5.5 %collective-permute-start.5 = (bf16[256,256]{1,0:T(8,128)(2,1)S(1)}, bf16[256,256]{1,0:T(8,128)(2,1)S(1)}, u32[]{:S(2)}, u32[]{:S(2)}) collective-permute-start(bf16[256,256]{1,0:T(8,128)(2,1)S(1)} %collective-permute-done.4.refs_1_), channel_id=1, source_target_pairs={{0,1},{1,2},{2,3},{3,4},{4,5},{5,6},{6,7},{7,0},{8,9},{9,10},{10,1... | collective-permute-start | bytes 393224 | tf_op jit(solution)/shard_map/ppermute | solution.py:18
  13.9 0.0 collective-permute-done.8.refs_7_
  13.9 0.0 copy-start.2
  13.9 1.9 %collective-permute-start.9 = (bf16[256,256]{1,0:T(8,128)(2,1)S(1)}, bf16[256,256]{1,0:T(8,128)(2,1)S(1)}, u32[]{:S(2)}, u32[]{:S(2)}) collective-permute-start(bf16[256,256]{1,0:T(8,128)(2,1)S(1)} %collective-permute-done.8.refs_7_), channel_id=1, source_target_pairs={{0,7},{1,0},{2,1},{3,2},{4,3},{5,4},{6,5},{7,6},{8,15},{9,8},{10,9... | collective-permute-start | bytes 393224 | tf_op jit(solution)/shard_map/ppermute | solution.py:18
  15.8 0.6 collective-permute-done.5.refs_2_
  16.4 0.0 copy-start.3
  16.4 5.6 %collective-permute-start.6 = (bf16[256,256]{1,0:T(8,128)(2,1)S(1)}, bf16[256,256]{1,0:T(8,128)(2,1)S(1)}, u32[]{:S(2)}, u32[]{:S(2)}) collective-permute-start(bf16[256,256]{1,0:T(8,128)(2,1)S(1)} %collective-permute-done.5.refs_2_), channel_id=1, source_target_pairs={{0,1},{1,2},{2,3},{3,4},{4,5},{5,6},{6,7},{7,0},{8,9},{9,10},{10,1... | collective-permute-start | bytes 393224 | tf_op jit(solution)/shard_map/ppermute | solution.py:18
  21.9 1.3 %collective-permute-start = (bf16[2,256,128]{2,1,0:T(8,128)(2,1)}, bf16[2,256,128]{2,1,0:T(8,128)(2,1)S(1)}, u32[]{:S(2)}, u32[]{:S(2)}) collective-permute-start(bf16[2,256,128]{2,1,0:T(8,128)(2,1)} %near_ref.1), channel_id=1, source_target_pairs={{0,8},{8,16},{16,24},{24,32},{32,40},{40,48},{48,56},{56,64},{64,7... | collective-permute-start | bytes 393224 | tf_op jit(solution)/shard_map/ppermute | solution.py:18
  23.2 4.9 %collective-permute-start.1 = (bf16[2,256,128]{2,1,0:T(8,128)(2,1)}, bf16[2,256,128]{2,1,0:T(8,128)(2,1)S(1)}, u32[]{:S(2)}, u32[]{:S(2)}) collective-permute-start(bf16[2,256,128]{2,1,0:T(8,128)(2,1)} %near_ref.1), channel_id=1, source_target_pairs={{0,16},{8,24},{16,32},{24,40},{32,48},{40,56},{48,64},{56,72},{64,... | collective-permute-start | bytes 393224 | tf_op jit(solution)/shard_map/ppermute | solution.py:18
  28.2 0.0 collective-permute-done.9.refs_6_
  28.2 0.0 copy-start.4
  28.2 1.9 %collective-permute-start.10 = (bf16[256,256]{1,0:T(8,128)(2,1)S(1)}, bf16[256,256]{1,0:T(8,128)(2,1)S(1)}, u32[]{:S(2)}, u32[]{:S(2)}) collective-permute-start(bf16[256,256]{1,0:T(8,128)(2,1)S(1)} %collective-permute-done.9.refs_6_), channel_id=1, source_target_pairs={{0,7},{1,0},{2,1},{3,2},{4,3},{5,4},{6,5},{7,6},{8,15},{9,8},{10,9... | collective-permute-start | bytes 393224 | tf_op jit(solution)/shard_map/ppermute | solution.py:18
  30.1 0.0 collective-permute-done.6.refs_3_
  30.1 0.0 copy-start.5
  30.1 5.1 %collective-permute-start.7 = (bf16[256,256]{1,0:T(8,128)(2,1)S(1)}, bf16[256,256]{1,0:T(8,128)(2,1)S(1)}, u32[]{:S(2)}, u32[]{:S(2)}) collective-permute-start(bf16[256,256]{1,0:T(8,128)(2,1)S(1)} %collective-permute-done.6.refs_3_), channel_id=1, source_target_pairs={{0,1},{1,2},{2,3},{3,4},{4,5},{5,6},{6,7},{7,0},{8,9},{9,10},{10,1... | collective-permute-start | bytes 393224 | tf_op jit(solution)/shard_map/ppermute | solution.py:18
  35.3 0.0 collective-permute-done.one_ref
  35.3 0.0 copy-start.8
  35.3 0.0 collective-permute-done.1.two_ref
  35.3 0.0 copy-start.9
  35.3 0.6 copy-done.8
  35.9 0.0 copy-done.9
  36.0 7.1 %attention_backward.1 = (bf16[256,512]{1,0:T(8,128)(2,1)}, f32[2,256,128]{2,1,0:T(8,128)}, bf16[2,256,128]{2,1,0:T(8,128)(2,1)}, bf16[2,256,128]{2,1,0:T(8,128)(2,1)}) custom-call(s32[1,256]{1,0:T(1,128)} %bitcast.1, bf16[256,512]{1,0:T(8,128)(2,1)} %q_ref.1, bf16[256,512]{1,0:T(8,128)(2,1)} %o_ref.1, bf16[256,512]{1,0:T(8,128)(2,1)} %g_ref.1, ...), custom_call_target="tpu_custom_call" | custom-call | tf_op jit(solution)/shard_map/attention_backward/pallas_call | solution.py:71
  43.0 0.0 collective-permute-done.10.refs_5_
  43.0 0.0 copy-start.6
  43.1 0.0 collective-permute-done.7.refs_4_
  43.1 0.0 copy-start.7
  43.1 0.0 copy-done.1
  43.1 0.0 copy-done.2
  43.1 0.0 copy-done.3
  43.1 0.0 copy-done.4
  43.1 0.0 copy-done.5
  43.1 0.6 copy-done.6
  43.7 0.1 copy-done.7
  43.7 3.4 %weight_parts.1 = (bf16[32,32,512]{2,1,0:T(8,128)(2,1)}, bf16[32,32,512]{2,1,0:T(8,128)(2,1)}) custom-call(bf16[256,256]{1,0:T(8,128)(2,1)} %refs_0_.1, bf16[256,256]{1,0:T(8,128)(2,1)} %copy-done.1, bf16[256,256]{1,0:T(8,128)(2,1)} %copy-done.3, bf16[256,256]{1,0:T(8,128)(2,1)} %copy-done.5, bf16[256,256]{1,0:T(8,128)(2,1)} %copy-done.7, ...), custom_call_target="tpu_custom_call" | custom-call | tf_op jit(solution)/shard_map/weight_parts/pallas_call | solution.py:104
  47.2 3.5 %collective-permute-start.11 = (bf16[32,32,512]{2,1,0:T(8,128)(2,1)}, bf16[32,32,512]{2,1,0:T(8,128)(2,1)S(1)}, u32[]{:S(2)}, u32[]{:S(2)}) collective-permute-start(bf16[32,32,512]{2,1,0:T(8,128)(2,1)} %get-tuple-element.14), channel_id=1, source_target_pairs={{0,8},{8,0},{1,9},{9,1},{2,10},{10,2},{3,11},{11,3},{4,12},{12,4},... | collective-permute-start | bytes 3145736 | tf_op jit(solution)/shard_map/ppermute | solution.py:124
  50.7 2.5 %collective-permute-done.11 = bf16[32,32,512]{2,1,0:T(8,128)(2,1)S(1)} collective-permute-done((bf16[32,32,512]{2,1,0:T(8,128)(2,1)}, bf16[32,32,512]{2,1,0:T(8,128)(2,1)S(1)}, u32[]{:S(2)}, u32[]{:S(2)}) %collective-permute-start.11) | collective-permute-done | bytes 1048608 | tf_op jit(solution)/shard_map/ppermute | solution.py:124
  53.2 2.6 %add.11 = bf16[32,32,512]{2,1,0:T(8,128)(2,1)} add(bf16[32,32,512]{2,1,0:T(8,128)(2,1)} %get-tuple-element.13, bf16[32,32,512]{2,1,0:T(8,128)(2,1)S(1)} %collective-permute-done.11) | non-fusion elementwise | flops 524288 | bytes 3145728 | tf_op jit(solution)/shard_map/add | solution.py:124
  55.8 0.0 copy-start.11
  55.8 0.0 copy-start.10
  55.8 0.0 copy-start
  55.8 11.5 %all-to-all-start = ((bf16[32,32,512]{2,1,0:T(8,128)(2,1)}), bf16[32,32,512]{2,1,0:T(8,128)(2,1)S(1)}, u32[]{:S(2)}, u32[]{:S(2)}) async-start(bf16[32,32,512]{2,1,0:T(8,128)(2,1)} %add.11), calls=%async_computation | async-start | bytes 2097152 | tf_op jit(solution)/shard_map/all_to_all | solution.py:125
  67.3 0.0 copy-done.11
  67.3 1.3 %collective-permute-start.2 = (bf16[2,256,128]{2,1,0:T(8,128)(2,1)S(1)}, bf16[2,256,128]{2,1,0:T(8,128)(2,1)S(1)}, u32[]{:S(2)}, u32[]{:S(2)}) collective-permute-start(bf16[2,256,128]{2,1,0:T(8,128)(2,1)S(1)} %copy-done.11), channel_id=1, source_target_pairs={{8,0},{16,8},{24,16},{32,24},{40,32},{48,40},{56,48},{64,56},{72,6... | collective-permute-start | bytes 393224 | tf_op jit(solution)/shard_map/ppermute | solution.py:18
  68.6 0.0 copy-done.10
  68.6 1.3 %collective-permute-start.3 = (bf16[2,256,128]{2,1,0:T(8,128)(2,1)S(1)}, bf16[2,256,128]{2,1,0:T(8,128)(2,1)S(1)}, u32[]{:S(2)}, u32[]{:S(2)}) collective-permute-start(bf16[2,256,128]{2,1,0:T(8,128)(2,1)S(1)} %copy-done.10), channel_id=1, source_target_pairs={{16,0},{24,8},{32,16},{40,24},{48,32},{56,40},{64,48},{72,56},{80,... | collective-permute-start | bytes 393224 | tf_op jit(solution)/shard_map/ppermute | solution.py:18
  69.9 0.6 collective-permute-done.2
  70.5 26.0 %collective-permute-done.3 = bf16[2,256,128]{2,1,0:T(8,128)(2,1)S(1)} collective-permute-done((bf16[2,256,128]{2,1,0:T(8,128)(2,1)S(1)}, bf16[2,256,128]{2,1,0:T(8,128)(2,1)S(1)}, u32[]{:S(2)}, u32[]{:S(2)}) %collective-permute-start.3) | collective-permute-done | bytes 131104 | tf_op jit(solution)/shard_map/ppermute | solution.py:18
  96.6 0.0 copy-done
  96.6 0.7 add_convert_fusion
  97.3 0.0 all-to-all-done
  97.3 0.8 convert_reduce_fusion
Async XLA Ops:
  0.6 7.8 %collective-permute-start.4 = (bf16[256,256]{1,0:T(8,128)(2,1)}, bf16[256,256]{1,0:T(8,128)(2,1)S(1)}, u32[]{:S(2)}, u32[]{:S(2)}) collective-permute-start(bf16[256,256]{1,0:T(8,128)(2,1)} %refs_0_.1), channel_id=1, source_target_pairs={{0,1},{1,2},{2,3},{3,4},{4,5},{5,6},{6,7},{7,0},{8,9},{9,10},{10,1... | collective-permute-start | bytes 393224 | tf_op jit(solution)/shard_map/ppermute | solution.py:18
  5.3 8.5 %collective-permute-start.8 = (bf16[256,256]{1,0:T(8,128)(2,1)}, bf16[256,256]{1,0:T(8,128)(2,1)S(1)}, u32[]{:S(2)}, u32[]{:S(2)}) collective-permute-start(bf16[256,256]{1,0:T(8,128)(2,1)} %refs_0_.1), channel_id=1, source_target_pairs={{0,7},{1,0},{2,1},{3,2},{4,3},{5,4},{6,5},{7,6},{8,15},{9,8},{10,9... | collective-permute-start | bytes 393224 | tf_op jit(solution)/shard_map/ppermute | solution.py:18
  8.4 34.7 %copy-start.1 = (bf16[256,256]{1,0:T(8,128)(2,1)}, bf16[256,256]{1,0:T(8,128)(2,1)S(1)}, u32[]{:S(2)}) copy-start(bf16[256,256]{1,0:T(8,128)(2,1)S(1)} %collective-permute-done.4.refs_1_) | copy-start | bytes 393220
  8.4 8.0 %collective-permute-start.5 = (bf16[256,256]{1,0:T(8,128)(2,1)S(1)}, bf16[256,256]{1,0:T(8,128)(2,1)S(1)}, u32[]{:S(2)}, u32[]{:S(2)}) collective-permute-start(bf16[256,256]{1,0:T(8,128)(2,1)S(1)} %collective-permute-done.4.refs_1_), channel_id=1, source_target_pairs={{0,1},{1,2},{2,3},{3,4},{4,5},{5,6},{6,7},{7,0},{8,9},{9,10},{10,1... | collective-permute-start | bytes 393224 | tf_op jit(solution)/shard_map/ppermute | solution.py:18
  13.9 29.2 %copy-start.2 = (bf16[256,256]{1,0:T(8,128)(2,1)}, bf16[256,256]{1,0:T(8,128)(2,1)S(1)}, u32[]{:S(2)}) copy-start(bf16[256,256]{1,0:T(8,128)(2,1)S(1)} %collective-permute-done.8.refs_7_) | copy-start | bytes 393220
  13.9 14.3 %collective-permute-start.9 = (bf16[256,256]{1,0:T(8,128)(2,1)S(1)}, bf16[256,256]{1,0:T(8,128)(2,1)S(1)}, u32[]{:S(2)}, u32[]{:S(2)}) collective-permute-start(bf16[256,256]{1,0:T(8,128)(2,1)S(1)} %collective-permute-done.8.refs_7_), channel_id=1, source_target_pairs={{0,7},{1,0},{2,1},{3,2},{4,3},{5,4},{6,5},{7,6},{8,15},{9,8},{10,9... | collective-permute-start | bytes 393224 | tf_op jit(solution)/shard_map/ppermute | solution.py:18
  16.4 26.7 %copy-start.3 = (bf16[256,256]{1,0:T(8,128)(2,1)}, bf16[256,256]{1,0:T(8,128)(2,1)S(1)}, u32[]{:S(2)}) copy-start(bf16[256,256]{1,0:T(8,128)(2,1)S(1)} %collective-permute-done.5.refs_2_) | copy-start | bytes 393220
  16.4 13.7 %collective-permute-start.6 = (bf16[256,256]{1,0:T(8,128)(2,1)S(1)}, bf16[256,256]{1,0:T(8,128)(2,1)S(1)}, u32[]{:S(2)}, u32[]{:S(2)}) collective-permute-start(bf16[256,256]{1,0:T(8,128)(2,1)S(1)} %collective-permute-done.5.refs_2_), channel_id=1, source_target_pairs={{0,1},{1,2},{2,3},{3,4},{4,5},{5,6},{6,7},{7,0},{8,9},{9,10},{10,1... | collective-permute-start | bytes 393224 | tf_op jit(solution)/shard_map/ppermute | solution.py:18
  21.9 13.3 %collective-permute-start = (bf16[2,256,128]{2,1,0:T(8,128)(2,1)}, bf16[2,256,128]{2,1,0:T(8,128)(2,1)S(1)}, u32[]{:S(2)}, u32[]{:S(2)}) collective-permute-start(bf16[2,256,128]{2,1,0:T(8,128)(2,1)} %near_ref.1), channel_id=1, source_target_pairs={{0,8},{8,16},{16,24},{24,32},{32,40},{40,48},{48,56},{56,64},{64,7... | collective-permute-start | bytes 393224 | tf_op jit(solution)/shard_map/ppermute | solution.py:18
  23.2 12.0 %collective-permute-start.1 = (bf16[2,256,128]{2,1,0:T(8,128)(2,1)}, bf16[2,256,128]{2,1,0:T(8,128)(2,1)S(1)}, u32[]{:S(2)}, u32[]{:S(2)}) collective-permute-start(bf16[2,256,128]{2,1,0:T(8,128)(2,1)} %near_ref.1), channel_id=1, source_target_pairs={{0,16},{8,24},{16,32},{24,40},{32,48},{40,56},{48,64},{56,72},{64,... | collective-permute-start | bytes 393224 | tf_op jit(solution)/shard_map/ppermute | solution.py:18
  28.2 14.9 %copy-start.4 = (bf16[256,256]{1,0:T(8,128)(2,1)}, bf16[256,256]{1,0:T(8,128)(2,1)S(1)}, u32[]{:S(2)}) copy-start(bf16[256,256]{1,0:T(8,128)(2,1)S(1)} %collective-permute-done.9.refs_6_) | copy-start | bytes 393220
  28.2 14.9 %collective-permute-start.10 = (bf16[256,256]{1,0:T(8,128)(2,1)S(1)}, bf16[256,256]{1,0:T(8,128)(2,1)S(1)}, u32[]{:S(2)}, u32[]{:S(2)}) collective-permute-start(bf16[256,256]{1,0:T(8,128)(2,1)S(1)} %collective-permute-done.9.refs_6_), channel_id=1, source_target_pairs={{0,7},{1,0},{2,1},{3,2},{4,3},{5,4},{6,5},{7,6},{8,15},{9,8},{10,9... | collective-permute-start | bytes 393224 | tf_op jit(solution)/shard_map/ppermute | solution.py:18
  30.1 13.0 %copy-start.5 = (bf16[256,256]{1,0:T(8,128)(2,1)}, bf16[256,256]{1,0:T(8,128)(2,1)S(1)}, u32[]{:S(2)}) copy-start(bf16[256,256]{1,0:T(8,128)(2,1)S(1)} %collective-permute-done.6.refs_3_) | copy-start | bytes 393220
  30.1 12.9 %collective-permute-start.7 = (bf16[256,256]{1,0:T(8,128)(2,1)S(1)}, bf16[256,256]{1,0:T(8,128)(2,1)S(1)}, u32[]{:S(2)}, u32[]{:S(2)}) collective-permute-start(bf16[256,256]{1,0:T(8,128)(2,1)S(1)} %collective-permute-done.6.refs_3_), channel_id=1, source_target_pairs={{0,1},{1,2},{2,3},{3,4},{4,5},{5,6},{6,7},{7,0},{8,9},{9,10},{10,1... | collective-permute-start | bytes 393224 | tf_op jit(solution)/shard_map/ppermute | solution.py:18
  35.3 0.7 copy-start.8
  35.3 0.7 copy-start.9
  43.0 0.6 copy-start.6
  43.1 0.7 copy-start.7
  47.2 6.0 %collective-permute-start.11 = (bf16[32,32,512]{2,1,0:T(8,128)(2,1)}, bf16[32,32,512]{2,1,0:T(8,128)(2,1)S(1)}, u32[]{:S(2)}, u32[]{:S(2)}) collective-permute-start(bf16[32,32,512]{2,1,0:T(8,128)(2,1)} %get-tuple-element.14), channel_id=1, source_target_pairs={{0,8},{8,0},{1,9},{9,1},{2,10},{10,2},{3,11},{11,3},{4,12},{12,4},... | collective-permute-start | bytes 3145736 | tf_op jit(solution)/shard_map/ppermute | solution.py:124
  55.8 11.5 %copy-start.11 = (bf16[2,256,128]{2,1,0:T(8,128)(2,1)S(1)}, bf16[2,256,128]{2,1,0:T(8,128)(2,1)}, u32[]{:S(2)}) copy-start(bf16[2,256,128]{2,1,0:T(8,128)(2,1)} %get-tuple-element.11) | copy-start | bytes 393220
  55.8 12.8 %copy-start.10 = (bf16[2,256,128]{2,1,0:T(8,128)(2,1)S(1)}, bf16[2,256,128]{2,1,0:T(8,128)(2,1)}, u32[]{:S(2)}) copy-start(bf16[2,256,128]{2,1,0:T(8,128)(2,1)} %get-tuple-element.12) | copy-start | bytes 393220
  55.8 40.8 %copy-start = (f32[2,256,128]{2,1,0:T(8,128)S(1)}, f32[2,256,128]{2,1,0:T(8,128)}, u32[]{:S(2)}) copy-start(f32[2,256,128]{2,1,0:T(8,128)} %get-tuple-element.10) | copy-start | bytes 786436
  55.8 41.5 %all-to-all-start = ((bf16[32,32,512]{2,1,0:T(8,128)(2,1)}), bf16[32,32,512]{2,1,0:T(8,128)(2,1)S(1)}, u32[]{:S(2)}, u32[]{:S(2)}) async-start(bf16[32,32,512]{2,1,0:T(8,128)(2,1)} %add.11), calls=%async_computation | async-start | bytes 2097152 | tf_op jit(solution)/shard_map/all_to_all | solution.py:125
  67.3 3.2 %collective-permute-start.2 = (bf16[2,256,128]{2,1,0:T(8,128)(2,1)S(1)}, bf16[2,256,128]{2,1,0:T(8,128)(2,1)S(1)}, u32[]{:S(2)}, u32[]{:S(2)}) collective-permute-start(bf16[2,256,128]{2,1,0:T(8,128)(2,1)S(1)} %copy-done.11), channel_id=1, source_target_pairs={{8,0},{16,8},{24,16},{32,24},{40,32},{48,40},{56,48},{64,56},{72,6... | collective-permute-start | bytes 393224 | tf_op jit(solution)/shard_map/ppermute | solution.py:18
  68.6 28.0 %collective-permute-start.3 = (bf16[2,256,128]{2,1,0:T(8,128)(2,1)S(1)}, bf16[2,256,128]{2,1,0:T(8,128)(2,1)S(1)}, u32[]{:S(2)}, u32[]{:S(2)}) collective-permute-start(bf16[2,256,128]{2,1,0:T(8,128)(2,1)S(1)} %copy-done.10), channel_id=1, source_target_pairs={{16,0},{24,8},{32,16},{40,24},{48,32},{56,40},{64,48},{72,56},{80,... | collective-permute-start | bytes 393224 | tf_op jit(solution)/shard_map/ppermute | solution.py:18

commit v2 on v1

--- a/solution.py
+++ b/solution.py
@@ -6,6 +6,7 @@
 from jax.experimental import pallas as pl
 from jax.experimental.pallas import tpu as pltpu
 from jax.sharding import Mesh, PartitionSpec as P
+
 
 HD = 128
 REACH = 2
@@ -84,50 +85,71 @@
     )(document_start.reshape(1, rows), queries, attention_out, output_grad, near, one, two)
 
 
-def weight_parts(pieces, query_grad):
-    tokens, width = pieces[0].shape
-    columns = query_grad.shape[1]
-    owners = width // 64
+def weight_term(features, mine, other):
+    blocks, _, width, tokens = features.shape
+    columns = mine.shape[2]
 
-    def body(*refs):
-        shards, dq_ref, keep_ref, send_ref = refs[:YS], refs[YS], refs[YS + 1], refs[YS + 2]
-        y = lax.axis_index("y")
-        first_core = lax.axis_index("c") == 0
-        dq = dq_ref[...]
-        for d in range(YS):
-            term = dot(shards[d][...], dq, 0, 0).astype(jnp.bfloat16).reshape(owners, 2, 32, columns)
-            at = lax.rem(y + YS - d, YS) * owners
-            keep_ref[pl.ds(at, owners)] = jnp.where(first_core, term[:, 0], term[:, 1])
-            send_ref[pl.ds(at, owners)] = jnp.where(first_core, term[:, 1], term[:, 0])
+    def body(f_ref, mine_ref, other_ref, out_ref):
+        x = lax.axis_index("x")
+        c = lax.axis_index("c")
+        even = lax.rem(x, 2) == 0
+        beside = jnp.where(even, x + 1, x - 1)
+        total = None
+        for at, place in enumerate((x, beside, XS - 1 - x, XS - 1 - beside)):
+            for source, rows in ((CS * place + c, mine_ref), (CS * place + 1 - c, other_ref)):
+                left = f_ref[:, pl.ds(source, 1)].reshape(blocks * width, tokens)
+                term = dot(left, rows[at], 1, 0)
+                total = term if total is None else total + term
+        out_ref[...] = total.astype(jnp.bfloat16).reshape(blocks, width, columns)
 
-    shape = jax.ShapeDtypeStruct((YS * owners, 32, columns), jnp.bfloat16)
-    return pl.pallas_call(body, out_shape=[shape, shape], name="weight_parts")(*pieces, query_grad)
+    shape = jax.ShapeDtypeStruct((blocks, width, columns), jnp.bfloat16)
+    return pl.pallas_call(body, out_shape=shape, name="weight_term")(features, mine, other)
 
 
-def shards(layer_input, queries, key_values, attention_out, output_grad, document_start):
-    pieces = [layer_input] + [None] * (YS - 1)
-    forward = backward = layer_input
-    one = two = None
-    for step in range(1, YS // 2 + 1):
-        forward = moved(forward, "y", YS, 1, True)
-        pieces[step] = forward
-        if step < YS // 2:
-            backward = moved(backward, "y", YS, -1, True)
-            pieces[YS - step] = backward
-        if step == 1:
-            one = moved(key_values, SEQ, XS * ZS * CS, 1, False)
-            two = moved(key_values, SEQ, XS * ZS * CS, 2, False)
+A = [(x, x ^ 1) for x in range(XS)]
+B = [(x, XS - 1 - x) for x in range(XS)]
+
+
+def exchanged(shard, pairs):
+    return lax.ppermute(shard, "x", pairs)
+
+
+def sent_to_all(shard, axis, size):
+    copies = jnp.broadcast_to(shard, (size, *shard.shape))
+    return lax.all_to_all(copies, axis, split_axis=0, concat_axis=0, tiled=True)
+
+
+def step(layer_input, queries, key_values, attention_out, output_grad, document_start):
+    rows = layer_input.shape[0]
+    one = moved(key_values, SEQ, XS * ZS * CS, 1, False)
+    two = moved(key_values, SEQ, XS * ZS * CS, 2, False)
+    width = layer_input.shape[1] // (XS * CS)
+    features = layer_input.T.reshape(XS * CS, width, rows)
+    features = lax.all_to_all(features, ("x", "c"), split_axis=0, concat_axis=0, tiled=True)
+    features = sent_to_all(features.reshape(XS * CS * width, rows), "y", YS)
+    features = features.reshape(YS, XS * CS, width, rows)
     query_grad, own, part_one, part_two = attention_backward(
         queries, attention_out, output_grad, document_start, key_values, one, two
     )
-    keep, send = weight_parts(pieces, query_grad)
-    summed = keep + lax.ppermute(send, "c", [(0, 1), (1, 0)])
-    arrived = lax.all_to_all(summed, ("x", "z"), split_axis=0, concat_axis=0, tiled=True)
     back_one = moved(part_one, SEQ, XS * ZS * CS, -1, False)
     back_two = moved(part_two, SEQ, XS * ZS * CS, -2, False)
     pair_total = own + back_one.astype(jnp.float32) + back_two.astype(jnp.float32)
-    weight_grad = arrived.astype(jnp.float32).sum(axis=0)
-    return query_grad, pair_total.astype(jnp.bfloat16), weight_grad
+    pair_total = pair_total.astype(jnp.bfloat16)
+    low, high = query_grad[: rows // 2], query_grad[rows // 2 :]
+    low_a, high_b = exchanged(low, A), exchanged(high, B)
+    low_b = exchanged(jnp.concatenate([low, low_a]), B)
+    high_a = exchanged(jnp.concatenate([high, high_b]), A)
+    low_b, low_ab = jnp.split(low_b, 2)
+    high_a, high_ab = jnp.split(high_a, 2)
+    mine = jnp.concatenate([query_grad, low_a, high_a, low_b, high_b, low_ab, high_ab])
+    mine = mine.reshape(XS, rows, query_grad.shape[1])
+    other = lax.ppermute(mine, "c", [(0, 1), (1, 0)])
+    term = weight_term(features, mine, other)
+    arrived = lax.all_to_all(term, "z", split_axis=0, concat_axis=0, tiled=True)
+    summed = arrived.astype(jnp.float32).sum(axis=0)
+    half = ZS // 2
+    owners = [(x * ZS + z, (z // 2) * ZS + half * (z % 2) + x) for x in range(XS) for z in range(ZS)]
+    return query_grad, pair_total, lax.ppermute(summed, ("x", "z"), owners)
 
 
 def solution(mesh):
@@ -141,7 +163,7 @@
         P(SEQ),
     )
     return jax.shard_map(
-        shards,
+        step,
         mesh=split,
         in_specs=placed,
         out_specs=(P(SEQ, "y"), P(None, SEQ, "y"), P(SEQ, "y")),

time: 98.7 us -> 109 us (1.10)
  the two profiles are of different devices: /device:TPU:24 before, /device:TPU:4 now
where the time goes in v2:
time: 109 us; the launch traced here: 108 us
  starting transfers between devices  44.6 us (41%)
  waiting for transfers between devices  38.3 us (35%)
  Pallas kernels  10.3 us (9%)
  blocking collectives  8.81 us (8%)
  local copies, waits for them, and re-layouts  4.53 us (4%)
    ppermute x4, starting transfers between devices, moved(): return lax.ppermute(shard, axis, pairs)  14.6 us
    ppermute x4, starting transfers between devices, exchanged(): return lax.ppermute(shard, 'x', pairs)  12 us
    ppermute x4, waiting for transfers between devices, moved(): return lax.ppermute(shard, axis, pairs)  10.3 us
    all_to_all x1, blocking collectives, step(): lax.all_to_all(features, ('x', 'c'), split_axis=0, concat_axis=0, tiled=T...  8.81 us
    all_to_all x1, waiting for transfers between devices, sent_to_all(): return lax.all_to_all(copies, axis, split_axis=0, concat_axis=0, tiled=True)  8.23 us
    ppermute x1, waiting for transfers between devices, step(): return (query_grad, pair_total, lax.ppermute(summed, ('x', 'z'), owners))  7.28 us
    all_to_all x1, starting transfers between devices, sent_to_all(): return lax.all_to_all(copies, axis, split_axis=0, concat_axis=0, tiled=True)  7.1 us
    pallas_call x1, Pallas kernels, attention_backward(): pl.pallas_call(body, grid=(heads,), in_specs=[pl.BlockSpec((1, rows), lam...  7.05 us
  transfers between devices with their start and end apart: 12, of which 9 were waited for; matrix products, arithmetic and copies ran while one was open for 2% of the time, Pallas kernels for 0%

profile of v2, /device:TPU:4, one launch (start us, length us, event | category | flops | bytes accessed | tf_op | source)
XLA Modules:
  0.0 108.3 jit_solution(15066435568872133034)
XLA Ops:
  0.6 1.9 %collective-permute-start = (bf16[2,256,128]{2,1,0:T(8,128)(2,1)}, bf16[2,256,128]{2,1,0:T(8,128)(2,1)S(1)}, u32[]{:S(2)}, u32[]{:S(2)}) collective-permute-start(bf16[2,256,128]{2,1,0:T(8,128)(2,1)} %near_ref.1), channel_id=1, source_target_pairs={{0,8},{8,16},{16,24},{24,32},{32,40},{40,48},{48,56},{56,64},{64,7... | collective-permute-start | bytes 393224 | tf_op jit(solution)/shard_map/ppermute | solution.py:19
  2.6 4.3 %collective-permute-start.1 = (bf16[2,256,128]{2,1,0:T(8,128)(2,1)}, bf16[2,256,128]{2,1,0:T(8,128)(2,1)S(1)}, u32[]{:S(2)}, u32[]{:S(2)}) collective-permute-start(bf16[2,256,128]{2,1,0:T(8,128)(2,1)} %near_ref.1), channel_id=1, source_target_pairs={{0,16},{8,24},{16,32},{24,40},{32,48},{40,56},{48,64},{56,72},{64,... | collective-permute-start | bytes 393224 | tf_op jit(solution)/shard_map/ppermute | solution.py:19
  6.8 7.0 %collective-permute-done.one_ref = bf16[2,256,128]{2,1,0:T(8,128)(2,1)S(1)} collective-permute-done((bf16[2,256,128]{2,1,0:T(8,128)(2,1)}, bf16[2,256,128]{2,1,0:T(8,128)(2,1)S(1)}, u32[]{:S(2)}, u32[]{:S(2)}) %collective-permute-start) | collective-permute-done | bytes 131104 | tf_op jit(solution)/shard_map/ppermute | solution.py:19
  13.8 0.0 copy-start.6
  13.8 3.3 %collective-permute-done.1.two_ref = bf16[2,256,128]{2,1,0:T(8,128)(2,1)S(1)} collective-permute-done((bf16[2,256,128]{2,1,0:T(8,128)(2,1)}, bf16[2,256,128]{2,1,0:T(8,128)(2,1)S(1)}, u32[]{:S(2)}, u32[]{:S(2)}) %collective-permute-start.1) | collective-permute-done | bytes 131104 | tf_op jit(solution)/shard_map/ppermute | solution.py:19
  17.2 0.0 copy-start.7
  17.2 0.0 copy-done.6
  17.2 0.6 copy-done.7
  17.8 7.1 %attention_backward.1 = (bf16[256,512]{1,0:T(8,128)(2,1)}, f32[2,256,128]{2,1,0:T(8,128)}, bf16[2,256,128]{2,1,0:T(8,128)(2,1)}, bf16[2,256,128]{2,1,0:T(8,128)(2,1)}) custom-call(s32[1,256]{1,0:T(1,128)} %bitcast.12, bf16[256,512]{1,0:T(8,128)(2,1)} %q_ref.1, bf16[256,512]{1,0:T(8,128)(2,1)} %o_ref.1, bf16[256,512]{1,0:T(8,128)(2,1)} %g_ref.1, ...), custom_call_target="tpu_custom_call" | custom-call | tf_op jit(solution)/shard_map/attention_backward/pallas_call | solution.py:72
  24.9 0.0 copy-start.5
  24.9 1.0 fusion
  25.9 2.4 %collective-permute-start.5 = (bf16[128,512]{1,0:T(8,128)(2,1)S(1)}, bf16[128,512]{1,0:T(8,128)(2,1)S(1)}, u32[]{:S(2)}, u32[]{:S(2)}) collective-permute-start(bf16[128,512]{1,0:T(8,128)(2,1)S(1)} %get-tuple-element.11), channel_id=1, source_target_pairs={{0,384},{128,256},{256,128},{384,0},{1,385},{129,257},{257,129},{3... | collective-permute-start | bytes 393224 | tf_op jit(solution)/shard_map/ppermute | solution.py:114
  28.4 0.0 copy-done.5
  28.4 0.1 copy.10
  28.5 8.8 %all_to_all.15 = bf16[8,32,256]{2,1,0:T(8,128)(2,1)S(1)} all-to-all(bf16[8,32,256]{2,1,0:T(8,128)(2,1)S(1)} %bitcast.11), channel_id=1, replica_groups=mesh['x'=4,'z'=8,'c'=2,'y'=8] {'x','c'}, dimensions={0} | all-to-all | bytes 262144 | tf_op jit(solution)/shard_map/all_to_all | solution.py:128
  37.3 1.0 broadcast_in_dim.3
  38.3 7.1 %all-to-all-start.1 = ((bf16[8,256,256]{2,1,0:T(8,128)(2,1)}), bf16[8,256,256]{2,1,0:T(8,128)(2,1)S(1)}, u32[]{:S(2)}, u32[]{:S(2)}) async-start(bf16[8,256,256]{2,1,0:T(8,128)(2,1)} %broadcast_in_dim.3), calls=%async_computation.1 | async-start | bytes 2097152 | tf_op jit(solution)/shard_map/all_to_all | solution.py:119
  45.4 0.0 copy-start.3
  45.4 3.8 %collective-permute-start.4 = (bf16[128,512]{1,0:T(8,128)(2,1)S(1)}, bf16[128,512]{1,0:T(8,128)(2,1)S(1)}, u32[]{:S(2)}, u32[]{:S(2)}) collective-permute-start(bf16[128,512]{1,0:T(8,128)(2,1)S(1)} %get-tuple-element.12), channel_id=1, source_target_pairs={{0,128},{128,0},{256,384},{384,256},{1,129},{129,1},{257,385},{385... | collective-permute-start | bytes 393224 | tf_op jit(solution)/shard_map/ppermute | solution.py:114
  49.3 0.0 collective-permute-done.5
  49.3 2.1 %collective-permute-start.6 = (bf16[256,512]{1,0:T(8,128)(2,1)S(1)}, bf16[256,512]{1,0:T(8,128)(2,1)S(1)}, u32[]{:S(2)}, u32[]{:S(2)}) collective-permute-start(bf16[256,512]{1,0:T(8,128)(2,1)S(1)} %pad_maximum_fusion), channel_id=1, source_target_pairs={{0,128},{128,0},{256,384},{384,256},{1,129},{129,1},{257,385},{385... | collective-permute-start | bytes 786440 | tf_op jit(solution)/shard_map/ppermute | solution.py:114
  51.5 0.0 copy-done.3
  51.5 1.1 %collective-permute-done.4 = bf16[128,512]{1,0:T(8,128)(2,1)S(1)} collective-permute-done((bf16[128,512]{1,0:T(8,128)(2,1)S(1)}, bf16[128,512]{1,0:T(8,128)(2,1)S(1)}, u32[]{:S(2)}, u32[]{:S(2)}) %collective-permute-start.4) | collective-permute-done | bytes 131104 | tf_op jit(solution)/shard_map/ppermute | solution.py:114
  52.6 3.5 %collective-permute-start.7 = (bf16[256,512]{1,0:T(8,128)(2,1)S(1)}, bf16[256,512]{1,0:T(8,128)(2,1)S(1)}, u32[]{:S(2)}, u32[]{:S(2)}) collective-permute-start(bf16[256,512]{1,0:T(8,128)(2,1)S(1)} %pad_maximum_fusion.1), channel_id=1, source_target_pairs={{0,384},{128,256},{256,128},{384,0},{1,385},{129,257},{257,129},{3... | collective-permute-start | bytes 786440 | tf_op jit(solution)/shard_map/ppermute | solution.py:114
  56.2 2.3 %collective-permute-done.6 = bf16[256,512]{1,0:T(8,128)(2,1)S(1)} collective-permute-done((bf16[256,512]{1,0:T(8,128)(2,1)S(1)}, bf16[256,512]{1,0:T(8,128)(2,1)S(1)}, u32[]{:S(2)}, u32[]{:S(2)}) %collective-permute-start.6) | collective-permute-done | bytes 262176 | tf_op jit(solution)/shard_map/ppermute | solution.py:114
  58.5 2.8 %collective-permute-done.7 = bf16[256,512]{1,0:T(8,128)(2,1)S(1)} collective-permute-done((bf16[256,512]{1,0:T(8,128)(2,1)S(1)}, bf16[256,512]{1,0:T(8,128)(2,1)S(1)}, u32[]{:S(2)}, u32[]{:S(2)}) %collective-permute-start.7) | collective-permute-done | bytes 262176 | tf_op jit(solution)/shard_map/ppermute | solution.py:114
  61.4 0.0 copy-start.1
  61.4 1.9 %collective-permute-start.8 = (bf16[4,256,512]{2,1,0:T(8,128)(2,1)S(1)}, bf16[4,256,512]{2,1,0:T(8,128)(2,1)S(1)}, u32[]{:S(2)}, u32[]{:S(2)}) collective-permute-start(bf16[4,256,512]{2,1,0:T(8,128)(2,1)S(1)} %bitcast.8), channel_id=1, source_target_pairs={{0,8},{8,0},{1,9},{9,1},{2,10},{10,2},{3,11},{11,3},{4,12},{12,4},... | collective-permute-start | bytes 3145736 | tf_op jit(solution)/shard_map/ppermute | solution.py:146
  63.4 2.6 %collective-permute-done.8.other_ref = bf16[4,256,512]{2,1,0:T(8,128)(2,1)S(1)} collective-permute-done((bf16[4,256,512]{2,1,0:T(8,128)(2,1)S(1)}, bf16[4,256,512]{2,1,0:T(8,128)(2,1)S(1)}, u32[]{:S(2)}, u32[]{:S(2)}) %collective-permute-start.8) | collective-permute-done | bytes 1048608 | tf_op jit(solution)/shard_map/ppermute | solution.py:146
  66.0 0.0 copy-start.2
  66.0 8.2 %all-to-all-done.1 = bf16[8,256,256]{2,1,0:T(8,128)(2,1)S(1)} async-done(((bf16[8,256,256]{2,1,0:T(8,128)(2,1)}), bf16[8,256,256]{2,1,0:T(8,128)(2,1)S(1)}, u32[]{:S(2)}, u32[]{:S(2)}) %all-to-all-start.1) | async-done | bytes 1048608 | tf_op jit(solution)/shard_map/all_to_all | solution.py:119
  74.2 0.0 copy-start
  74.2 0.0 copy-done.1
  74.2 0.0 copy-done.2
  74.2 1.0 copy-done
  75.2 3.3 %weight_term.1 = bf16[8,32,512]{2,1,0:T(8,128)(2,1)} custom-call(bf16[8,8,32,256]{3,2,1,0:T(8,128)(2,1)} %bitcast.7, bf16[4,256,512]{2,1,0:T(8,128)(2,1)} %bitcast.9, bf16[4,256,512]{2,1,0:T(8,128)(2,1)} %copy-done.2), custom_call_target="tpu_custom_call" | custom-call | tf_op jit(solution)/shard_map/weight_term/pallas_call | solution.py:106
  78.5 0.0 copy-start.9
  78.5 0.0 copy-start.8
  78.5 4.6 %all-to-all-start.2 = ((bf16[8,32,512]{2,1,0:T(8,128)(2,1)}), bf16[8,32,512]{2,1,0:T(8,128)(2,1)S(1)}, u32[]{:S(2)}, u32[]{:S(2)}) async-start(bf16[8,32,512]{2,1,0:T(8,128)(2,1)} %weight_term.1), calls=%async_computation.2 | async-start | bytes 524288 | tf_op jit(solution)/shard_map/all_to_all | solution.py:148
  83.1 0.0 copy-start.4
  83.1 0.0 copy-done.9
  83.1 6.3 %collective-permute-start.3 = (bf16[2,256,128]{2,1,0:T(8,128)(2,1)S(1)}, bf16[2,256,128]{2,1,0:T(8,128)(2,1)S(1)}, u32[]{:S(2)}, u32[]{:S(2)}) collective-permute-start(bf16[2,256,128]{2,1,0:T(8,128)(2,1)S(1)} %copy-done.9), channel_id=1, source_target_pairs={{16,0},{24,8},{32,16},{40,24},{48,32},{56,40},{64,48},{72,56},{80,... | collective-permute-start | bytes 393224 | tf_op jit(solution)/shard_map/ppermute | solution.py:19
  89.3 0.0 copy-done.8
  89.4 2.2 %collective-permute-start.2 = (bf16[2,256,128]{2,1,0:T(8,128)(2,1)S(1)}, bf16[2,256,128]{2,1,0:T(8,128)(2,1)S(1)}, u32[]{:S(2)}, u32[]{:S(2)}) collective-permute-start(bf16[2,256,128]{2,1,0:T(8,128)(2,1)S(1)} %copy-done.8), channel_id=1, source_target_pairs={{8,0},{16,8},{24,16},{32,24},{40,32},{48,40},{56,48},{64,56},{72,6... | collective-permute-start | bytes 393224 | tf_op jit(solution)/shard_map/ppermute | solution.py:19
  91.5 3.6 %all-to-all-done.2 = bf16[8,32,512]{2,1,0:T(8,128)(2,1)S(1)} async-done(((bf16[8,32,512]{2,1,0:T(8,128)(2,1)}), bf16[8,32,512]{2,1,0:T(8,128)(2,1)S(1)}, u32[]{:S(2)}, u32[]{:S(2)}) %all-to-all-start.2) | async-done | bytes 262176 | tf_op jit(solution)/shard_map/all_to_all | solution.py:148
  95.2 4.4 %collective-permute-start.9 = (f32[32,512]{1,0:T(8,128)S(1)}, f32[32,512]{1,0:T(8,128)S(1)}, u32[]{:S(2)}, u32[]{:S(2)}) collective-permute-start(f32[32,512]{1,0:T(8,128)S(1)} %convert_reduce_fusion), channel_id=1, source_target_pairs={{0,0},{16,64},{32,128},{48,192},{64,256},{80,320},{96,384},{112,44... | collective-permute-start | bytes 196616 | tf_op jit(solution)/shard_map/ppermute | solution.py:152
  99.6 0.0 collective-permute-done.3
  99.6 0.0 collective-permute-done.2
  99.6 0.0 copy-done.4
  99.6 0.7 add_convert_fusion
  100.3 7.3 %collective-permute-done.9 = f32[32,512]{1,0:T(8,128)S(1)} collective-permute-done((f32[32,512]{1,0:T(8,128)S(1)}, f32[32,512]{1,0:T(8,128)S(1)}, u32[]{:S(2)}, u32[]{:S(2)}) %collective-permute-start.9) | collective-permute-done | bytes 65568 | tf_op jit(solution)/shard_map/ppermute | solution.py:152
  107.6 0.6 copy.18
  (10 shorter events, 0.2 us)
Async XLA Ops:
  0.6 13.2 %collective-permute-start = (bf16[2,256,128]{2,1,0:T(8,128)(2,1)}, bf16[2,256,128]{2,1,0:T(8,128)(2,1)S(1)}, u32[]{:S(2)}, u32[]{:S(2)}) collective-permute-start(bf16[2,256,128]{2,1,0:T(8,128)(2,1)} %near_ref.1), channel_id=1, source_target_pairs={{0,8},{8,16},{16,24},{24,32},{32,40},{40,48},{48,56},{56,64},{64,7... | collective-permute-start | bytes 393224 | tf_op jit(solution)/shard_map/ppermute | solution.py:19
  2.6 14.6 %collective-permute-start.1 = (bf16[2,256,128]{2,1,0:T(8,128)(2,1)}, bf16[2,256,128]{2,1,0:T(8,128)(2,1)S(1)}, u32[]{:S(2)}, u32[]{:S(2)}) collective-permute-start(bf16[2,256,128]{2,1,0:T(8,128)(2,1)} %near_ref.1), channel_id=1, source_target_pairs={{0,16},{8,24},{16,32},{24,40},{32,48},{40,56},{48,64},{56,72},{64,... | collective-permute-start | bytes 393224 | tf_op jit(solution)/shard_map/ppermute | solution.py:19
  13.8 3.3 %copy-start.6 = (bf16[2,256,128]{2,1,0:T(8,128)(2,1)}, bf16[2,256,128]{2,1,0:T(8,128)(2,1)S(1)}, u32[]{:S(2)}) copy-start(bf16[2,256,128]{2,1,0:T(8,128)(2,1)S(1)} %collective-permute-done.one_ref) | copy-start | bytes 393220
  17.2 0.6 copy-start.7
  24.9 3.5 %copy-start.5 = (bf16[256,256]{1,0:T(8,128)(2,1)S(1)}, bf16[256,256]{1,0:T(8,128)(2,1)}, u32[]{:S(2)}) copy-start(bf16[256,256]{1,0:T(8,128)(2,1)} %param.6) | copy-start | bytes 393220
  25.9 23.4 %collective-permute-start.5 = (bf16[128,512]{1,0:T(8,128)(2,1)S(1)}, bf16[128,512]{1,0:T(8,128)(2,1)S(1)}, u32[]{:S(2)}, u32[]{:S(2)}) collective-permute-start(bf16[128,512]{1,0:T(8,128)(2,1)S(1)} %get-tuple-element.11), channel_id=1, source_target_pairs={{0,384},{128,256},{256,128},{384,0},{1,385},{129,257},{257,129},{3... | collective-permute-start | bytes 393224 | tf_op jit(solution)/shard_map/ppermute | solution.py:114
  38.3 35.9 %all-to-all-start.1 = ((bf16[8,256,256]{2,1,0:T(8,128)(2,1)}), bf16[8,256,256]{2,1,0:T(8,128)(2,1)S(1)}, u32[]{:S(2)}, u32[]{:S(2)}) async-start(bf16[8,256,256]{2,1,0:T(8,128)(2,1)} %broadcast_in_dim.3), calls=%async_computation.1 | async-start | bytes 2097152 | tf_op jit(solution)/shard_map/all_to_all | solution.py:119
  45.4 6.0 %copy-start.3 = (bf16[256,512]{1,0:T(8,128)(2,1)S(1)}, bf16[256,512]{1,0:T(8,128)(2,1)}, u32[]{:S(2)}) copy-start(bf16[256,512]{1,0:T(8,128)(2,1)} %get-tuple-element.16) | copy-start | bytes 786436
  45.4 7.2 %collective-permute-start.4 = (bf16[128,512]{1,0:T(8,128)(2,1)S(1)}, bf16[128,512]{1,0:T(8,128)(2,1)S(1)}, u32[]{:S(2)}, u32[]{:S(2)}) collective-permute-start(bf16[128,512]{1,0:T(8,128)(2,1)S(1)} %get-tuple-element.12), channel_id=1, source_target_pairs={{0,128},{128,0},{256,384},{384,256},{1,129},{129,1},{257,385},{385... | collective-permute-start | bytes 393224 | tf_op jit(solution)/shard_map/ppermute | solution.py:114
  49.3 9.2 %collective-permute-start.6 = (bf16[256,512]{1,0:T(8,128)(2,1)S(1)}, bf16[256,512]{1,0:T(8,128)(2,1)S(1)}, u32[]{:S(2)}, u32[]{:S(2)}) collective-permute-start(bf16[256,512]{1,0:T(8,128)(2,1)S(1)} %pad_maximum_fusion), channel_id=1, source_target_pairs={{0,128},{128,0},{256,384},{384,256},{1,129},{129,1},{257,385},{385... | collective-permute-start | bytes 786440 | tf_op jit(solution)/shard_map/ppermute | solution.py:114
  52.6 8.7 %collective-permute-start.7 = (bf16[256,512]{1,0:T(8,128)(2,1)S(1)}, bf16[256,512]{1,0:T(8,128)(2,1)S(1)}, u32[]{:S(2)}, u32[]{:S(2)}) collective-permute-start(bf16[256,512]{1,0:T(8,128)(2,1)S(1)} %pad_maximum_fusion.1), channel_id=1, source_target_pairs={{0,384},{128,256},{256,128},{384,0},{1,385},{129,257},{257,129},{3... | collective-permute-start | bytes 786440 | tf_op jit(solution)/shard_map/ppermute | solution.py:114
  61.4 12.8 %copy-start.1 = (bf16[1024,512]{1,0:T(8,128)(2,1)}, bf16[1024,512]{1,0:T(8,128)(2,1)S(1)}, u32[]{:S(2)}) copy-start(bf16[1024,512]{1,0:T(8,128)(2,1)S(1)} %slice_dynamic-update-slice_fusion) | copy-start | bytes 3145732
  61.4 4.6 %collective-permute-start.8 = (bf16[4,256,512]{2,1,0:T(8,128)(2,1)S(1)}, bf16[4,256,512]{2,1,0:T(8,128)(2,1)S(1)}, u32[]{:S(2)}, u32[]{:S(2)}) collective-permute-start(bf16[4,256,512]{2,1,0:T(8,128)(2,1)S(1)} %bitcast.8), channel_id=1, source_target_pairs={{0,8},{8,0},{1,9},{9,1},{2,10},{10,2},{3,11},{11,3},{4,12},{12,4},... | collective-permute-start | bytes 3145736 | tf_op jit(solution)/shard_map/ppermute | solution.py:146
  66.0 8.2 %copy-start.2 = (bf16[4,256,512]{2,1,0:T(8,128)(2,1)}, bf16[4,256,512]{2,1,0:T(8,128)(2,1)S(1)}, u32[]{:S(2)}) copy-start(bf16[4,256,512]{2,1,0:T(8,128)(2,1)S(1)} %collective-permute-done.8.other_ref) | copy-start | bytes 3145732
  74.2 1.0 copy-start
  78.5 4.6 %copy-start.9 = (bf16[2,256,128]{2,1,0:T(8,128)(2,1)S(1)}, bf16[2,256,128]{2,1,0:T(8,128)(2,1)}, u32[]{:S(2)}) copy-start(bf16[2,256,128]{2,1,0:T(8,128)(2,1)} %get-tuple-element.10) | copy-start | bytes 393220
  78.5 10.9 %copy-start.8 = (bf16[2,256,128]{2,1,0:T(8,128)(2,1)S(1)}, bf16[2,256,128]{2,1,0:T(8,128)(2,1)}, u32[]{:S(2)}) copy-start(bf16[2,256,128]{2,1,0:T(8,128)(2,1)} %get-tuple-element.9) | copy-start | bytes 393220
  78.5 16.6 %all-to-all-start.2 = ((bf16[8,32,512]{2,1,0:T(8,128)(2,1)}), bf16[8,32,512]{2,1,0:T(8,128)(2,1)S(1)}, u32[]{:S(2)}, u32[]{:S(2)}) async-start(bf16[8,32,512]{2,1,0:T(8,128)(2,1)} %weight_term.1), calls=%async_computation.2 | async-start | bytes 524288 | tf_op jit(solution)/shard_map/all_to_all | solution.py:148
  83.1 16.6 %copy-start.4 = (f32[2,256,128]{2,1,0:T(8,128)S(1)}, f32[2,256,128]{2,1,0:T(8,128)}, u32[]{:S(2)}) copy-start(f32[2,256,128]{2,1,0:T(8,128)} %get-tuple-element.8) | copy-start | bytes 786436
  83.1 16.5 %collective-permute-start.3 = (bf16[2,256,128]{2,1,0:T(8,128)(2,1)S(1)}, bf16[2,256,128]{2,1,0:T(8,128)(2,1)S(1)}, u32[]{:S(2)}, u32[]{:S(2)}) collective-permute-start(bf16[2,256,128]{2,1,0:T(8,128)(2,1)S(1)} %copy-done.9), channel_id=1, source_target_pairs={{16,0},{24,8},{32,16},{40,24},{48,32},{56,40},{64,48},{72,56},{80,... | collective-permute-start | bytes 393224 | tf_op jit(solution)/shard_map/ppermute | solution.py:19
  89.4 10.3 %collective-permute-start.2 = (bf16[2,256,128]{2,1,0:T(8,128)(2,1)S(1)}, bf16[2,256,128]{2,1,0:T(8,128)(2,1)S(1)}, u32[]{:S(2)}, u32[]{:S(2)}) collective-permute-start(bf16[2,256,128]{2,1,0:T(8,128)(2,1)S(1)} %copy-done.8), channel_id=1, source_target_pairs={{8,0},{16,8},{24,16},{32,24},{40,32},{48,40},{56,48},{64,56},{72,6... | collective-permute-start | bytes 393224 | tf_op jit(solution)/shard_map/ppermute | solution.py:19
  95.2 12.5 %collective-permute-start.9 = (f32[32,512]{1,0:T(8,128)S(1)}, f32[32,512]{1,0:T(8,128)S(1)}, u32[]{:S(2)}, u32[]{:S(2)}) collective-permute-start(f32[32,512]{1,0:T(8,128)S(1)} %convert_reduce_fusion), channel_id=1, source_target_pairs={{0,0},{16,64},{32,128},{48,192},{64,256},{80,320},{96,384},{112,44... | collective-permute-start | bytes 196616 | tf_op jit(solution)/shard_map/ppermute | solution.py:152

commit v3 on v1

--- a/solution.py
+++ b/solution.py
@@ -7,10 +7,12 @@
 from jax.experimental.pallas import tpu as pltpu
 from jax.sharding import Mesh, PartitionSpec as P
 
+
 HD = 128
 REACH = 2
-SEQ = ("x", "z", "c")
-XS, ZS, CS, YS = 4, 8, 2, 8
+SEQ = ("x", "zh", "zl", "c")
+XS, ZH, ZL, CS, YS = 4, 4, 2, 2, 8
+SHARDS = XS * ZH * ZL * CS
 
 
 def moved(shard, axis, size, by, wrap):
@@ -84,54 +86,52 @@
     )(document_start.reshape(1, rows), queries, attention_out, output_grad, near, one, two)
 
 
-def weight_parts(pieces, query_grad):
-    tokens, width = pieces[0].shape
-    columns = query_grad.shape[1]
-    owners = width // 64
+def weight_term(features, gathered):
+    blocks, sources, width, tokens = features.shape
+    columns = gathered[0].shape[1]
 
-    def body(*refs):
-        shards, dq_ref, keep_ref, send_ref = refs[:YS], refs[YS], refs[YS + 1], refs[YS + 2]
-        y = lax.axis_index("y")
-        first_core = lax.axis_index("c") == 0
-        dq = dq_ref[...]
-        for d in range(YS):
-            term = dot(shards[d][...], dq, 0, 0).astype(jnp.bfloat16).reshape(owners, 2, 32, columns)
-            at = lax.rem(y + YS - d, YS) * owners
-            keep_ref[pl.ds(at, owners)] = jnp.where(first_core, term[:, 0], term[:, 1])
-            send_ref[pl.ds(at, owners)] = jnp.where(first_core, term[:, 1], term[:, 0])
+    def body(f_ref, *refs):
+        rows, out_ref = refs[:-1], refs[-1]
+        own = CS * lax.axis_index("zl") + lax.axis_index("c")
+        swapped = CS * lax.axis_index("zl") + 1 - lax.axis_index("c")
+        total = None
+        for source, row in zip((own, swapped, sources - 1 - swapped, sources - 1 - own), rows):
+            left = f_ref[:, pl.ds(source, 1)].reshape(blocks * width, tokens)
+            term = dot(left, row[...], 1, 0)
+            total = term if total is None else total + term
+        out_ref[...] = total.astype(jnp.bfloat16).reshape(out_ref.shape)
 
-    shape = jax.ShapeDtypeStruct((YS * owners, 32, columns), jnp.bfloat16)
-    return pl.pallas_call(body, out_shape=[shape, shape], name="weight_parts")(*pieces, query_grad)
+    shape = jax.ShapeDtypeStruct((blocks * width // 32, 32, columns), jnp.bfloat16)
+    return pl.pallas_call(body, out_shape=shape, name="weight_term")(features, *gathered)
 
 
-def shards(layer_input, queries, key_values, attention_out, output_grad, document_start):
-    pieces = [layer_input] + [None] * (YS - 1)
-    forward = backward = layer_input
-    one = two = None
-    for step in range(1, YS // 2 + 1):
-        forward = moved(forward, "y", YS, 1, True)
-        pieces[step] = forward
-        if step < YS // 2:
-            backward = moved(backward, "y", YS, -1, True)
-            pieces[YS - step] = backward
-        if step == 1:
-            one = moved(key_values, SEQ, XS * ZS * CS, 1, False)
-            two = moved(key_values, SEQ, XS * ZS * CS, 2, False)
+def step(layer_input, queries, key_values, attention_out, output_grad, document_start):
+    rows, features_here = layer_input.shape
+    one = moved(key_values, SEQ, SHARDS, 1, False)
+    two = moved(key_values, SEQ, SHARDS, 2, False)
+    parts = layer_input.T.reshape(2, ZL * CS, features_here // (2 * ZL * CS), rows).swapaxes(0, 1)
+    parts = parts.reshape(ZL * CS, features_here // (ZL * CS), rows)
+    copies = jnp.broadcast_to(parts, (YS, *parts.shape)).reshape(YS * ZL * CS, *parts.shape[1:])
+    features = lax.all_to_all(copies, ("y", "zl", "c"), split_axis=0, concat_axis=0, tiled=True)
+    features = features.reshape(YS, *parts.shape)
     query_grad, own, part_one, part_two = attention_backward(
         queries, attention_out, output_grad, document_start, key_values, one, two
     )
-    keep, send = weight_parts(pieces, query_grad)
-    summed = keep + lax.ppermute(send, "c", [(0, 1), (1, 0)])
-    arrived = lax.all_to_all(summed, ("x", "z"), split_axis=0, concat_axis=0, tiled=True)
-    back_one = moved(part_one, SEQ, XS * ZS * CS, -1, False)
-    back_two = moved(part_two, SEQ, XS * ZS * CS, -2, False)
+    swap = [(0, 1), (1, 0)]
+    beyond = lax.ppermute(query_grad, "zl", swap)
+    beside = lax.ppermute(query_grad, "c", swap)
+    across = lax.ppermute(beyond, "c", swap)
+    back_one = moved(part_one, SEQ, SHARDS, -1, False)
+    back_two = moved(part_two, SEQ, SHARDS, -2, False)
     pair_total = own + back_one.astype(jnp.float32) + back_two.astype(jnp.float32)
-    weight_grad = arrived.astype(jnp.float32).sum(axis=0)
-    return query_grad, pair_total.astype(jnp.bfloat16), weight_grad
+    pair_total = pair_total.astype(jnp.bfloat16)
+    term = weight_term(features, (query_grad, beside, beyond, across))
+    arrived = lax.all_to_all(term, ("x", "zh"), split_axis=0, concat_axis=0, tiled=True)
+    return query_grad, pair_total, arrived.astype(jnp.float32).sum(axis=0)
 
 
 def solution(mesh):
-    split = Mesh(mesh.devices.reshape(XS, ZS, CS, YS), SEQ + ("y",))
+    split = Mesh(mesh.devices.reshape(XS, ZH, ZL, CS, YS), SEQ + ("y",))
     placed = (
         P(SEQ, "y"),
         P(SEQ, "y"),
@@ -141,7 +141,7 @@
         P(SEQ),
     )
     return jax.shard_map(
-        shards,
+        step,
         mesh=split,
         in_specs=placed,
         out_specs=(P(SEQ, "y"), P(None, SEQ, "y"), P(SEQ, "y")),

time: 98.7 us -> 84.2 us (0.85)
  the two profiles are of different devices: /device:TPU:24 before, /device:TPU:1 now
where the time goes in v3:
time: 84.2 us; the launch traced here: 83.7 us
  starting transfers between devices  43.2 us (51%)
  waiting for transfers between devices  24.3 us (29%)
  Pallas kernels  10.1 us (12%)
  local copies, waits for them, and re-layouts  3.84 us (5%)
  other arithmetic  1.41 us (2%)
    ppermute x4, waiting for transfers between devices, moved(): return lax.ppermute(shard, axis, pairs)  18.3 us
    all_to_all x1, starting transfers between devices, step(): lax.all_to_all(term, ('x', 'zh'), split_axis=0, concat_axis=0, tiled=True)  12.1 us
    ppermute x4, starting transfers between devices, moved(): return lax.ppermute(shard, axis, pairs)  12 us
    all_to_all x1, starting transfers between devices, step(): lax.all_to_all(copies, ('y', 'zl', 'c'), split_axis=0, concat_axis=0, til...  10.7 us
    pallas_call x1, Pallas kernels, attention_backward(): pl.pallas_call(body, grid=(heads,), in_specs=[pl.BlockSpec((1, rows), lam...  7.07 us
    ppermute x1, waiting for transfers between devices, step(): beyond = lax.ppermute(query_grad, 'zl', swap)  4.91 us
    ppermute x1, starting transfers between devices, step(): beyond = lax.ppermute(query_grad, 'zl', swap)  4.16 us
    pallas_call x1, Pallas kernels, weight_term(): pl.pallas_call(body, out_shape=shape, name='weight_term')  3.03 us
  transfers between devices with their start and end apart: 9, of which 5 were waited for; matrix products, arithmetic and copies ran while one was open for 1% of the time, Pallas kernels for 8%

profile of v3, /device:TPU:1, one launch (start us, length us, event | category | flops | bytes accessed | tf_op | source)
XLA Modules:
  0.0 83.7 jit_solution(13672951985944373847)
XLA Ops:
  0.6 1.0 %copy.9 = bf16[256,256]{0,1:T(8,128)(2,1)S(1)} copy(bf16[256,256]{1,0:T(8,128)(2,1)} %param.6) | data formatting | bytes 262144 | tf_op args[0]
  1.7 1.1 %broadcast_in_dim.3 = bf16[8,4,64,256]{3,2,1,0:T(8,128)(2,1)} broadcast(bf16[4,64,256]{2,1,0:T(8,128)(2,1)S(1)} %bitcast.10), dimensions={1,2,3} | broadcast | bytes 1179648 | tf_op jit(solution)/shard_map/broadcast_in_dim | solution.py:114
  2.8 0.0 copy-start.5
  2.8 10.7 %all-to-all-start = ((bf16[32,64,256]{2,1,0:T(8,128)(2,1)}), bf16[32,64,256]{2,1,0:T(8,128)(2,1)S(1)}, u32[]{:S(2)}, u32[]{:S(2)}) async-start(bf16[32,64,256]{2,1,0:T(8,128)(2,1)} %bitcast.5), calls=%async_computation | async-start | bytes 2097152 | tf_op jit(solution)/shard_map/all_to_all | solution.py:115
  13.5 0.0 copy-done.5
  13.5 3.5 %collective-permute-start = (bf16[2,256,128]{2,1,0:T(8,128)(2,1)S(1)}, bf16[2,256,128]{2,1,0:T(8,128)(2,1)S(1)}, u32[]{:S(2)}, u32[]{:S(2)}) collective-permute-start(bf16[2,256,128]{2,1,0:T(8,128)(2,1)S(1)} %copy-done.5), channel_id=1, source_target_pairs={{0,8},{8,16},{16,24},{24,32},{32,40},{40,48},{48,56},{56,64},{64,7... | collective-permute-start | bytes 393224 | tf_op jit(solution)/shard_map/ppermute | solution.py:20
  17.0 4.6 %collective-permute-start.1 = (bf16[2,256,128]{2,1,0:T(8,128)(2,1)S(1)}, bf16[2,256,128]{2,1,0:T(8,128)(2,1)S(1)}, u32[]{:S(2)}, u32[]{:S(2)}) collective-permute-start(bf16[2,256,128]{2,1,0:T(8,128)(2,1)S(1)} %copy-done.5), channel_id=1, source_target_pairs={{0,16},{8,24},{16,32},{24,40},{32,48},{40,56},{48,64},{56,72},{64,... | collective-permute-start | bytes 393224 | tf_op jit(solution)/shard_map/ppermute | solution.py:20
  21.6 0.0 collective-permute-done.one_ref
  21.6 0.0 copy-start.6
  21.6 4.3 %collective-permute-done.1.two_ref = bf16[2,256,128]{2,1,0:T(8,128)(2,1)S(1)} collective-permute-done((bf16[2,256,128]{2,1,0:T(8,128)(2,1)S(1)}, bf16[2,256,128]{2,1,0:T(8,128)(2,1)S(1)}, u32[]{:S(2)}, u32[]{:S(2)}) %collective-permute-start.1) | collective-permute-done | bytes 131104 | tf_op jit(solution)/shard_map/ppermute | solution.py:20
  25.9 0.0 copy-start.7
  25.9 0.0 copy-done.6
  25.9 0.6 copy-done.7
  26.6 7.1 %attention_backward.1 = (bf16[256,512]{1,0:T(8,128)(2,1)}, f32[2,256,128]{2,1,0:T(8,128)}, bf16[2,256,128]{2,1,0:T(8,128)(2,1)}, bf16[2,256,128]{2,1,0:T(8,128)(2,1)}) custom-call(s32[1,256]{1,0:T(1,128)} %bitcast.12, bf16[256,512]{1,0:T(8,128)(2,1)} %q_ref.1, bf16[256,512]{1,0:T(8,128)(2,1)} %o_ref.1, bf16[256,512]{1,0:T(8,128)(2,1)} %g_ref.1, ...), custom_call_target="tpu_custom_call" | custom-call | tf_op jit(solution)/shard_map/attention_backward/pallas_call | solution.py:73
  33.6 4.2 %collective-permute-start.5 = (bf16[256,512]{1,0:T(8,128)(2,1)}, bf16[256,512]{1,0:T(8,128)(2,1)S(1)}, u32[]{:S(2)}, u32[]{:S(2)}) collective-permute-start(bf16[256,512]{1,0:T(8,128)(2,1)} %get-tuple-element.4.refs_0_), channel_id=1, source_target_pairs={{0,16},{16,0},{1,17},{17,1},{2,18},{18,2},{3,19},{19,3},{4,20},{20... | collective-permute-start | bytes 786440 | tf_op jit(solution)/shard_map/ppermute | solution.py:121
  37.8 1.9 %collective-permute-start.4 = (bf16[256,512]{1,0:T(8,128)(2,1)}, bf16[256,512]{1,0:T(8,128)(2,1)S(1)}, u32[]{:S(2)}, u32[]{:S(2)}) collective-permute-start(bf16[256,512]{1,0:T(8,128)(2,1)} %get-tuple-element.4.refs_0_), channel_id=1, source_target_pairs={{0,8},{8,0},{1,9},{9,1},{2,10},{10,2},{3,11},{11,3},{4,12},{12,4},... | collective-permute-start | bytes 786440 | tf_op jit(solution)/shard_map/ppermute | solution.py:122
  39.7 4.9 %collective-permute-done.5.refs_2_ = bf16[256,512]{1,0:T(8,128)(2,1)S(1)} collective-permute-done((bf16[256,512]{1,0:T(8,128)(2,1)}, bf16[256,512]{1,0:T(8,128)(2,1)S(1)}, u32[]{:S(2)}, u32[]{:S(2)}) %collective-permute-start.5) | collective-permute-done | bytes 262176 | tf_op jit(solution)/shard_map/ppermute | solution.py:121
  44.7 0.0 copy-start.1
  44.7 2.3 %collective-permute-start.6 = (bf16[256,512]{1,0:T(8,128)(2,1)S(1)}, bf16[256,512]{1,0:T(8,128)(2,1)S(1)}, u32[]{:S(2)}, u32[]{:S(2)}) collective-permute-start(bf16[256,512]{1,0:T(8,128)(2,1)S(1)} %collective-permute-done.5.refs_2_), channel_id=1, source_target_pairs={{0,8},{8,0},{1,9},{9,1},{2,10},{10,2},{3,11},{11,3},{4,12},{12,4},... | collective-permute-start | bytes 786440 | tf_op jit(solution)/shard_map/ppermute | solution.py:123
  47.0 0.0 collective-permute-done.4.refs_1_
  47.0 0.0 copy-start.2
  47.0 1.1 %collective-permute-done.6.refs_3_ = bf16[256,512]{1,0:T(8,128)(2,1)S(1)} collective-permute-done((bf16[256,512]{1,0:T(8,128)(2,1)S(1)}, bf16[256,512]{1,0:T(8,128)(2,1)S(1)}, u32[]{:S(2)}, u32[]{:S(2)}) %collective-permute-start.6) | collective-permute-done | bytes 262176 | tf_op jit(solution)/shard_map/ppermute | solution.py:123
  48.1 0.0 copy-start.3
  48.1 0.0 all-to-all-done
  48.1 0.0 copy-start
  48.1 0.0 copy-done.1
  48.1 0.0 copy-done.2
  48.1 0.7 copy-done.3
  48.8 0.4 copy-done
  49.2 3.0 %weight_term.1 = bf16[16,32,512]{2,1,0:T(8,128)(2,1)} custom-call(bf16[8,4,64,256]{3,2,1,0:T(8,128)(2,1)} %bitcast.9, bf16[256,512]{1,0:T(8,128)(2,1)} %get-tuple-element.4.refs_0_, bf16[256,512]{1,0:T(8,128)(2,1)} %copy-done.2, bf16[256,512]{1,0:T(8,128)(2,1)} %copy-done.1, bf16[256,512]{1,0:T(8,128)(2,1)} %copy-done.3), custom_call_target="tpu_custom_call" | custom-call | tf_op jit(solution)/shard_map/weight_term/pallas_call | solution.py:105
  52.2 0.0 copy-start.9
  52.2 0.0 copy-start.8
  52.2 0.0 copy-start.4
  52.2 12.1 %all-to-all-start.1 = ((bf16[16,32,512]{2,1,0:T(8,128)(2,1)}), bf16[16,32,512]{2,1,0:T(8,128)(2,1)S(1)}, u32[]{:S(2)}, u32[]{:S(2)}) async-start(bf16[16,32,512]{2,1,0:T(8,128)(2,1)} %weight_term.1), calls=%async_computation.1 | async-start | bytes 1048576 | tf_op jit(solution)/shard_map/all_to_all | solution.py:129
  64.3 0.0 copy-done.9
  64.3 1.3 %collective-permute-start.3 = (bf16[2,256,128]{2,1,0:T(8,128)(2,1)S(1)}, bf16[2,256,128]{2,1,0:T(8,128)(2,1)S(1)}, u32[]{:S(2)}, u32[]{:S(2)}) collective-permute-start(bf16[2,256,128]{2,1,0:T(8,128)(2,1)S(1)} %copy-done.9), channel_id=1, source_target_pairs={{16,0},{24,8},{32,16},{40,24},{48,32},{56,40},{64,48},{72,56},{80,... | collective-permute-start | bytes 393224 | tf_op jit(solution)/shard_map/ppermute | solution.py:20
  65.6 0.0 copy-done.8
  65.7 2.6 %collective-permute-start.2 = (bf16[2,256,128]{2,1,0:T(8,128)(2,1)S(1)}, bf16[2,256,128]{2,1,0:T(8,128)(2,1)S(1)}, u32[]{:S(2)}, u32[]{:S(2)}) collective-permute-start(bf16[2,256,128]{2,1,0:T(8,128)(2,1)S(1)} %copy-done.8), channel_id=1, source_target_pairs={{8,0},{16,8},{24,16},{32,24},{40,32},{48,40},{56,48},{64,56},{72,6... | collective-permute-start | bytes 393224 | tf_op jit(solution)/shard_map/ppermute | solution.py:20
  68.2 12.0 %collective-permute-done.3 = bf16[2,256,128]{2,1,0:T(8,128)(2,1)S(1)} collective-permute-done((bf16[2,256,128]{2,1,0:T(8,128)(2,1)S(1)}, bf16[2,256,128]{2,1,0:T(8,128)(2,1)S(1)}, u32[]{:S(2)}, u32[]{:S(2)}) %collective-permute-start.3) | collective-permute-done | bytes 131104 | tf_op jit(solution)/shard_map/ppermute | solution.py:20
  80.2 2.0 %collective-permute-done.2 = bf16[2,256,128]{2,1,0:T(8,128)(2,1)S(1)} collective-permute-done((bf16[2,256,128]{2,1,0:T(8,128)(2,1)S(1)}, bf16[2,256,128]{2,1,0:T(8,128)(2,1)S(1)}, u32[]{:S(2)}, u32[]{:S(2)}) %collective-permute-start.2) | collective-permute-done | bytes 131104 | tf_op jit(solution)/shard_map/ppermute | solution.py:20
  82.2 0.0 copy-done.4
  82.2 0.7 add_convert_fusion
  82.9 0.0 all-to-all-done.1
  83.0 0.7 convert_reduce_fusion
  (1 shorter events, 0.0 us)
Async XLA Ops:
  2.8 10.7 %copy-start.5 = (bf16[2,256,128]{2,1,0:T(8,128)(2,1)S(1)}, bf16[2,256,128]{2,1,0:T(8,128)(2,1)}, u32[]{:S(2)}) copy-start(bf16[2,256,128]{2,1,0:T(8,128)(2,1)} %near_ref.1) | copy-start | bytes 393220
  2.8 45.3 %all-to-all-start = ((bf16[32,64,256]{2,1,0:T(8,128)(2,1)}), bf16[32,64,256]{2,1,0:T(8,128)(2,1)S(1)}, u32[]{:S(2)}, u32[]{:S(2)}) async-start(bf16[32,64,256]{2,1,0:T(8,128)(2,1)} %bitcast.5), calls=%async_computation | async-start | bytes 2097152 | tf_op jit(solution)/shard_map/all_to_all | solution.py:115
  13.5 8.1 %collective-permute-start = (bf16[2,256,128]{2,1,0:T(8,128)(2,1)S(1)}, bf16[2,256,128]{2,1,0:T(8,128)(2,1)S(1)}, u32[]{:S(2)}, u32[]{:S(2)}) collective-permute-start(bf16[2,256,128]{2,1,0:T(8,128)(2,1)S(1)} %copy-done.5), channel_id=1, source_target_pairs={{0,8},{8,16},{16,24},{24,32},{32,40},{40,48},{48,56},{56,64},{64,7... | collective-permute-start | bytes 393224 | tf_op jit(solution)/shard_map/ppermute | solution.py:20
  17.0 8.9 %collective-permute-start.1 = (bf16[2,256,128]{2,1,0:T(8,128)(2,1)S(1)}, bf16[2,256,128]{2,1,0:T(8,128)(2,1)S(1)}, u32[]{:S(2)}, u32[]{:S(2)}) collective-permute-start(bf16[2,256,128]{2,1,0:T(8,128)(2,1)S(1)} %copy-done.5), channel_id=1, source_target_pairs={{0,16},{8,24},{16,32},{24,40},{32,48},{40,56},{48,64},{56,72},{64,... | collective-permute-start | bytes 393224 | tf_op jit(solution)/shard_map/ppermute | solution.py:20
  21.6 4.3 %copy-start.6 = (bf16[2,256,128]{2,1,0:T(8,128)(2,1)}, bf16[2,256,128]{2,1,0:T(8,128)(2,1)S(1)}, u32[]{:S(2)}) copy-start(bf16[2,256,128]{2,1,0:T(8,128)(2,1)S(1)} %collective-permute-done.one_ref) | copy-start | bytes 393220
  25.9 0.7 copy-start.7
  33.6 11.0 %collective-permute-start.5 = (bf16[256,512]{1,0:T(8,128)(2,1)}, bf16[256,512]{1,0:T(8,128)(2,1)S(1)}, u32[]{:S(2)}, u32[]{:S(2)}) collective-permute-start(bf16[256,512]{1,0:T(8,128)(2,1)} %get-tuple-element.4.refs_0_), channel_id=1, source_target_pairs={{0,16},{16,0},{1,17},{17,1},{2,18},{18,2},{3,19},{19,3},{4,20},{20... | collective-permute-start | bytes 786440 | tf_op jit(solution)/shard_map/ppermute | solution.py:121
  37.8 9.1 %collective-permute-start.4 = (bf16[256,512]{1,0:T(8,128)(2,1)}, bf16[256,512]{1,0:T(8,128)(2,1)S(1)}, u32[]{:S(2)}, u32[]{:S(2)}) collective-permute-start(bf16[256,512]{1,0:T(8,128)(2,1)} %get-tuple-element.4.refs_0_), channel_id=1, source_target_pairs={{0,8},{8,0},{1,9},{9,1},{2,10},{10,2},{3,11},{11,3},{4,12},{12,4},... | collective-permute-start | bytes 786440 | tf_op jit(solution)/shard_map/ppermute | solution.py:122
  44.7 3.5 %copy-start.1 = (bf16[256,512]{1,0:T(8,128)(2,1)}, bf16[256,512]{1,0:T(8,128)(2,1)S(1)}, u32[]{:S(2)}) copy-start(bf16[256,512]{1,0:T(8,128)(2,1)S(1)} %collective-permute-done.5.refs_2_) | copy-start | bytes 786436
  44.7 3.4 %collective-permute-start.6 = (bf16[256,512]{1,0:T(8,128)(2,1)S(1)}, bf16[256,512]{1,0:T(8,128)(2,1)S(1)}, u32[]{:S(2)}, u32[]{:S(2)}) collective-permute-start(bf16[256,512]{1,0:T(8,128)(2,1)S(1)} %collective-permute-done.5.refs_2_), channel_id=1, source_target_pairs={{0,8},{8,0},{1,9},{9,1},{2,10},{10,2},{3,11},{11,3},{4,12},{12,4},... | collective-permute-start | bytes 786440 | tf_op jit(solution)/shard_map/ppermute | solution.py:123
  47.0 1.1 %copy-start.2 = (bf16[256,512]{1,0:T(8,128)(2,1)}, bf16[256,512]{1,0:T(8,128)(2,1)S(1)}, u32[]{:S(2)}) copy-start(bf16[256,512]{1,0:T(8,128)(2,1)S(1)} %collective-permute-done.4.refs_1_) | copy-start | bytes 786436
  48.1 0.7 copy-start.3
  48.1 1.1 %copy-start = (bf16[32,64,256]{2,1,0:T(8,128)(2,1)}, bf16[32,64,256]{2,1,0:T(8,128)(2,1)S(1)}, u32[]{:S(2)}) copy-start(bf16[32,64,256]{2,1,0:T(8,128)(2,1)S(1)} %all-to-all-done) | copy-start | bytes 3145732
  52.2 12.1 %copy-start.9 = (bf16[2,256,128]{2,1,0:T(8,128)(2,1)S(1)}, bf16[2,256,128]{2,1,0:T(8,128)(2,1)}, u32[]{:S(2)}) copy-start(bf16[2,256,128]{2,1,0:T(8,128)(2,1)} %get-tuple-element.10) | copy-start | bytes 393220
  52.2 13.4 %copy-start.8 = (bf16[2,256,128]{2,1,0:T(8,128)(2,1)S(1)}, bf16[2,256,128]{2,1,0:T(8,128)(2,1)}, u32[]{:S(2)}) copy-start(bf16[2,256,128]{2,1,0:T(8,128)(2,1)} %get-tuple-element.9) | copy-start | bytes 393220
  52.2 30.0 %copy-start.4 = (f32[2,256,128]{2,1,0:T(8,128)S(1)}, f32[2,256,128]{2,1,0:T(8,128)}, u32[]{:S(2)}) copy-start(f32[2,256,128]{2,1,0:T(8,128)} %get-tuple-element.8) | copy-start | bytes 786436
  52.2 30.7 %all-to-all-start.1 = ((bf16[16,32,512]{2,1,0:T(8,128)(2,1)}), bf16[16,32,512]{2,1,0:T(8,128)(2,1)S(1)}, u32[]{:S(2)}, u32[]{:S(2)}) async-start(bf16[16,32,512]{2,1,0:T(8,128)(2,1)} %weight_term.1), calls=%async_computation.1 | async-start | bytes 1048576 | tf_op jit(solution)/shard_map/all_to_all | solution.py:129
  64.3 15.8 %collective-permute-start.3 = (bf16[2,256,128]{2,1,0:T(8,128)(2,1)S(1)}, bf16[2,256,128]{2,1,0:T(8,128)(2,1)S(1)}, u32[]{:S(2)}, u32[]{:S(2)}) collective-permute-start(bf16[2,256,128]{2,1,0:T(8,128)(2,1)S(1)} %copy-done.9), channel_id=1, source_target_pairs={{16,0},{24,8},{32,16},{40,24},{48,32},{56,40},{64,48},{72,56},{80,... | collective-permute-start | bytes 393224 | tf_op jit(solution)/shard_map/ppermute | solution.py:20
  65.7 16.6 %collective-permute-start.2 = (bf16[2,256,128]{2,1,0:T(8,128)(2,1)S(1)}, bf16[2,256,128]{2,1,0:T(8,128)(2,1)S(1)}, u32[]{:S(2)}, u32[]{:S(2)}) collective-permute-start(bf16[2,256,128]{2,1,0:T(8,128)(2,1)S(1)} %copy-done.8), channel_id=1, source_target_pairs={{8,0},{16,8},{24,16},{32,24},{40,32},{48,40},{56,48},{64,56},{72,6... | collective-permute-start | bytes 393224 | tf_op jit(solution)/shard_map/ppermute | solution.py:20

commit v4 on v3

--- a/solution.py
+++ b/solution.py
@@ -22,6 +22,10 @@
 
 def dot(a, b, ca, cb):
     return lax.dot_general(a, b, (((ca,), (cb,)), ((), ())), preferred_element_type=jnp.float32)
+
+
+def in_vmem(array):
+    return pltpu.with_memory_space_constraint(array, pltpu.VMEM)
 
 
 def attention_backward(queries, attention_out, output_grad, document_start, near, one, two):
@@ -70,10 +74,11 @@
 
     by_head = pl.BlockSpec((rows, HD), lambda h: (0, h))
     pair = pl.BlockSpec((2, rows, HD), lambda h: (0, 0, 0))
+    whole = pl.BlockSpec(memory_space=pltpu.VMEM)
     return pl.pallas_call(
         body,
         grid=(heads,),
-        in_specs=[pl.BlockSpec((1, rows), lambda h: (0, 0)), by_head, by_head, by_head, pair, pair, pair],
+        in_specs=[pl.BlockSpec((1, rows), lambda h: (0, 0)), by_head, by_head, by_head, whole, whole, whole],
         out_specs=[by_head, pair, pair, pair],
         out_shape=[
             jax.ShapeDtypeStruct(queries.shape, jnp.bfloat16),
@@ -83,7 +88,23 @@
         ],
         scratch_shapes=[pltpu.VMEM((2, span, HD), jnp.float32)],
         name="attention_backward",
-    )(document_start.reshape(1, rows), queries, attention_out, output_grad, near, one, two)
+    )(document_start.reshape(1, rows), queries, attention_out, output_grad, *map(in_vmem, (near, one, two)))
+
+
+def feature_copies(layer_input):
+    rows, width = layer_input.shape
+    owners = ZL * CS
+    piece = width // (2 * owners)
+
+    def body(x_ref, out_ref):
+        turned = x_ref[...].T.reshape(2, owners, piece, rows)
+        for owner in range(owners):
+            for half in range(2):
+                for y in range(YS):
+                    out_ref[y * owners + owner, pl.ds(half * piece, piece)] = turned[half, owner]
+
+    shape = jax.ShapeDtypeStruct((YS * owners, 2 * piece, rows), layer_input.dtype)
+    return pl.pallas_call(body, out_shape=shape, name="feature_copies")(layer_input)
 
 
 def weight_term(features, gathered):
@@ -102,18 +123,17 @@
         out_ref[...] = total.astype(jnp.bfloat16).reshape(out_ref.shape)
 
     shape = jax.ShapeDtypeStruct((blocks * width // 32, 32, columns), jnp.bfloat16)
-    return pl.pallas_call(body, out_shape=shape, name="weight_term")(features, *gathered)
+    whole = pl.BlockSpec(memory_space=pltpu.VMEM)
+    specs = [whole] * (1 + len(gathered))
+    return pl.pallas_call(body, in_specs=specs, out_shape=shape, name="weight_term")(*map(in_vmem, (features, *gathered)))
 
 
 def step(layer_input, queries, key_values, attention_out, output_grad, document_start):
-    rows, features_here = layer_input.shape
     one = moved(key_values, SEQ, SHARDS, 1, False)
     two = moved(key_values, SEQ, SHARDS, 2, False)
-    parts = layer_input.T.reshape(2, ZL * CS, features_here // (2 * ZL * CS), rows).swapaxes(0, 1)
-    parts = parts.reshape(ZL * CS, features_here // (ZL * CS), rows)
-    copies = jnp.broadcast_to(parts, (YS, *parts.shape)).reshape(YS * ZL * CS, *parts.shape[1:])
+    copies = feature_copies(layer_input)
     features = lax.all_to_all(copies, ("y", "zl", "c"), split_axis=0, concat_axis=0, tiled=True)
-    features = features.reshape(YS, *parts.shape)
+    features = features.reshape(YS, ZL * CS, *copies.shape[1:])
     query_grad, own, part_one, part_two = attention_backward(
         queries, attention_out, output_grad, document_start, key_values, one, two
     )

time: 84.2 us -> 81.9 us (0.973)
  local copies, waits for them, and re-layouts: 3.84 us -> 0.97 us
    unnamed x21 -> x10, local copies, waits for them, and re-layouts: 2.74 us -> 0.97 us
    broadcast_in_dim x1 -> x0, local copies, waits for them, and re-layouts: 1.1 us -> none  [step(): jnp.broadcast_to(parts, (YS, *parts.shape))]
    pallas_call x1 -> x2, Pallas kernels: 3.03 us -> 3.53 us  [the longest x1 2.03 us: feature_copies(): pl.pallas_call(body, out_shape=shape, name='feature_copies')(layer_input)]
where the time goes in v4:
time: 81.9 us; the launch traced here: 81.3 us
  starting transfers between devices  43.1 us (53%)
  waiting for transfers between devices  24.8 us (30%)
  Pallas kernels  10.3 us (13%)
  other arithmetic  1.41 us (2%)
  local copies, waits for them, and re-layouts  0.97 us (1%)
    ppermute x4, waiting for transfers between devices, moved(): return lax.ppermute(shard, axis, pairs)  18.2 us
    all_to_all x1, starting transfers between devices, step(): lax.all_to_all(term, ('x', 'zh'), split_axis=0, concat_axis=0, tiled=True)  12.1 us
    ppermute x4, starting transfers between devices, moved(): return lax.ppermute(shard, axis, pairs)  12 us
    all_to_all x1, starting transfers between devices, step(): lax.all_to_all(copies, ('y', 'zl', 'c'), split_axis=0, concat_axis=0, til...  10.7 us
    pallas_call x1, Pallas kernels, attention_backward(): pl.pallas_call(body, grid=(heads,), in_specs=[pl.BlockSpec((1, rows), lam...  6.76 us
    ppermute x1, waiting for transfers between devices, step(): beyond = lax.ppermute(query_grad, 'zl', swap)  5.44 us
    ppermute x1, starting transfers between devices, step(): beyond = lax.ppermute(query_grad, 'zl', swap)  4.18 us
    ppermute x1, starting transfers between devices, step(): across = lax.ppermute(beyond, 'c', swap)  2.29 us
  transfers between devices with their start and end apart: 9, of which 5 were waited for; matrix products, arithmetic and copies ran while one was open for 1% of the time, Pallas kernels for 8%

profile of v4, /device:TPU:1, one launch (start us, length us, event | category | flops | bytes accessed | tf_op | source)
XLA Modules:
  0.0 81.3 jit_solution(3374113610086261105)
XLA Ops:
  0.6 2.0 %feature_copies.1 = bf16[32,64,256]{2,1,0:T(8,128)(2,1)} custom-call(bf16[256,256]{1,0:T(8,128)(2,1)} %x_ref.1), custom_call_target="tpu_custom_call" | custom-call | tf_op jit(solution)/shard_map/feature_copies/pallas_call | solution.py:107
  2.7 0.0 copy-start.1
  2.7 10.7 %all-to-all-start = ((bf16[32,64,256]{2,1,0:T(8,128)(2,1)}), bf16[32,64,256]{2,1,0:T(8,128)(2,1)S(1)}, u32[]{:S(2)}, u32[]{:S(2)}) async-start(bf16[32,64,256]{2,1,0:T(8,128)(2,1)} %feature_copies.1), calls=%async_computation | async-start | bytes 2097152 | tf_op jit(solution)/shard_map/all_to_all | solution.py:135
  13.4 0.0 copy-done.1
  13.4 3.5 %collective-permute-start = (bf16[2,256,128]{2,1,0:T(8,128)(2,1)S(1)}, bf16[2,256,128]{2,1,0:T(8,128)(2,1)S(1)}, u32[]{:S(2)}, u32[]{:S(2)}) collective-permute-start(bf16[2,256,128]{2,1,0:T(8,128)(2,1)S(1)} %copy-done.1), channel_id=1, source_target_pairs={{0,8},{8,16},{16,24},{24,32},{32,40},{40,48},{48,56},{56,64},{64,7... | collective-permute-start | bytes 393224 | tf_op jit(solution)/shard_map/ppermute | solution.py:20
  16.9 4.6 %collective-permute-start.1 = (bf16[2,256,128]{2,1,0:T(8,128)(2,1)S(1)}, bf16[2,256,128]{2,1,0:T(8,128)(2,1)S(1)}, u32[]{:S(2)}, u32[]{:S(2)}) collective-permute-start(bf16[2,256,128]{2,1,0:T(8,128)(2,1)S(1)} %copy-done.1), channel_id=1, source_target_pairs={{0,16},{8,24},{16,32},{24,40},{32,48},{40,56},{48,64},{56,72},{64,... | collective-permute-start | bytes 393224 | tf_op jit(solution)/shard_map/ppermute | solution.py:20
  21.5 0.0 collective-permute-done.one_ref
  21.5 4.3 %collective-permute-done.1.two_ref = bf16[2,256,128]{2,1,0:T(8,128)(2,1)S(1)} collective-permute-done((bf16[2,256,128]{2,1,0:T(8,128)(2,1)S(1)}, bf16[2,256,128]{2,1,0:T(8,128)(2,1)S(1)}, u32[]{:S(2)}, u32[]{:S(2)}) %collective-permute-start.1) | collective-permute-done | bytes 131104 | tf_op jit(solution)/shard_map/ppermute | solution.py:20
  25.8 6.8 %attention_backward.1 = (bf16[256,512]{1,0:T(8,128)(2,1)}, f32[2,256,128]{2,1,0:T(8,128)}, bf16[2,256,128]{2,1,0:T(8,128)(2,1)}, bf16[2,256,128]{2,1,0:T(8,128)(2,1)}) custom-call(s32[1,256]{1,0:T(1,128)} %bitcast.3, bf16[256,512]{1,0:T(8,128)(2,1)} %q_ref.1, bf16[256,512]{1,0:T(8,128)(2,1)} %o_ref.1, bf16[256,512]{1,0:T(8,128)(2,1)} %g_ref.1, ...), custom_call_target="tpu_custom_call" | custom-call | tf_op jit(solution)/shard_map/attention_backward/pallas_call | solution.py:78
  32.6 4.2 %collective-permute-start.5 = (bf16[256,512]{1,0:T(8,128)(2,1)}, bf16[256,512]{1,0:T(8,128)(2,1)S(1)}, u32[]{:S(2)}, u32[]{:S(2)}) collective-permute-start(bf16[256,512]{1,0:T(8,128)(2,1)} %get-tuple-element.4.refs_0_), channel_id=1, source_target_pairs={{0,16},{16,0},{1,17},{17,1},{2,18},{18,2},{3,19},{19,3},{4,20},{20... | collective-permute-start | bytes 786440 | tf_op jit(solution)/shard_map/ppermute | solution.py:141
  36.8 1.9 %collective-permute-start.4 = (bf16[256,512]{1,0:T(8,128)(2,1)}, bf16[256,512]{1,0:T(8,128)(2,1)S(1)}, u32[]{:S(2)}, u32[]{:S(2)}) collective-permute-start(bf16[256,512]{1,0:T(8,128)(2,1)} %get-tuple-element.4.refs_0_), channel_id=1, source_target_pairs={{0,8},{8,0},{1,9},{9,1},{2,10},{10,2},{3,11},{11,3},{4,12},{12,4},... | collective-permute-start | bytes 786440 | tf_op jit(solution)/shard_map/ppermute | solution.py:142
  38.7 5.4 %collective-permute-done.5.refs_2_ = bf16[256,512]{1,0:T(8,128)(2,1)S(1)} collective-permute-done((bf16[256,512]{1,0:T(8,128)(2,1)}, bf16[256,512]{1,0:T(8,128)(2,1)S(1)}, u32[]{:S(2)}, u32[]{:S(2)}) %collective-permute-start.5) | collective-permute-done | bytes 262176 | tf_op jit(solution)/shard_map/ppermute | solution.py:141
  44.1 2.3 %collective-permute-start.6 = (bf16[256,512]{1,0:T(8,128)(2,1)S(1)}, bf16[256,512]{1,0:T(8,128)(2,1)S(1)}, u32[]{:S(2)}, u32[]{:S(2)}) collective-permute-start(bf16[256,512]{1,0:T(8,128)(2,1)S(1)} %collective-permute-done.5.refs_2_), channel_id=1, source_target_pairs={{0,8},{8,0},{1,9},{9,1},{2,10},{10,2},{3,11},{11,3},{4,12},{12,4},... | collective-permute-start | bytes 786440 | tf_op jit(solution)/shard_map/ppermute | solution.py:143
  46.4 0.0 collective-permute-done.4.refs_1_
  46.5 1.1 %collective-permute-done.6.refs_3_ = bf16[256,512]{1,0:T(8,128)(2,1)S(1)} collective-permute-done((bf16[256,512]{1,0:T(8,128)(2,1)S(1)}, bf16[256,512]{1,0:T(8,128)(2,1)S(1)}, u32[]{:S(2)}, u32[]{:S(2)}) %collective-permute-start.6) | collective-permute-done | bytes 262176 | tf_op jit(solution)/shard_map/ppermute | solution.py:143
  47.6 0.0 all-to-all-done
  47.6 0.0 copy-start
  47.6 0.9 %copy-done = bf16[256,512]{1,0:T(8,128)(2,1)S(1)} copy-done((bf16[256,512]{1,0:T(8,128)(2,1)S(1)}, bf16[256,512]{1,0:T(8,128)(2,1)}, u32[]{:S(2)}) %copy-start) | copy-done | bytes 262168
  48.5 1.5 %weight_term.1 = bf16[16,32,512]{2,1,0:T(8,128)(2,1)} custom-call(bf16[8,4,64,256]{3,2,1,0:T(8,128)(2,1)S(1)} %bitcast.2, bf16[256,512]{1,0:T(8,128)(2,1)S(1)} %copy-done, bf16[256,512]{1,0:T(8,128)(2,1)S(1)} %collective-permute-done.4.refs_1_, bf16[256,512]{1,0:T(8,128)(2,1)S(1)} %collective-permute-done.5.refs_2_, ...), custom_call_target="tpu_custom_call" | custom-call | tf_op jit(solution)/shard_map/weight_term/pallas_call | solution.py:128
  50.0 0.0 copy-start.4
  50.0 0.0 copy-start.3
  50.0 0.0 copy-start.2
  50.0 12.1 %all-to-all-start.1 = ((bf16[16,32,512]{2,1,0:T(8,128)(2,1)}), bf16[16,32,512]{2,1,0:T(8,128)(2,1)S(1)}, u32[]{:S(2)}, u32[]{:S(2)}) async-start(bf16[16,32,512]{2,1,0:T(8,128)(2,1)} %weight_term.1), calls=%async_computation.1 | async-start | bytes 1048576 | tf_op jit(solution)/shard_map/all_to_all | solution.py:149
  62.1 0.0 copy-done.4
  62.1 1.3 %collective-permute-start.3 = (bf16[2,256,128]{2,1,0:T(8,128)(2,1)S(1)}, bf16[2,256,128]{2,1,0:T(8,128)(2,1)S(1)}, u32[]{:S(2)}, u32[]{:S(2)}) collective-permute-start(bf16[2,256,128]{2,1,0:T(8,128)(2,1)S(1)} %copy-done.4), channel_id=1, source_target_pairs={{16,0},{24,8},{32,16},{40,24},{48,32},{56,40},{64,48},{72,56},{80,... | collective-permute-start | bytes 393224 | tf_op jit(solution)/shard_map/ppermute | solution.py:20
  63.4 0.0 copy-done.3
  63.5 2.6 %collective-permute-start.2 = (bf16[2,256,128]{2,1,0:T(8,128)(2,1)S(1)}, bf16[2,256,128]{2,1,0:T(8,128)(2,1)S(1)}, u32[]{:S(2)}, u32[]{:S(2)}) collective-permute-start(bf16[2,256,128]{2,1,0:T(8,128)(2,1)S(1)} %copy-done.3), channel_id=1, source_target_pairs={{8,0},{16,8},{24,16},{32,24},{40,32},{48,40},{56,48},{64,56},{72,6... | collective-permute-start | bytes 393224 | tf_op jit(solution)/shard_map/ppermute | solution.py:20
  66.0 11.6 %collective-permute-done.3 = bf16[2,256,128]{2,1,0:T(8,128)(2,1)S(1)} collective-permute-done((bf16[2,256,128]{2,1,0:T(8,128)(2,1)S(1)}, bf16[2,256,128]{2,1,0:T(8,128)(2,1)S(1)}, u32[]{:S(2)}, u32[]{:S(2)}) %collective-permute-start.3) | collective-permute-done | bytes 131104 | tf_op jit(solution)/shard_map/ppermute | solution.py:20
  77.6 2.3 %collective-permute-done.2 = bf16[2,256,128]{2,1,0:T(8,128)(2,1)S(1)} collective-permute-done((bf16[2,256,128]{2,1,0:T(8,128)(2,1)S(1)}, bf16[2,256,128]{2,1,0:T(8,128)(2,1)S(1)}, u32[]{:S(2)}, u32[]{:S(2)}) %collective-permute-start.2) | collective-permute-done | bytes 131104 | tf_op jit(solution)/shard_map/ppermute | solution.py:20
  79.9 0.0 copy-done.2
  79.9 0.7 add_convert_fusion
  80.6 0.0 all-to-all-done.1
  80.6 0.7 convert_reduce_fusion
Async XLA Ops:
  2.7 10.7 %copy-start.1 = (bf16[2,256,128]{2,1,0:T(8,128)(2,1)S(1)}, bf16[2,256,128]{2,1,0:T(8,128)(2,1)}, u32[]{:S(2)}) copy-start(bf16[2,256,128]{2,1,0:T(8,128)(2,1)} %near_ref.1) | copy-start | bytes 393220
  2.7 44.9 %all-to-all-start = ((bf16[32,64,256]{2,1,0:T(8,128)(2,1)}), bf16[32,64,256]{2,1,0:T(8,128)(2,1)S(1)}, u32[]{:S(2)}, u32[]{:S(2)}) async-start(bf16[32,64,256]{2,1,0:T(8,128)(2,1)} %feature_copies.1), calls=%async_computation | async-start | bytes 2097152 | tf_op jit(solution)/shard_map/all_to_all | solution.py:135
  13.4 8.1 %collective-permute-start = (bf16[2,256,128]{2,1,0:T(8,128)(2,1)S(1)}, bf16[2,256,128]{2,1,0:T(8,128)(2,1)S(1)}, u32[]{:S(2)}, u32[]{:S(2)}) collective-permute-start(bf16[2,256,128]{2,1,0:T(8,128)(2,1)S(1)} %copy-done.1), channel_id=1, source_target_pairs={{0,8},{8,16},{16,24},{24,32},{32,40},{40,48},{48,56},{56,64},{64,7... | collective-permute-start | bytes 393224 | tf_op jit(solution)/shard_map/ppermute | solution.py:20
  16.9 8.9 %collective-permute-start.1 = (bf16[2,256,128]{2,1,0:T(8,128)(2,1)S(1)}, bf16[2,256,128]{2,1,0:T(8,128)(2,1)S(1)}, u32[]{:S(2)}, u32[]{:S(2)}) collective-permute-start(bf16[2,256,128]{2,1,0:T(8,128)(2,1)S(1)} %copy-done.1), channel_id=1, source_target_pairs={{0,16},{8,24},{16,32},{24,40},{32,48},{40,56},{48,64},{56,72},{64,... | collective-permute-start | bytes 393224 | tf_op jit(solution)/shard_map/ppermute | solution.py:20
  32.6 11.6 %collective-permute-start.5 = (bf16[256,512]{1,0:T(8,128)(2,1)}, bf16[256,512]{1,0:T(8,128)(2,1)S(1)}, u32[]{:S(2)}, u32[]{:S(2)}) collective-permute-start(bf16[256,512]{1,0:T(8,128)(2,1)} %get-tuple-element.4.refs_0_), channel_id=1, source_target_pairs={{0,16},{16,0},{1,17},{17,1},{2,18},{18,2},{3,19},{19,3},{4,20},{20... | collective-permute-start | bytes 786440 | tf_op jit(solution)/shard_map/ppermute | solution.py:141
  36.8 9.7 %collective-permute-start.4 = (bf16[256,512]{1,0:T(8,128)(2,1)}, bf16[256,512]{1,0:T(8,128)(2,1)S(1)}, u32[]{:S(2)}, u32[]{:S(2)}) collective-permute-start(bf16[256,512]{1,0:T(8,128)(2,1)} %get-tuple-element.4.refs_0_), channel_id=1, source_target_pairs={{0,8},{8,0},{1,9},{9,1},{2,10},{10,2},{3,11},{11,3},{4,12},{12,4},... | collective-permute-start | bytes 786440 | tf_op jit(solution)/shard_map/ppermute | solution.py:142
  44.1 3.4 %collective-permute-start.6 = (bf16[256,512]{1,0:T(8,128)(2,1)S(1)}, bf16[256,512]{1,0:T(8,128)(2,1)S(1)}, u32[]{:S(2)}, u32[]{:S(2)}) collective-permute-start(bf16[256,512]{1,0:T(8,128)(2,1)S(1)} %collective-permute-done.5.refs_2_), channel_id=1, source_target_pairs={{0,8},{8,0},{1,9},{9,1},{2,10},{10,2},{3,11},{11,3},{4,12},{12,4},... | collective-permute-start | bytes 786440 | tf_op jit(solution)/shard_map/ppermute | solution.py:143
  47.6 1.0 %copy-start = (bf16[256,512]{1,0:T(8,128)(2,1)S(1)}, bf16[256,512]{1,0:T(8,128)(2,1)}, u32[]{:S(2)}) copy-start(bf16[256,512]{1,0:T(8,128)(2,1)} %get-tuple-element.4.refs_0_) | copy-start | bytes 786436
  50.0 12.1 %copy-start.4 = (bf16[2,256,128]{2,1,0:T(8,128)(2,1)S(1)}, bf16[2,256,128]{2,1,0:T(8,128)(2,1)}, u32[]{:S(2)}) copy-start(bf16[2,256,128]{2,1,0:T(8,128)(2,1)} %get-tuple-element.10) | copy-start | bytes 393220
  50.0 13.4 %copy-start.3 = (bf16[2,256,128]{2,1,0:T(8,128)(2,1)S(1)}, bf16[2,256,128]{2,1,0:T(8,128)(2,1)}, u32[]{:S(2)}) copy-start(bf16[2,256,128]{2,1,0:T(8,128)(2,1)} %get-tuple-element.9) | copy-start | bytes 393220
  50.0 29.9 %copy-start.2 = (f32[2,256,128]{2,1,0:T(8,128)S(1)}, f32[2,256,128]{2,1,0:T(8,128)}, u32[]{:S(2)}) copy-start(f32[2,256,128]{2,1,0:T(8,128)} %get-tuple-element.8) | copy-start | bytes 786436
  50.0 30.6 %all-to-all-start.1 = ((bf16[16,32,512]{2,1,0:T(8,128)(2,1)}), bf16[16,32,512]{2,1,0:T(8,128)(2,1)S(1)}, u32[]{:S(2)}, u32[]{:S(2)}) async-start(bf16[16,32,512]{2,1,0:T(8,128)(2,1)} %weight_term.1), calls=%async_computation.1 | async-start | bytes 1048576 | tf_op jit(solution)/shard_map/all_to_all | solution.py:149
  62.1 15.4 %collective-permute-start.3 = (bf16[2,256,128]{2,1,0:T(8,128)(2,1)S(1)}, bf16[2,256,128]{2,1,0:T(8,128)(2,1)S(1)}, u32[]{:S(2)}, u32[]{:S(2)}) collective-permute-start(bf16[2,256,128]{2,1,0:T(8,128)(2,1)S(1)} %copy-done.4), channel_id=1, source_target_pairs={{16,0},{24,8},{32,16},{40,24},{48,32},{56,40},{64,48},{72,56},{80,... | collective-permute-start | bytes 393224 | tf_op jit(solution)/shard_map/ppermute | solution.py:20
  63.5 16.4 %collective-permute-start.2 = (bf16[2,256,128]{2,1,0:T(8,128)(2,1)S(1)}, bf16[2,256,128]{2,1,0:T(8,128)(2,1)S(1)}, u32[]{:S(2)}, u32[]{:S(2)}) collective-permute-start(bf16[2,256,128]{2,1,0:T(8,128)(2,1)S(1)} %copy-done.3), channel_id=1, source_target_pairs={{8,0},{16,8},{24,16},{32,24},{40,32},{48,40},{56,48},{64,56},{72,6... | collective-permute-start | bytes 393224 | tf_op jit(solution)/shard_map/ppermute | solution.py:20

commit v5 on v4

--- a/solution.py
+++ b/solution.py
@@ -107,25 +107,34 @@
     return pl.pallas_call(body, out_shape=shape, name="feature_copies")(layer_input)
 
 
-def weight_term(features, gathered):
+def weight_term(features, own, gathered):
     blocks, sources, width, tokens = features.shape
-    columns = gathered[0].shape[1]
+    columns = own.shape[1]
 
-    def body(f_ref, *refs):
-        rows, out_ref = refs[:-1], refs[-1]
-        own = CS * lax.axis_index("zl") + lax.axis_index("c")
-        swapped = CS * lax.axis_index("zl") + 1 - lax.axis_index("c")
-        total = None
-        for source, row in zip((own, swapped, sources - 1 - swapped, sources - 1 - own), rows):
+    def body(f_ref, own_ref, beside_ref, beyond_ref, across_ref, out_ref, own_here, arrived):
+        fetch = pltpu.make_async_copy(own_ref, own_here, arrived)
+        fetch.start()
+        here = CS * lax.axis_index("zl") + lax.axis_index("c")
+        partner = CS * lax.axis_index("zl") + 1 - lax.axis_index("c")
+
+        def term(source, rows):
             left = f_ref[:, pl.ds(source, 1)].reshape(blocks * width, tokens)
-            term = dot(left, row[...], 1, 0)
-            total = term if total is None else total + term
+            return dot(left, rows[...], 1, 0)
+
+        total = term(partner, beside_ref) + term(sources - 1 - partner, beyond_ref)
+        total += term(sources - 1 - here, across_ref)
+        fetch.wait()
+        total += term(here, own_here)
         out_ref[...] = total.astype(jnp.bfloat16).reshape(out_ref.shape)
 
-    shape = jax.ShapeDtypeStruct((blocks * width // 32, 32, columns), jnp.bfloat16)
     whole = pl.BlockSpec(memory_space=pltpu.VMEM)
-    specs = [whole] * (1 + len(gathered))
-    return pl.pallas_call(body, in_specs=specs, out_shape=shape, name="weight_term")(*map(in_vmem, (features, *gathered)))
+    return pl.pallas_call(
+        body,
+        in_specs=[whole, pl.BlockSpec(memory_space=pl.ANY), whole, whole, whole],
+        out_shape=jax.ShapeDtypeStruct((blocks * width // 32, 32, columns), jnp.bfloat16),
+        scratch_shapes=[pltpu.VMEM(own.shape, own.dtype), pltpu.SemaphoreType.DMA(())],
+        name="weight_term",
+    )(in_vmem(features), own, *map(in_vmem, gathered))
 
 
 def step(layer_input, queries, key_values, attention_out, output_grad, document_start):
@@ -145,8 +154,10 @@
     back_two = moved(part_two, SEQ, SHARDS, -2, False)
     pair_total = own + back_one.astype(jnp.float32) + back_two.astype(jnp.float32)
     pair_total = pair_total.astype(jnp.bfloat16)
-    term = weight_term(features, (query_grad, beside, beyond, across))
-    arrived = lax.all_to_all(term, ("x", "zh"), split_axis=0, concat_axis=0, tiled=True)
+    term = weight_term(features, query_grad, (beside, beyond, across))
+    arrived = lax.all_to_all(term, "x", split_axis=0, concat_axis=0, tiled=True)
+    summed = arrived.reshape(XS, ZH, *arrived.shape[1:]).astype(jnp.float32).sum(axis=0).astype(jnp.bfloat16)
+    arrived = lax.all_to_all(summed, "zh", split_axis=0, concat_axis=0, tiled=True)
     return query_grad, pair_total, arrived.astype(jnp.float32).sum(axis=0)
 
 

time: 81.9 us -> 85.7 us (1.046)
  the two profiles are of different devices: /device:TPU:1 before, /device:TPU:74 now
where the time goes in v5:
time: 85.7 us; the launch traced here: 85 us
  starting transfers between devices  53.7 us (63%)
  waiting for transfers between devices  17.5 us (20%)
  Pallas kernels  11 us (13%)
  other arithmetic  2.09 us (2%)
    ppermute x4, starting transfers between devices, moved(): return lax.ppermute(shard, axis, pairs)  18 us
    all_to_all x1, starting transfers between devices, step(): lax.all_to_all(summed, 'zh', split_axis=0, concat_axis=0, tiled=True)  10.9 us
    all_to_all x1, starting transfers between devices, step(): lax.all_to_all(copies, ('y', 'zl', 'c'), split_axis=0, concat_axis=0, til...  8.74 us
    all_to_all x1, waiting for transfers between devices, step(): lax.all_to_all(summed, 'zh', split_axis=0, concat_axis=0, tiled=True)  8.01 us
    ppermute x1, starting transfers between devices, step(): beyond = lax.ppermute(query_grad, 'zl', swap)  7.24 us
    pallas_call x1, Pallas kernels, attention_backward(): pl.pallas_call(body, grid=(heads,), in_specs=[pl.BlockSpec((1, rows), lam...  6.77 us
    all_to_all x1, starting transfers between devices, step(): arrived = lax.all_to_all(term, 'x', split_axis=0, concat_axis=0, tiled=True)  4.96 us
    ppermute x1, waiting for transfers between devices, step(): beyond = lax.ppermute(query_grad, 'zl', swap)  4.31 us
  transfers between devices with their start and end apart: 10, of which 4 were waited for; matrix products, arithmetic and copies ran while one was open for 2% of the time, Pallas kernels for 8%

profile of v5, /device:TPU:74, one launch (start us, length us, event | category | flops | bytes accessed | tf_op | source)
XLA Modules:
  0.0 85.0 jit_solution(1506182580017709176)
XLA Ops:
  0.6 2.0 %feature_copies.1 = bf16[32,64,256]{2,1,0:T(8,128)(2,1)} custom-call(bf16[256,256]{1,0:T(8,128)(2,1)} %x_ref.1), custom_call_target="tpu_custom_call" | custom-call | tf_op jit(solution)/shard_map/feature_copies/pallas_call | solution.py:107
  2.6 0.0 copy-start
  2.6 8.7 %all-to-all-start = ((bf16[32,64,256]{2,1,0:T(8,128)(2,1)}), bf16[32,64,256]{2,1,0:T(8,128)(2,1)S(1)}, u32[]{:S(2)}, u32[]{:S(2)}) async-start(bf16[32,64,256]{2,1,0:T(8,128)(2,1)} %feature_copies.1), calls=%async_computation | async-start | bytes 2097152 | tf_op jit(solution)/shard_map/all_to_all | solution.py:144
  11.4 0.0 copy-done
  11.4 2.0 %collective-permute-start = (bf16[2,256,128]{2,1,0:T(8,128)(2,1)S(1)}, bf16[2,256,128]{2,1,0:T(8,128)(2,1)S(1)}, u32[]{:S(2)}, u32[]{:S(2)}) collective-permute-start(bf16[2,256,128]{2,1,0:T(8,128)(2,1)S(1)} %copy-done), channel_id=1, source_target_pairs={{0,8},{8,16},{16,24},{24,32},{32,40},{40,48},{48,56},{56,64},{64,7... | collective-permute-start | bytes 393224 | tf_op jit(solution)/shard_map/ppermute | solution.py:20
  13.4 5.2 %collective-permute-start.1 = (bf16[2,256,128]{2,1,0:T(8,128)(2,1)S(1)}, bf16[2,256,128]{2,1,0:T(8,128)(2,1)S(1)}, u32[]{:S(2)}, u32[]{:S(2)}) collective-permute-start(bf16[2,256,128]{2,1,0:T(8,128)(2,1)S(1)} %copy-done), channel_id=1, source_target_pairs={{0,16},{8,24},{16,32},{24,40},{32,48},{40,56},{48,64},{56,72},{64,... | collective-permute-start | bytes 393224 | tf_op jit(solution)/shard_map/ppermute | solution.py:20
  18.6 0.0 collective-permute-done.one_ref
  18.7 3.7 %collective-permute-done.1.two_ref = bf16[2,256,128]{2,1,0:T(8,128)(2,1)S(1)} collective-permute-done((bf16[2,256,128]{2,1,0:T(8,128)(2,1)S(1)}, bf16[2,256,128]{2,1,0:T(8,128)(2,1)S(1)}, u32[]{:S(2)}, u32[]{:S(2)}) %collective-permute-start.1) | collective-permute-done | bytes 131104 | tf_op jit(solution)/shard_map/ppermute | solution.py:20
  22.3 6.8 %attention_backward.1 = (bf16[256,512]{1,0:T(8,128)(2,1)}, f32[2,256,128]{2,1,0:T(8,128)}, bf16[2,256,128]{2,1,0:T(8,128)(2,1)}, bf16[2,256,128]{2,1,0:T(8,128)(2,1)}) custom-call(s32[1,256]{1,0:T(1,128)} %bitcast.5, bf16[256,512]{1,0:T(8,128)(2,1)} %q_ref.1, bf16[256,512]{1,0:T(8,128)(2,1)} %o_ref.1, bf16[256,512]{1,0:T(8,128)(2,1)} %g_ref.1, ...), custom_call_target="tpu_custom_call" | custom-call | tf_op jit(solution)/shard_map/attention_backward/pallas_call | solution.py:78
  29.1 7.2 %collective-permute-start.5 = (bf16[256,512]{1,0:T(8,128)(2,1)}, bf16[256,512]{1,0:T(8,128)(2,1)S(1)}, u32[]{:S(2)}, u32[]{:S(2)}) collective-permute-start(bf16[256,512]{1,0:T(8,128)(2,1)} %get-tuple-element.4.own_ref), channel_id=1, source_target_pairs={{0,16},{16,0},{1,17},{17,1},{2,18},{18,2},{3,19},{19,3},{4,20},{20... | collective-permute-start | bytes 786440 | tf_op jit(solution)/shard_map/ppermute | solution.py:150
  36.3 1.9 %collective-permute-start.4 = (bf16[256,512]{1,0:T(8,128)(2,1)}, bf16[256,512]{1,0:T(8,128)(2,1)S(1)}, u32[]{:S(2)}, u32[]{:S(2)}) collective-permute-start(bf16[256,512]{1,0:T(8,128)(2,1)} %get-tuple-element.4.own_ref), channel_id=1, source_target_pairs={{0,8},{8,0},{1,9},{9,1},{2,10},{10,2},{3,11},{11,3},{4,12},{12,4},... | collective-permute-start | bytes 786440 | tf_op jit(solution)/shard_map/ppermute | solution.py:151
  38.3 4.3 %collective-permute-done.5.beyond_ref = bf16[256,512]{1,0:T(8,128)(2,1)S(1)} collective-permute-done((bf16[256,512]{1,0:T(8,128)(2,1)}, bf16[256,512]{1,0:T(8,128)(2,1)S(1)}, u32[]{:S(2)}, u32[]{:S(2)}) %collective-permute-start.5) | collective-permute-done | bytes 262176 | tf_op jit(solution)/shard_map/ppermute | solution.py:150
  42.6 1.9 %collective-permute-start.6 = (bf16[256,512]{1,0:T(8,128)(2,1)S(1)}, bf16[256,512]{1,0:T(8,128)(2,1)S(1)}, u32[]{:S(2)}, u32[]{:S(2)}) collective-permute-start(bf16[256,512]{1,0:T(8,128)(2,1)S(1)} %collective-permute-done.5.beyond_ref), channel_id=1, source_target_pairs={{0,8},{8,0},{1,9},{9,1},{2,10},{10,2},{3,11},{11,3},{4,12},{12,4},... | collective-permute-start | bytes 786440 | tf_op jit(solution)/shard_map/ppermute | solution.py:152
  44.5 0.0 collective-permute-done.4.beside_ref
  44.5 1.5 %collective-permute-done.6.across_ref = bf16[256,512]{1,0:T(8,128)(2,1)S(1)} collective-permute-done((bf16[256,512]{1,0:T(8,128)(2,1)S(1)}, bf16[256,512]{1,0:T(8,128)(2,1)S(1)}, u32[]{:S(2)}, u32[]{:S(2)}) %collective-permute-start.6) | collective-permute-done | bytes 262176 | tf_op jit(solution)/shard_map/ppermute | solution.py:152
  46.0 0.0 all-to-all-done
  46.0 2.2 %weight_term.1 = bf16[16,32,512]{2,1,0:T(8,128)(2,1)} custom-call(bf16[8,4,64,256]{3,2,1,0:T(8,128)(2,1)S(1)} %bitcast.3, bf16[256,512]{1,0:T(8,128)(2,1)} %get-tuple-element.4.own_ref, bf16[256,512]{1,0:T(8,128)(2,1)S(1)} %collective-permute-done.4.beside_ref, bf16[256,512]{1,0:T(8,128)(2,1)S(1)} %collective-permute-done.5.beyond_ref, ...), custom_call_target="tpu_custom_call" | custom-call | tf_op jit(solution)/shard_map/weight_term/pallas_call | solution.py:131
  48.2 0.0 copy-start.3
  48.2 0.0 copy-start.2
  48.2 5.0 %all-to-all-start.1 = ((bf16[16,32,512]{2,1,0:T(8,128)(2,1)}), bf16[16,32,512]{2,1,0:T(8,128)(2,1)S(1)}, u32[]{:S(2)}, u32[]{:S(2)}) async-start(bf16[16,32,512]{2,1,0:T(8,128)(2,1)} %weight_term.1), calls=%async_computation.1 | async-start | bytes 1048576 | tf_op jit(solution)/shard_map/all_to_all | solution.py:158
  53.2 0.0 copy-done.3
  53.2 3.5 %collective-permute-start.3 = (bf16[2,256,128]{2,1,0:T(8,128)(2,1)S(1)}, bf16[2,256,128]{2,1,0:T(8,128)(2,1)S(1)}, u32[]{:S(2)}, u32[]{:S(2)}) collective-permute-start(bf16[2,256,128]{2,1,0:T(8,128)(2,1)S(1)} %copy-done.3), channel_id=1, source_target_pairs={{16,0},{24,8},{32,16},{40,24},{48,32},{56,40},{64,48},{72,56},{80,... | collective-permute-start | bytes 393224 | tf_op jit(solution)/shard_map/ppermute | solution.py:20
  56.7 0.0 copy-done.2
  56.7 7.3 %collective-permute-start.2 = (bf16[2,256,128]{2,1,0:T(8,128)(2,1)S(1)}, bf16[2,256,128]{2,1,0:T(8,128)(2,1)S(1)}, u32[]{:S(2)}, u32[]{:S(2)}) collective-permute-start(bf16[2,256,128]{2,1,0:T(8,128)(2,1)S(1)} %copy-done.2), channel_id=1, source_target_pairs={{8,0},{16,8},{24,16},{32,24},{40,32},{48,40},{56,48},{64,56},{72,6... | collective-permute-start | bytes 393224 | tf_op jit(solution)/shard_map/ppermute | solution.py:20
  64.0 0.0 all-to-all-done.1
  64.0 0.7 reduce_sum.21
  64.8 0.0 copy-start.1
  64.8 10.9 %all-to-all-start.2 = ((bf16[4,32,512]{2,1,0:T(8,128)(2,1)}), bf16[4,32,512]{2,1,0:T(8,128)(2,1)S(1)}, u32[]{:S(2)}, u32[]{:S(2)}) async-start(bf16[4,32,512]{2,1,0:T(8,128)(2,1)} %reduce_sum.21), calls=%async_computation.2 | async-start | bytes 262144 | tf_op jit(solution)/shard_map/all_to_all | solution.py:160
  75.7 0.0 collective-permute-done.3
  75.7 0.0 collective-permute-done.2
  75.7 0.0 copy-done.1
  75.7 0.7 add_convert_fusion
  76.4 8.0 %all-to-all-done.2 = bf16[4,32,512]{2,1,0:T(8,128)(2,1)S(1)} async-done(((bf16[4,32,512]{2,1,0:T(8,128)(2,1)}), bf16[4,32,512]{2,1,0:T(8,128)(2,1)S(1)}, u32[]{:S(2)}, u32[]{:S(2)}) %all-to-all-start.2) | async-done | bytes 131104 | tf_op jit(solution)/shard_map/all_to_all | solution.py:160
  84.4 0.6 convert_reduce_fusion
Async XLA Ops:
  2.6 8.7 %copy-start = (bf16[2,256,128]{2,1,0:T(8,128)(2,1)S(1)}, bf16[2,256,128]{2,1,0:T(8,128)(2,1)}, u32[]{:S(2)}) copy-start(bf16[2,256,128]{2,1,0:T(8,128)(2,1)} %near_ref.1) | copy-start | bytes 393220
  2.6 43.4 %all-to-all-start = ((bf16[32,64,256]{2,1,0:T(8,128)(2,1)}), bf16[32,64,256]{2,1,0:T(8,128)(2,1)S(1)}, u32[]{:S(2)}, u32[]{:S(2)}) async-start(bf16[32,64,256]{2,1,0:T(8,128)(2,1)} %feature_copies.1), calls=%async_computation | async-start | bytes 2097152 | tf_op jit(solution)/shard_map/all_to_all | solution.py:144
  11.4 7.2 %collective-permute-start = (bf16[2,256,128]{2,1,0:T(8,128)(2,1)S(1)}, bf16[2,256,128]{2,1,0:T(8,128)(2,1)S(1)}, u32[]{:S(2)}, u32[]{:S(2)}) collective-permute-start(bf16[2,256,128]{2,1,0:T(8,128)(2,1)S(1)} %copy-done), channel_id=1, source_target_pairs={{0,8},{8,16},{16,24},{24,32},{32,40},{40,48},{48,56},{56,64},{64,7... | collective-permute-start | bytes 393224 | tf_op jit(solution)/shard_map/ppermute | solution.py:20
  13.4 8.9 %collective-permute-start.1 = (bf16[2,256,128]{2,1,0:T(8,128)(2,1)S(1)}, bf16[2,256,128]{2,1,0:T(8,128)(2,1)S(1)}, u32[]{:S(2)}, u32[]{:S(2)}) collective-permute-start(bf16[2,256,128]{2,1,0:T(8,128)(2,1)S(1)} %copy-done), channel_id=1, source_target_pairs={{0,16},{8,24},{16,32},{24,40},{32,48},{40,56},{48,64},{56,72},{64,... | collective-permute-start | bytes 393224 | tf_op jit(solution)/shard_map/ppermute | solution.py:20
  29.1 13.5 %collective-permute-start.5 = (bf16[256,512]{1,0:T(8,128)(2,1)}, bf16[256,512]{1,0:T(8,128)(2,1)S(1)}, u32[]{:S(2)}, u32[]{:S(2)}) collective-permute-start(bf16[256,512]{1,0:T(8,128)(2,1)} %get-tuple-element.4.own_ref), channel_id=1, source_target_pairs={{0,16},{16,0},{1,17},{17,1},{2,18},{18,2},{3,19},{19,3},{4,20},{20... | collective-permute-start | bytes 786440 | tf_op jit(solution)/shard_map/ppermute | solution.py:150
  36.3 8.2 %collective-permute-start.4 = (bf16[256,512]{1,0:T(8,128)(2,1)}, bf16[256,512]{1,0:T(8,128)(2,1)S(1)}, u32[]{:S(2)}, u32[]{:S(2)}) collective-permute-start(bf16[256,512]{1,0:T(8,128)(2,1)} %get-tuple-element.4.own_ref), channel_id=1, source_target_pairs={{0,8},{8,0},{1,9},{9,1},{2,10},{10,2},{3,11},{11,3},{4,12},{12,4},... | collective-permute-start | bytes 786440 | tf_op jit(solution)/shard_map/ppermute | solution.py:151
  42.6 3.4 %collective-permute-start.6 = (bf16[256,512]{1,0:T(8,128)(2,1)S(1)}, bf16[256,512]{1,0:T(8,128)(2,1)S(1)}, u32[]{:S(2)}, u32[]{:S(2)}) collective-permute-start(bf16[256,512]{1,0:T(8,128)(2,1)S(1)} %collective-permute-done.5.beyond_ref), channel_id=1, source_target_pairs={{0,8},{8,0},{1,9},{9,1},{2,10},{10,2},{3,11},{11,3},{4,12},{12,4},... | collective-permute-start | bytes 786440 | tf_op jit(solution)/shard_map/ppermute | solution.py:152
  48.2 5.0 %copy-start.3 = (bf16[2,256,128]{2,1,0:T(8,128)(2,1)S(1)}, bf16[2,256,128]{2,1,0:T(8,128)(2,1)}, u32[]{:S(2)}) copy-start(bf16[2,256,128]{2,1,0:T(8,128)(2,1)} %get-tuple-element.10) | copy-start | bytes 393220
  48.2 8.5 %copy-start.2 = (bf16[2,256,128]{2,1,0:T(8,128)(2,1)S(1)}, bf16[2,256,128]{2,1,0:T(8,128)(2,1)}, u32[]{:S(2)}) copy-start(bf16[2,256,128]{2,1,0:T(8,128)(2,1)} %get-tuple-element.9) | copy-start | bytes 393220
  48.2 15.8 %all-to-all-start.1 = ((bf16[16,32,512]{2,1,0:T(8,128)(2,1)}), bf16[16,32,512]{2,1,0:T(8,128)(2,1)S(1)}, u32[]{:S(2)}, u32[]{:S(2)}) async-start(bf16[16,32,512]{2,1,0:T(8,128)(2,1)} %weight_term.1), calls=%async_computation.1 | async-start | bytes 1048576 | tf_op jit(solution)/shard_map/all_to_all | solution.py:158
  53.2 22.5 %collective-permute-start.3 = (bf16[2,256,128]{2,1,0:T(8,128)(2,1)S(1)}, bf16[2,256,128]{2,1,0:T(8,128)(2,1)S(1)}, u32[]{:S(2)}, u32[]{:S(2)}) collective-permute-start(bf16[2,256,128]{2,1,0:T(8,128)(2,1)S(1)} %copy-done.3), channel_id=1, source_target_pairs={{16,0},{24,8},{32,16},{40,24},{48,32},{56,40},{64,48},{72,56},{80,... | collective-permute-start | bytes 393224 | tf_op jit(solution)/shard_map/ppermute | solution.py:20
  56.7 19.0 %collective-permute-start.2 = (bf16[2,256,128]{2,1,0:T(8,128)(2,1)S(1)}, bf16[2,256,128]{2,1,0:T(8,128)(2,1)S(1)}, u32[]{:S(2)}, u32[]{:S(2)}) collective-permute-start(bf16[2,256,128]{2,1,0:T(8,128)(2,1)S(1)} %copy-done.2), channel_id=1, source_target_pairs={{8,0},{16,8},{24,16},{32,24},{40,32},{48,40},{56,48},{64,56},{72,6... | collective-permute-start | bytes 393224 | tf_op jit(solution)/shard_map/ppermute | solution.py:20
  64.8 10.9 %copy-start.1 = (f32[2,256,128]{2,1,0:T(8,128)S(1)}, f32[2,256,128]{2,1,0:T(8,128)}, u32[]{:S(2)}) copy-start(f32[2,256,128]{2,1,0:T(8,128)} %get-tuple-element.8) | copy-start | bytes 786436
  64.8 19.6 %all-to-all-start.2 = ((bf16[4,32,512]{2,1,0:T(8,128)(2,1)}), bf16[4,32,512]{2,1,0:T(8,128)(2,1)S(1)}, u32[]{:S(2)}, u32[]{:S(2)}) async-start(bf16[4,32,512]{2,1,0:T(8,128)(2,1)} %reduce_sum.21), calls=%async_computation.2 | async-start | bytes 262144 | tf_op jit(solution)/shard_map/all_to_all | solution.py:160

commit v6 on v5

--- a/solution.py
+++ b/solution.py
@@ -91,38 +91,50 @@
     )(document_start.reshape(1, rows), queries, attention_out, output_grad, *map(in_vmem, (near, one, two)))
 
 
-def feature_copies(layer_input):
+def feature_halves(layer_input):
     rows, width = layer_input.shape
-    owners = ZL * CS
-    piece = width // (2 * owners)
+    upper = width // (32 * ZL * CS)
 
-    def body(x_ref, out_ref):
-        turned = x_ref[...].T.reshape(2, owners, piece, rows)
-        for owner in range(owners):
-            for half in range(2):
-                for y in range(YS):
-                    out_ref[y * owners + owner, pl.ds(half * piece, piece)] = turned[half, owner]
+    def body(x_ref, keep_ref, send_ref):
+        turned = x_ref[...].T.reshape(upper, ZL, CS, 32, rows)
+        even = lax.axis_index("zl") == 0
+        keep = jnp.where(even, turned[:, 0], turned[:, 1])
+        send = jnp.where(even, turned[:, 1], turned[:, 0])
+        for core in range(CS):
+            keep_ref[core] = keep[:, core].reshape(upper * 32, rows)
+            send_ref[core] = send[:, core].reshape(upper * 32, rows)
 
-    shape = jax.ShapeDtypeStruct((YS * owners, 2 * piece, rows), layer_input.dtype)
-    return pl.pallas_call(body, out_shape=shape, name="feature_copies")(layer_input)
+    shape = jax.ShapeDtypeStruct((CS, upper * 32, rows), layer_input.dtype)
+    return pl.pallas_call(body, out_shape=[shape, shape], name="feature_halves")(layer_input)
+
+
+def feature_copies(kept, got):
+    def body(kept_ref, got_ref, out_ref):
+        for y in range(YS):
+            for core in range(CS):
+                out_ref[y * CS + core, 0] = kept_ref[core]
+                out_ref[y * CS + core, 1] = got_ref[core]
+
+    shape = jax.ShapeDtypeStruct((YS * CS, ZL, *kept.shape[1:]), kept.dtype)
+    return pl.pallas_call(body, out_shape=shape, name="feature_copies")(kept, in_vmem(got))
 
 
 def weight_term(features, own, gathered):
-    blocks, sources, width, tokens = features.shape
+    blocks, _, width, tokens = features.shape
     columns = own.shape[1]
 
     def body(f_ref, own_ref, beside_ref, beyond_ref, across_ref, out_ref, own_here, arrived):
         fetch = pltpu.make_async_copy(own_ref, own_here, arrived)
         fetch.start()
-        here = CS * lax.axis_index("zl") + lax.axis_index("c")
-        partner = CS * lax.axis_index("zl") + 1 - lax.axis_index("c")
+        here = ZL * lax.axis_index("c")
+        partner = ZL - here
 
         def term(source, rows):
             left = f_ref[:, pl.ds(source, 1)].reshape(blocks * width, tokens)
             return dot(left, rows[...], 1, 0)
 
-        total = term(partner, beside_ref) + term(sources - 1 - partner, beyond_ref)
-        total += term(sources - 1 - here, across_ref)
+        total = term(partner, beside_ref) + term(here + 1, beyond_ref)
+        total += term(partner + 1, across_ref)
         fetch.wait()
         total += term(here, own_here)
         out_ref[...] = total.astype(jnp.bfloat16).reshape(out_ref.shape)
@@ -140,13 +152,15 @@
 def step(layer_input, queries, key_values, attention_out, output_grad, document_start):
     one = moved(key_values, SEQ, SHARDS, 1, False)
     two = moved(key_values, SEQ, SHARDS, 2, False)
-    copies = feature_copies(layer_input)
-    features = lax.all_to_all(copies, ("y", "zl", "c"), split_axis=0, concat_axis=0, tiled=True)
-    features = features.reshape(YS, ZL * CS, *copies.shape[1:])
+    swap = [(0, 1), (1, 0)]
+    kept, sent = feature_halves(layer_input)
+    got = lax.ppermute(sent, "zl", swap)
+    copies = feature_copies(kept, got)
+    features = lax.all_to_all(copies, ("y", "c"), split_axis=0, concat_axis=0, tiled=True)
+    features = features.reshape(YS, CS * ZL, *copies.shape[2:])
     query_grad, own, part_one, part_two = attention_backward(
         queries, attention_out, output_grad, document_start, key_values, one, two
     )
-    swap = [(0, 1), (1, 0)]
     beyond = lax.ppermute(query_grad, "zl", swap)
     beside = lax.ppermute(query_grad, "c", swap)
     across = lax.ppermute(beyond, "c", swap)
@@ -155,9 +169,7 @@
     pair_total = own + back_one.astype(jnp.float32) + back_two.astype(jnp.float32)
     pair_total = pair_total.astype(jnp.bfloat16)
     term = weight_term(features, query_grad, (beside, beyond, across))
-    arrived = lax.all_to_all(term, "x", split_axis=0, concat_axis=0, tiled=True)
-    summed = arrived.reshape(XS, ZH, *arrived.shape[1:]).astype(jnp.float32).sum(axis=0).astype(jnp.bfloat16)
-    arrived = lax.all_to_all(summed, "zh", split_axis=0, concat_axis=0, tiled=True)
+    arrived = lax.all_to_all(term, ("x", "zh"), split_axis=0, concat_axis=0, tiled=True)
     return query_grad, pair_total, arrived.astype(jnp.float32).sum(axis=0)
 
 

time: 85.7 us -> 85.6 us (level)
  the two profiles are of different devices: /device:TPU:74 before, /device:TPU:1 now
where the time goes in v6:
time: 85.6 us; the launch traced here: 84.7 us
  starting transfers between devices  47.3 us (55%)
  waiting for transfers between devices  22.6 us (26%)
  Pallas kernels  12.5 us (15%)
  other arithmetic  1.41 us (2%)
    ppermute x4, waiting for transfers between devices, moved(): return lax.ppermute(shard, axis, pairs)  14.9 us
    all_to_all x1, starting transfers between devices, step(): lax.all_to_all(term, ('x', 'zh'), split_axis=0, concat_axis=0, tiled=True)  13.4 us
    ppermute x4, starting transfers between devices, moved(): return lax.ppermute(shard, axis, pairs)  10.5 us
    all_to_all x1, starting transfers between devices, step(): lax.all_to_all(copies, ('y', 'c'), split_axis=0, concat_axis=0, tiled=True)  10.1 us
    pallas_call x1, Pallas kernels, attention_backward(): pl.pallas_call(body, grid=(heads,), in_specs=[pl.BlockSpec((1, rows), lam...  6.76 us
    ppermute x1, starting transfers between devices, step(): got = lax.ppermute(sent, 'zl', swap)  4.81 us
    ppermute x1, waiting for transfers between devices, step(): beyond = lax.ppermute(query_grad, 'zl', swap)  4.76 us
    ppermute x1, starting transfers between devices, step(): beyond = lax.ppermute(query_grad, 'zl', swap)  4.24 us
  transfers between devices with their start and end apart: 10, of which 6 were waited for; matrix products, arithmetic and copies ran while one was open for 1% of the time, Pallas kernels for 8%

profile of v6, /device:TPU:1, one launch (start us, length us, event | category | flops | bytes accessed | tf_op | source)
XLA Modules:
  0.0 84.7 jit_solution(8251617220483790886)
XLA Ops:
  0.6 1.6 %feature_halves.1 = (bf16[2,64,256]{2,1,0:T(8,128)(2,1)}, bf16[2,64,256]{2,1,0:T(8,128)(2,1)}) custom-call(bf16[256,256]{1,0:T(8,128)(2,1)} %x_ref.1), custom_call_target="tpu_custom_call" | custom-call | tf_op jit(solution)/shard_map/feature_halves/pallas_call | solution.py:108
  2.3 4.8 %collective-permute-start.4 = (bf16[2,64,256]{2,1,0:T(8,128)(2,1)}, bf16[2,64,256]{2,1,0:T(8,128)(2,1)S(1)}, u32[]{:S(2)}, u32[]{:S(2)}) collective-permute-start(bf16[2,64,256]{2,1,0:T(8,128)(2,1)} %get-tuple-element.14), channel_id=1, source_target_pairs={{0,16},{16,0},{1,17},{17,1},{2,18},{18,2},{3,19},{19,3},{4,20},{20... | collective-permute-start | bytes 196616 | tf_op jit(solution)/shard_map/ppermute | solution.py:157
  7.1 1.9 %collective-permute-done.4.got_ref = bf16[2,64,256]{2,1,0:T(8,128)(2,1)S(1)} collective-permute-done((bf16[2,64,256]{2,1,0:T(8,128)(2,1)}, bf16[2,64,256]{2,1,0:T(8,128)(2,1)S(1)}, u32[]{:S(2)}, u32[]{:S(2)}) %collective-permute-start.4) | collective-permute-done | bytes 65568 | tf_op jit(solution)/shard_map/ppermute | solution.py:157
  8.9 1.9 %feature_copies.1 = bf16[16,2,64,256]{3,2,1,0:T(8,128)(2,1)} custom-call(bf16[2,64,256]{2,1,0:T(8,128)(2,1)} %get-tuple-element.13.kept_ref, bf16[2,64,256]{2,1,0:T(8,128)(2,1)S(1)} %collective-permute-done.4.got_ref), custom_call_target="tpu_custom_call" | custom-call | tf_op jit(solution)/shard_map/feature_copies/pallas_call | solution.py:119
  10.8 0.0 copy-start
  10.8 10.1 %all-to-all-start = ((bf16[16,2,64,256]{3,2,1,0:T(8,128)(2,1)}), bf16[16,2,64,256]{3,2,1,0:T(8,128)(2,1)S(1)}, u32[]{:S(2)}, u32[]{:S(2)}) async-start(bf16[16,2,64,256]{3,2,1,0:T(8,128)(2,1)} %feature_copies.1), calls=%async_computation | async-start | bytes 2097152 | tf_op jit(solution)/shard_map/all_to_all | solution.py:159
  20.9 0.0 copy-done
  20.9 2.3 %collective-permute-start = (bf16[2,256,128]{2,1,0:T(8,128)(2,1)S(1)}, bf16[2,256,128]{2,1,0:T(8,128)(2,1)S(1)}, u32[]{:S(2)}, u32[]{:S(2)}) collective-permute-start(bf16[2,256,128]{2,1,0:T(8,128)(2,1)S(1)} %copy-done), channel_id=1, source_target_pairs={{0,8},{8,16},{16,24},{24,32},{32,40},{40,48},{48,56},{56,64},{64,7... | collective-permute-start | bytes 393224 | tf_op jit(solution)/shard_map/ppermute | solution.py:20
  23.3 4.4 %collective-permute-start.1 = (bf16[2,256,128]{2,1,0:T(8,128)(2,1)S(1)}, bf16[2,256,128]{2,1,0:T(8,128)(2,1)S(1)}, u32[]{:S(2)}, u32[]{:S(2)}) collective-permute-start(bf16[2,256,128]{2,1,0:T(8,128)(2,1)S(1)} %copy-done), channel_id=1, source_target_pairs={{0,16},{8,24},{16,32},{24,40},{32,48},{40,56},{48,64},{56,72},{64,... | collective-permute-start | bytes 393224 | tf_op jit(solution)/shard_map/ppermute | solution.py:20
  27.6 0.0 collective-permute-done.one_ref
  27.6 1.9 %collective-permute-done.1.two_ref = bf16[2,256,128]{2,1,0:T(8,128)(2,1)S(1)} collective-permute-done((bf16[2,256,128]{2,1,0:T(8,128)(2,1)S(1)}, bf16[2,256,128]{2,1,0:T(8,128)(2,1)S(1)}, u32[]{:S(2)}, u32[]{:S(2)}) %collective-permute-start.1) | collective-permute-done | bytes 131104 | tf_op jit(solution)/shard_map/ppermute | solution.py:20
  29.6 6.8 %attention_backward.1 = (bf16[256,512]{1,0:T(8,128)(2,1)}, f32[2,256,128]{2,1,0:T(8,128)}, bf16[2,256,128]{2,1,0:T(8,128)(2,1)}, bf16[2,256,128]{2,1,0:T(8,128)(2,1)}) custom-call(s32[1,256]{1,0:T(1,128)} %bitcast.3, bf16[256,512]{1,0:T(8,128)(2,1)} %q_ref.1, bf16[256,512]{1,0:T(8,128)(2,1)} %o_ref.1, bf16[256,512]{1,0:T(8,128)(2,1)} %g_ref.1, ...), custom_call_target="tpu_custom_call" | custom-call | tf_op jit(solution)/shard_map/attention_backward/pallas_call | solution.py:78
  36.3 4.2 %collective-permute-start.6 = (bf16[256,512]{1,0:T(8,128)(2,1)}, bf16[256,512]{1,0:T(8,128)(2,1)S(1)}, u32[]{:S(2)}, u32[]{:S(2)}) collective-permute-start(bf16[256,512]{1,0:T(8,128)(2,1)} %get-tuple-element.6.own_ref), channel_id=1, source_target_pairs={{0,16},{16,0},{1,17},{17,1},{2,18},{18,2},{3,19},{19,3},{4,20},{20... | collective-permute-start | bytes 786440 | tf_op jit(solution)/shard_map/ppermute | solution.py:164
  40.6 1.9 %collective-permute-start.5 = (bf16[256,512]{1,0:T(8,128)(2,1)}, bf16[256,512]{1,0:T(8,128)(2,1)S(1)}, u32[]{:S(2)}, u32[]{:S(2)}) collective-permute-start(bf16[256,512]{1,0:T(8,128)(2,1)} %get-tuple-element.6.own_ref), channel_id=1, source_target_pairs={{0,8},{8,0},{1,9},{9,1},{2,10},{10,2},{3,11},{11,3},{4,12},{12,4},... | collective-permute-start | bytes 786440 | tf_op jit(solution)/shard_map/ppermute | solution.py:165
  42.5 4.8 %collective-permute-done.6.beyond_ref = bf16[256,512]{1,0:T(8,128)(2,1)S(1)} collective-permute-done((bf16[256,512]{1,0:T(8,128)(2,1)}, bf16[256,512]{1,0:T(8,128)(2,1)S(1)}, u32[]{:S(2)}, u32[]{:S(2)}) %collective-permute-start.6) | collective-permute-done | bytes 262176 | tf_op jit(solution)/shard_map/ppermute | solution.py:164
  47.3 2.3 %collective-permute-start.7 = (bf16[256,512]{1,0:T(8,128)(2,1)S(1)}, bf16[256,512]{1,0:T(8,128)(2,1)S(1)}, u32[]{:S(2)}, u32[]{:S(2)}) collective-permute-start(bf16[256,512]{1,0:T(8,128)(2,1)S(1)} %collective-permute-done.6.beyond_ref), channel_id=1, source_target_pairs={{0,8},{8,0},{1,9},{9,1},{2,10},{10,2},{3,11},{11,3},{4,12},{12,4},... | collective-permute-start | bytes 786440 | tf_op jit(solution)/shard_map/ppermute | solution.py:166
  49.6 0.0 collective-permute-done.5.beside_ref
  49.6 1.1 %collective-permute-done.7.across_ref = bf16[256,512]{1,0:T(8,128)(2,1)S(1)} collective-permute-done((bf16[256,512]{1,0:T(8,128)(2,1)S(1)}, bf16[256,512]{1,0:T(8,128)(2,1)S(1)}, u32[]{:S(2)}, u32[]{:S(2)}) %collective-permute-start.7) | collective-permute-done | bytes 262176 | tf_op jit(solution)/shard_map/ppermute | solution.py:166
  50.7 0.0 all-to-all-done
  50.7 2.2 %weight_term.1 = bf16[16,32,512]{2,1,0:T(8,128)(2,1)} custom-call(bf16[8,4,64,256]{3,2,1,0:T(8,128)(2,1)S(1)} %bitcast.2, bf16[256,512]{1,0:T(8,128)(2,1)} %get-tuple-element.6.own_ref, bf16[256,512]{1,0:T(8,128)(2,1)S(1)} %collective-permute-done.5.beside_ref, bf16[256,512]{1,0:T(8,128)(2,1)S(1)} %collective-permute-done.6.beyond_ref, ...), custom_call_target="tpu_custom_call" | custom-call | tf_op jit(solution)/shard_map/weight_term/pallas_call | solution.py:143
  53.0 0.0 copy-start.3
  53.0 0.0 copy-start.2
  53.0 0.0 copy-start.1
  53.0 13.4 %all-to-all-start.1 = ((bf16[16,32,512]{2,1,0:T(8,128)(2,1)}), bf16[16,32,512]{2,1,0:T(8,128)(2,1)S(1)}, u32[]{:S(2)}, u32[]{:S(2)}) async-start(bf16[16,32,512]{2,1,0:T(8,128)(2,1)} %weight_term.1), calls=%async_computation.1 | async-start | bytes 1048576 | tf_op jit(solution)/shard_map/all_to_all | solution.py:172
  66.4 0.0 copy-done.3
  66.4 1.3 %collective-permute-start.3 = (bf16[2,256,128]{2,1,0:T(8,128)(2,1)S(1)}, bf16[2,256,128]{2,1,0:T(8,128)(2,1)S(1)}, u32[]{:S(2)}, u32[]{:S(2)}) collective-permute-start(bf16[2,256,128]{2,1,0:T(8,128)(2,1)S(1)} %copy-done.3), channel_id=1, source_target_pairs={{16,0},{24,8},{32,16},{40,24},{48,32},{56,40},{64,48},{72,56},{80,... | collective-permute-start | bytes 393224 | tf_op jit(solution)/shard_map/ppermute | solution.py:20
  67.7 0.0 copy-done.2
  67.7 2.6 %collective-permute-start.2 = (bf16[2,256,128]{2,1,0:T(8,128)(2,1)S(1)}, bf16[2,256,128]{2,1,0:T(8,128)(2,1)S(1)}, u32[]{:S(2)}, u32[]{:S(2)}) collective-permute-start(bf16[2,256,128]{2,1,0:T(8,128)(2,1)S(1)} %copy-done.2), channel_id=1, source_target_pairs={{8,0},{16,8},{24,16},{32,24},{40,32},{48,40},{56,48},{64,56},{72,6... | collective-permute-start | bytes 393224 | tf_op jit(solution)/shard_map/ppermute | solution.py:20
  70.3 10.7 %collective-permute-done.3 = bf16[2,256,128]{2,1,0:T(8,128)(2,1)S(1)} collective-permute-done((bf16[2,256,128]{2,1,0:T(8,128)(2,1)S(1)}, bf16[2,256,128]{2,1,0:T(8,128)(2,1)S(1)}, u32[]{:S(2)}, u32[]{:S(2)}) %collective-permute-start.3) | collective-permute-done | bytes 131104 | tf_op jit(solution)/shard_map/ppermute | solution.py:20
  81.0 2.2 %collective-permute-done.2 = bf16[2,256,128]{2,1,0:T(8,128)(2,1)S(1)} collective-permute-done((bf16[2,256,128]{2,1,0:T(8,128)(2,1)S(1)}, bf16[2,256,128]{2,1,0:T(8,128)(2,1)S(1)}, u32[]{:S(2)}, u32[]{:S(2)}) %collective-permute-start.2) | collective-permute-done | bytes 131104 | tf_op jit(solution)/shard_map/ppermute | solution.py:20
  83.3 0.0 copy-done.1
  83.3 0.7 add_convert_fusion
  84.0 0.0 all-to-all-done.1
  84.0 0.7 convert_reduce_fusion
Async XLA Ops:
  2.3 6.7 %collective-permute-start.4 = (bf16[2,64,256]{2,1,0:T(8,128)(2,1)}, bf16[2,64,256]{2,1,0:T(8,128)(2,1)S(1)}, u32[]{:S(2)}, u32[]{:S(2)}) collective-permute-start(bf16[2,64,256]{2,1,0:T(8,128)(2,1)} %get-tuple-element.14), channel_id=1, source_target_pairs={{0,16},{16,0},{1,17},{17,1},{2,18},{18,2},{3,19},{19,3},{4,20},{20... | collective-permute-start | bytes 196616 | tf_op jit(solution)/shard_map/ppermute | solution.py:157
  10.8 10.1 %copy-start = (bf16[2,256,128]{2,1,0:T(8,128)(2,1)S(1)}, bf16[2,256,128]{2,1,0:T(8,128)(2,1)}, u32[]{:S(2)}) copy-start(bf16[2,256,128]{2,1,0:T(8,128)(2,1)} %near_ref.1) | copy-start | bytes 393220
  10.8 39.9 %all-to-all-start = ((bf16[16,2,64,256]{3,2,1,0:T(8,128)(2,1)}), bf16[16,2,64,256]{3,2,1,0:T(8,128)(2,1)S(1)}, u32[]{:S(2)}, u32[]{:S(2)}) async-start(bf16[16,2,64,256]{3,2,1,0:T(8,128)(2,1)} %feature_copies.1), calls=%async_computation | async-start | bytes 2097152 | tf_op jit(solution)/shard_map/all_to_all | solution.py:159
  20.9 6.7 %collective-permute-start = (bf16[2,256,128]{2,1,0:T(8,128)(2,1)S(1)}, bf16[2,256,128]{2,1,0:T(8,128)(2,1)S(1)}, u32[]{:S(2)}, u32[]{:S(2)}) collective-permute-start(bf16[2,256,128]{2,1,0:T(8,128)(2,1)S(1)} %copy-done), channel_id=1, source_target_pairs={{0,8},{8,16},{16,24},{24,32},{32,40},{40,48},{48,56},{56,64},{64,7... | collective-permute-start | bytes 393224 | tf_op jit(solution)/shard_map/ppermute | solution.py:20
  23.3 6.3 %collective-permute-start.1 = (bf16[2,256,128]{2,1,0:T(8,128)(2,1)S(1)}, bf16[2,256,128]{2,1,0:T(8,128)(2,1)S(1)}, u32[]{:S(2)}, u32[]{:S(2)}) collective-permute-start(bf16[2,256,128]{2,1,0:T(8,128)(2,1)S(1)} %copy-done), channel_id=1, source_target_pairs={{0,16},{8,24},{16,32},{24,40},{32,48},{40,56},{48,64},{56,72},{64,... | collective-permute-start | bytes 393224 | tf_op jit(solution)/shard_map/ppermute | solution.py:20
  36.3 10.9 %collective-permute-start.6 = (bf16[256,512]{1,0:T(8,128)(2,1)}, bf16[256,512]{1,0:T(8,128)(2,1)S(1)}, u32[]{:S(2)}, u32[]{:S(2)}) collective-permute-start(bf16[256,512]{1,0:T(8,128)(2,1)} %get-tuple-element.6.own_ref), channel_id=1, source_target_pairs={{0,16},{16,0},{1,17},{17,1},{2,18},{18,2},{3,19},{19,3},{4,20},{20... | collective-permute-start | bytes 786440 | tf_op jit(solution)/shard_map/ppermute | solution.py:164
  40.6 9.0 %collective-permute-start.5 = (bf16[256,512]{1,0:T(8,128)(2,1)}, bf16[256,512]{1,0:T(8,128)(2,1)S(1)}, u32[]{:S(2)}, u32[]{:S(2)}) collective-permute-start(bf16[256,512]{1,0:T(8,128)(2,1)} %get-tuple-element.6.own_ref), channel_id=1, source_target_pairs={{0,8},{8,0},{1,9},{9,1},{2,10},{10,2},{3,11},{11,3},{4,12},{12,4},... | collective-permute-start | bytes 786440 | tf_op jit(solution)/shard_map/ppermute | solution.py:165
  47.3 3.4 %collective-permute-start.7 = (bf16[256,512]{1,0:T(8,128)(2,1)S(1)}, bf16[256,512]{1,0:T(8,128)(2,1)S(1)}, u32[]{:S(2)}, u32[]{:S(2)}) collective-permute-start(bf16[256,512]{1,0:T(8,128)(2,1)S(1)} %collective-permute-done.6.beyond_ref), channel_id=1, source_target_pairs={{0,8},{8,0},{1,9},{9,1},{2,10},{10,2},{3,11},{11,3},{4,12},{12,4},... | collective-permute-start | bytes 786440 | tf_op jit(solution)/shard_map/ppermute | solution.py:166
  53.0 13.4 %copy-start.3 = (bf16[2,256,128]{2,1,0:T(8,128)(2,1)S(1)}, bf16[2,256,128]{2,1,0:T(8,128)(2,1)}, u32[]{:S(2)}) copy-start(bf16[2,256,128]{2,1,0:T(8,128)(2,1)} %get-tuple-element.12) | copy-start | bytes 393220
  53.0 14.7 %copy-start.2 = (bf16[2,256,128]{2,1,0:T(8,128)(2,1)S(1)}, bf16[2,256,128]{2,1,0:T(8,128)(2,1)}, u32[]{:S(2)}) copy-start(bf16[2,256,128]{2,1,0:T(8,128)(2,1)} %get-tuple-element.11) | copy-start | bytes 393220
  53.0 30.3 %copy-start.1 = (f32[2,256,128]{2,1,0:T(8,128)S(1)}, f32[2,256,128]{2,1,0:T(8,128)}, u32[]{:S(2)}) copy-start(f32[2,256,128]{2,1,0:T(8,128)} %get-tuple-element.10) | copy-start | bytes 786436
  53.0 31.0 %all-to-all-start.1 = ((bf16[16,32,512]{2,1,0:T(8,128)(2,1)}), bf16[16,32,512]{2,1,0:T(8,128)(2,1)S(1)}, u32[]{:S(2)}, u32[]{:S(2)}) async-start(bf16[16,32,512]{2,1,0:T(8,128)(2,1)} %weight_term.1), calls=%async_computation.1 | async-start | bytes 1048576 | tf_op jit(solution)/shard_map/all_to_all | solution.py:172
  66.4 14.6 %collective-permute-start.3 = (bf16[2,256,128]{2,1,0:T(8,128)(2,1)S(1)}, bf16[2,256,128]{2,1,0:T(8,128)(2,1)S(1)}, u32[]{:S(2)}, u32[]{:S(2)}) collective-permute-start(bf16[2,256,128]{2,1,0:T(8,128)(2,1)S(1)} %copy-done.3), channel_id=1, source_target_pairs={{16,0},{24,8},{32,16},{40,24},{48,32},{56,40},{64,48},{72,56},{80,... | collective-permute-start | bytes 393224 | tf_op jit(solution)/shard_map/ppermute | solution.py:20
  67.7 15.5 %collective-permute-start.2 = (bf16[2,256,128]{2,1,0:T(8,128)(2,1)S(1)}, bf16[2,256,128]{2,1,0:T(8,128)(2,1)S(1)}, u32[]{:S(2)}, u32[]{:S(2)}) collective-permute-start(bf16[2,256,128]{2,1,0:T(8,128)(2,1)S(1)} %copy-done.2), channel_id=1, source_target_pairs={{8,0},{16,8},{24,16},{32,24},{40,32},{48,40},{56,48},{64,56},{72,6... | collective-permute-start | bytes 393224 | tf_op jit(solution)/shard_map/ppermute | solution.py:20

commit v7 on v5

--- a/solution.py
+++ b/solution.py
@@ -1,3 +1,4 @@
+import functools
 import math
 
 import jax
@@ -10,6 +11,7 @@
 
 HD = 128
 REACH = 2
+BLOCK = 256
 SEQ = ("x", "zh", "zl", "c")
 XS, ZH, ZL, CS, YS = 4, 4, 2, 2, 8
 SHARDS = XS * ZH * ZL * CS
@@ -39,32 +41,34 @@
         first = lax.axis_index(SEQ) * rows - REACH * rows
         q = q_ref[...]
         g = g_ref[...]
-        keys = jnp.concatenate([two_ref[0], one_ref[0], near_ref[0]], axis=0)
-        values = jnp.concatenate([two_ref[1], one_ref[1], near_ref[1]], axis=0)
-        key_at = lax.broadcasted_iota(jnp.int32, (span, rows), 0)
+        starting = starts[...] - first
         query_at = lax.broadcasted_iota(jnp.int32, (1, rows), 1) + REACH * rows
-        allowed = (key_at >= starts[...] - first) & (key_at <= query_at)
-        scores = jnp.where(allowed, dot(keys, q, 1, 1) * scaling, -jnp.inf)
-        row_max = jnp.max(scores, axis=0, keepdims=True)
-        powers = jnp.exp(scores - row_max)
-        weights = powers * (1.0 / jnp.sum(powers, axis=0, keepdims=True))
+        blocks = [(ref, at) for ref in (two_ref, one_ref, near_ref) for at in range(0, rows, BLOCK)]
+        scores = []
+        for n, (ref, at) in enumerate(blocks):
+            key_at = lax.broadcasted_iota(jnp.int32, (BLOCK, rows), 0) + n * BLOCK
+            allowed = (key_at >= starting) & (key_at <= query_at)
+            scores.append(jnp.where(allowed, dot(ref[0, pl.ds(at, BLOCK)], q, 1, 1), -jnp.inf))
+        row_max = functools.reduce(jnp.maximum, [jnp.max(s, axis=0, keepdims=True) for s in scores])
+        powers = [jnp.exp2((s - row_max) * (scaling * math.log2(math.e))) for s in scores]
+        inverse = 1.0 / sum(jnp.sum(p, axis=0, keepdims=True) for p in powers)
         product = g.astype(jnp.float32) * o_ref[...].astype(jnp.float32)
         delta = jnp.sum(product.T, axis=0, keepdims=True)
-        dot_grad = dot(values, g, 1, 1)
-        score_grad = (weights * (dot_grad - delta) * scaling).astype(jnp.bfloat16)
-        value_part = dot(weights.astype(jnp.bfloat16), g, 1, 0)
-        key_part = dot(score_grad, q, 1, 0)
-        dq_ref[...] = dot(keys, score_grad, 0, 0).T.astype(jnp.bfloat16)
 
         @pl.when(head == 0)
         def _():
-            acc[0] = key_part
-            acc[1] = value_part
+            acc[...] = jnp.zeros_like(acc)
 
-        @pl.when(head > 0)
-        def _():
-            acc[0] += key_part
-            acc[1] += value_part
+        query_part = None
+        for n, (ref, at) in enumerate(blocks):
+            weights = powers[n] * inverse
+            dot_grad = dot(ref[1, pl.ds(at, BLOCK)], g, 1, 1)
+            score_grad = (weights * (dot_grad - delta) * scaling).astype(jnp.bfloat16)
+            acc[1, pl.ds(n * BLOCK, BLOCK)] += dot(weights.astype(jnp.bfloat16), g, 1, 0)
+            acc[0, pl.ds(n * BLOCK, BLOCK)] += dot(score_grad, q, 1, 0)
+            part = dot(ref[0, pl.ds(at, BLOCK)], score_grad, 0, 0)
+            query_part = part if query_part is None else query_part + part
+        dq_ref[...] = query_part.T.astype(jnp.bfloat16)
 
         @pl.when(head == heads - 1)
         def _():
@@ -155,9 +159,7 @@
     pair_total = own + back_one.astype(jnp.float32) + back_two.astype(jnp.float32)
     pair_total = pair_total.astype(jnp.bfloat16)
     term = weight_term(features, query_grad, (beside, beyond, across))
-    arrived = lax.all_to_all(term, "x", split_axis=0, concat_axis=0, tiled=True)
-    summed = arrived.reshape(XS, ZH, *arrived.shape[1:]).astype(jnp.float32).sum(axis=0).astype(jnp.bfloat16)
-    arrived = lax.all_to_all(summed, "zh", split_axis=0, concat_axis=0, tiled=True)
+    arrived = lax.all_to_all(term, ("x", "zh"), split_axis=0, concat_axis=0, tiled=True)
     return query_grad, pair_total, arrived.astype(jnp.float32).sum(axis=0)
 
 

time: 85.7 us -> 81.3 us (0.949)
  the two profiles are of different devices: /device:TPU:74 before, /device:TPU:1 now
where the time goes in v7:
time: 81.3 us; the launch traced here: 80.7 us
  starting transfers between devices  43.2 us (53%)
  waiting for transfers between devices  24.8 us (31%)
  Pallas kernels  10.5 us (13%)
  other arithmetic  1.41 us (2%)
    ppermute x4, waiting for transfers between devices, moved(): return lax.ppermute(shard, axis, pairs)  18.2 us
    all_to_all x1, starting transfers between devices, step(): lax.all_to_all(term, ('x', 'zh'), split_axis=0, concat_axis=0, tiled=True)  12.1 us
    ppermute x4, starting transfers between devices, moved(): return lax.ppermute(shard, axis, pairs)  12 us
    all_to_all x1, starting transfers between devices, step(): lax.all_to_all(copies, ('y', 'zl', 'c'), split_axis=0, concat_axis=0, til...  10.7 us
    pallas_call x1, Pallas kernels, attention_backward(): pl.pallas_call(body, grid=(heads,), in_specs=[pl.BlockSpec((1, rows), lam...  6.33 us
    ppermute x1, waiting for transfers between devices, step(): beyond = lax.ppermute(query_grad, 'zl', swap)  5.52 us
    ppermute x1, starting transfers between devices, step(): beyond = lax.ppermute(query_grad, 'zl', swap)  4.17 us
    ppermute x1, starting transfers between devices, step(): across = lax.ppermute(beyond, 'c', swap)  2.29 us
  transfers between devices with their start and end apart: 9, of which 5 were waited for; matrix products, arithmetic and copies ran while one was open for 1% of the time, Pallas kernels for 8%

profile of v7, /device:TPU:1, one launch (start us, length us, event | category | flops | bytes accessed | tf_op | source)
XLA Modules:
  0.0 80.7 jit_solution(642020887462864599)
XLA Ops:
  0.6 2.0 %feature_copies.1 = bf16[32,64,256]{2,1,0:T(8,128)(2,1)} custom-call(bf16[256,256]{1,0:T(8,128)(2,1)} %x_ref.1), custom_call_target="tpu_custom_call" | custom-call | tf_op jit(solution)/shard_map/feature_copies/pallas_call | solution.py:111
  2.6 0.0 copy-start
  2.6 10.7 %all-to-all-start = ((bf16[32,64,256]{2,1,0:T(8,128)(2,1)}), bf16[32,64,256]{2,1,0:T(8,128)(2,1)S(1)}, u32[]{:S(2)}, u32[]{:S(2)}) async-start(bf16[32,64,256]{2,1,0:T(8,128)(2,1)} %feature_copies.1), calls=%async_computation | async-start | bytes 2097152 | tf_op jit(solution)/shard_map/all_to_all | solution.py:148
  13.3 0.0 copy-done
  13.4 3.5 %collective-permute-start = (bf16[2,256,128]{2,1,0:T(8,128)(2,1)S(1)}, bf16[2,256,128]{2,1,0:T(8,128)(2,1)S(1)}, u32[]{:S(2)}, u32[]{:S(2)}) collective-permute-start(bf16[2,256,128]{2,1,0:T(8,128)(2,1)S(1)} %copy-done), channel_id=1, source_target_pairs={{0,8},{8,16},{16,24},{24,32},{32,40},{40,48},{48,56},{56,64},{64,7... | collective-permute-start | bytes 393224 | tf_op jit(solution)/shard_map/ppermute | solution.py:22
  16.9 4.6 %collective-permute-start.1 = (bf16[2,256,128]{2,1,0:T(8,128)(2,1)S(1)}, bf16[2,256,128]{2,1,0:T(8,128)(2,1)S(1)}, u32[]{:S(2)}, u32[]{:S(2)}) collective-permute-start(bf16[2,256,128]{2,1,0:T(8,128)(2,1)S(1)} %copy-done), channel_id=1, source_target_pairs={{0,16},{8,24},{16,32},{24,40},{32,48},{40,56},{48,64},{56,72},{64,... | collective-permute-start | bytes 393224 | tf_op jit(solution)/shard_map/ppermute | solution.py:22
  21.5 0.0 collective-permute-done.one_ref
  21.5 4.3 %collective-permute-done.1.two_ref = bf16[2,256,128]{2,1,0:T(8,128)(2,1)S(1)} collective-permute-done((bf16[2,256,128]{2,1,0:T(8,128)(2,1)S(1)}, bf16[2,256,128]{2,1,0:T(8,128)(2,1)S(1)}, u32[]{:S(2)}, u32[]{:S(2)}) %collective-permute-start.1) | collective-permute-done | bytes 131104 | tf_op jit(solution)/shard_map/ppermute | solution.py:22
  25.8 6.3 %attention_backward.1 = (bf16[256,512]{1,0:T(8,128)(2,1)}, f32[2,256,128]{2,1,0:T(8,128)}, bf16[2,256,128]{2,1,0:T(8,128)(2,1)}, bf16[2,256,128]{2,1,0:T(8,128)(2,1)}) custom-call(s32[1,256]{1,0:T(1,128)} %bitcast.3, bf16[256,512]{1,0:T(8,128)(2,1)} %q_ref.1, bf16[256,512]{1,0:T(8,128)(2,1)} %o_ref.1, bf16[256,512]{1,0:T(8,128)(2,1)} %g_ref.1, ...), custom_call_target="tpu_custom_call" | custom-call | tf_op jit(solution)/shard_map/attention_backward/pallas_call | solution.py:82
  32.1 4.2 %collective-permute-start.5 = (bf16[256,512]{1,0:T(8,128)(2,1)}, bf16[256,512]{1,0:T(8,128)(2,1)S(1)}, u32[]{:S(2)}, u32[]{:S(2)}) collective-permute-start(bf16[256,512]{1,0:T(8,128)(2,1)} %get-tuple-element.4.own_ref), channel_id=1, source_target_pairs={{0,16},{16,0},{1,17},{17,1},{2,18},{18,2},{3,19},{19,3},{4,20},{20... | collective-permute-start | bytes 786440 | tf_op jit(solution)/shard_map/ppermute | solution.py:154
  36.3 1.9 %collective-permute-start.4 = (bf16[256,512]{1,0:T(8,128)(2,1)}, bf16[256,512]{1,0:T(8,128)(2,1)S(1)}, u32[]{:S(2)}, u32[]{:S(2)}) collective-permute-start(bf16[256,512]{1,0:T(8,128)(2,1)} %get-tuple-element.4.own_ref), channel_id=1, source_target_pairs={{0,8},{8,0},{1,9},{9,1},{2,10},{10,2},{3,11},{11,3},{4,12},{12,4},... | collective-permute-start | bytes 786440 | tf_op jit(solution)/shard_map/ppermute | solution.py:155
  38.2 5.5 %collective-permute-done.5.beyond_ref = bf16[256,512]{1,0:T(8,128)(2,1)S(1)} collective-permute-done((bf16[256,512]{1,0:T(8,128)(2,1)}, bf16[256,512]{1,0:T(8,128)(2,1)S(1)}, u32[]{:S(2)}, u32[]{:S(2)}) %collective-permute-start.5) | collective-permute-done | bytes 262176 | tf_op jit(solution)/shard_map/ppermute | solution.py:154
  43.8 2.3 %collective-permute-start.6 = (bf16[256,512]{1,0:T(8,128)(2,1)S(1)}, bf16[256,512]{1,0:T(8,128)(2,1)S(1)}, u32[]{:S(2)}, u32[]{:S(2)}) collective-permute-start(bf16[256,512]{1,0:T(8,128)(2,1)S(1)} %collective-permute-done.5.beyond_ref), channel_id=1, source_target_pairs={{0,8},{8,0},{1,9},{9,1},{2,10},{10,2},{3,11},{11,3},{4,12},{12,4},... | collective-permute-start | bytes 786440 | tf_op jit(solution)/shard_map/ppermute | solution.py:156
  46.1 0.0 collective-permute-done.4.beside_ref
  46.1 1.1 %collective-permute-done.6.across_ref = bf16[256,512]{1,0:T(8,128)(2,1)S(1)} collective-permute-done((bf16[256,512]{1,0:T(8,128)(2,1)S(1)}, bf16[256,512]{1,0:T(8,128)(2,1)S(1)}, u32[]{:S(2)}, u32[]{:S(2)}) %collective-permute-start.6) | collective-permute-done | bytes 262176 | tf_op jit(solution)/shard_map/ppermute | solution.py:156
  47.2 0.0 all-to-all-done
  47.2 2.1 %weight_term.1 = bf16[16,32,512]{2,1,0:T(8,128)(2,1)} custom-call(bf16[8,4,64,256]{3,2,1,0:T(8,128)(2,1)S(1)} %bitcast.2, bf16[256,512]{1,0:T(8,128)(2,1)} %get-tuple-element.4.own_ref, bf16[256,512]{1,0:T(8,128)(2,1)S(1)} %collective-permute-done.4.beside_ref, bf16[256,512]{1,0:T(8,128)(2,1)S(1)} %collective-permute-done.5.beyond_ref, ...), custom_call_target="tpu_custom_call" | custom-call | tf_op jit(solution)/shard_map/weight_term/pallas_call | solution.py:135
  49.4 0.0 copy-start.3
  49.4 0.0 copy-start.2
  49.4 0.0 copy-start.1
  49.4 12.1 %all-to-all-start.1 = ((bf16[16,32,512]{2,1,0:T(8,128)(2,1)}), bf16[16,32,512]{2,1,0:T(8,128)(2,1)S(1)}, u32[]{:S(2)}, u32[]{:S(2)}) async-start(bf16[16,32,512]{2,1,0:T(8,128)(2,1)} %weight_term.1), calls=%async_computation.1 | async-start | bytes 1048576 | tf_op jit(solution)/shard_map/all_to_all | solution.py:162
  61.5 0.0 copy-done.3
  61.6 1.3 %collective-permute-start.3 = (bf16[2,256,128]{2,1,0:T(8,128)(2,1)S(1)}, bf16[2,256,128]{2,1,0:T(8,128)(2,1)S(1)}, u32[]{:S(2)}, u32[]{:S(2)}) collective-permute-start(bf16[2,256,128]{2,1,0:T(8,128)(2,1)S(1)} %copy-done.3), channel_id=1, source_target_pairs={{16,0},{24,8},{32,16},{40,24},{48,32},{56,40},{64,48},{72,56},{80,... | collective-permute-start | bytes 393224 | tf_op jit(solution)/shard_map/ppermute | solution.py:22
  62.9 0.0 copy-done.2
  62.9 2.6 %collective-permute-start.2 = (bf16[2,256,128]{2,1,0:T(8,128)(2,1)S(1)}, bf16[2,256,128]{2,1,0:T(8,128)(2,1)S(1)}, u32[]{:S(2)}, u32[]{:S(2)}) collective-permute-start(bf16[2,256,128]{2,1,0:T(8,128)(2,1)S(1)} %copy-done.2), channel_id=1, source_target_pairs={{8,0},{16,8},{24,16},{32,24},{40,32},{48,40},{56,48},{64,56},{72,6... | collective-permute-start | bytes 393224 | tf_op jit(solution)/shard_map/ppermute | solution.py:22
  65.4 11.5 %collective-permute-done.3 = bf16[2,256,128]{2,1,0:T(8,128)(2,1)S(1)} collective-permute-done((bf16[2,256,128]{2,1,0:T(8,128)(2,1)S(1)}, bf16[2,256,128]{2,1,0:T(8,128)(2,1)S(1)}, u32[]{:S(2)}, u32[]{:S(2)}) %collective-permute-start.3) | collective-permute-done | bytes 131104 | tf_op jit(solution)/shard_map/ppermute | solution.py:22
  77.0 2.3 %collective-permute-done.2 = bf16[2,256,128]{2,1,0:T(8,128)(2,1)S(1)} collective-permute-done((bf16[2,256,128]{2,1,0:T(8,128)(2,1)S(1)}, bf16[2,256,128]{2,1,0:T(8,128)(2,1)S(1)}, u32[]{:S(2)}, u32[]{:S(2)}) %collective-permute-start.2) | collective-permute-done | bytes 131104 | tf_op jit(solution)/shard_map/ppermute | solution.py:22
  79.3 0.0 copy-done.1
  79.3 0.7 add_convert_fusion
  80.0 0.0 all-to-all-done.1
  80.0 0.7 convert_reduce_fusion
Async XLA Ops:
  2.6 10.7 %copy-start = (bf16[2,256,128]{2,1,0:T(8,128)(2,1)S(1)}, bf16[2,256,128]{2,1,0:T(8,128)(2,1)}, u32[]{:S(2)}) copy-start(bf16[2,256,128]{2,1,0:T(8,128)(2,1)} %near_ref.1) | copy-start | bytes 393220
  2.6 44.6 %all-to-all-start = ((bf16[32,64,256]{2,1,0:T(8,128)(2,1)}), bf16[32,64,256]{2,1,0:T(8,128)(2,1)S(1)}, u32[]{:S(2)}, u32[]{:S(2)}) async-start(bf16[32,64,256]{2,1,0:T(8,128)(2,1)} %feature_copies.1), calls=%async_computation | async-start | bytes 2097152 | tf_op jit(solution)/shard_map/all_to_all | solution.py:148
  13.4 8.1 %collective-permute-start = (bf16[2,256,128]{2,1,0:T(8,128)(2,1)S(1)}, bf16[2,256,128]{2,1,0:T(8,128)(2,1)S(1)}, u32[]{:S(2)}, u32[]{:S(2)}) collective-permute-start(bf16[2,256,128]{2,1,0:T(8,128)(2,1)S(1)} %copy-done), channel_id=1, source_target_pairs={{0,8},{8,16},{16,24},{24,32},{32,40},{40,48},{48,56},{56,64},{64,7... | collective-permute-start | bytes 393224 | tf_op jit(solution)/shard_map/ppermute | solution.py:22
  16.9 8.9 %collective-permute-start.1 = (bf16[2,256,128]{2,1,0:T(8,128)(2,1)S(1)}, bf16[2,256,128]{2,1,0:T(8,128)(2,1)S(1)}, u32[]{:S(2)}, u32[]{:S(2)}) collective-permute-start(bf16[2,256,128]{2,1,0:T(8,128)(2,1)S(1)} %copy-done), channel_id=1, source_target_pairs={{0,16},{8,24},{16,32},{24,40},{32,48},{40,56},{48,64},{56,72},{64,... | collective-permute-start | bytes 393224 | tf_op jit(solution)/shard_map/ppermute | solution.py:22
  32.1 11.6 %collective-permute-start.5 = (bf16[256,512]{1,0:T(8,128)(2,1)}, bf16[256,512]{1,0:T(8,128)(2,1)S(1)}, u32[]{:S(2)}, u32[]{:S(2)}) collective-permute-start(bf16[256,512]{1,0:T(8,128)(2,1)} %get-tuple-element.4.own_ref), channel_id=1, source_target_pairs={{0,16},{16,0},{1,17},{17,1},{2,18},{18,2},{3,19},{19,3},{4,20},{20... | collective-permute-start | bytes 786440 | tf_op jit(solution)/shard_map/ppermute | solution.py:154
  36.3 9.8 %collective-permute-start.4 = (bf16[256,512]{1,0:T(8,128)(2,1)}, bf16[256,512]{1,0:T(8,128)(2,1)S(1)}, u32[]{:S(2)}, u32[]{:S(2)}) collective-permute-start(bf16[256,512]{1,0:T(8,128)(2,1)} %get-tuple-element.4.own_ref), channel_id=1, source_target_pairs={{0,8},{8,0},{1,9},{9,1},{2,10},{10,2},{3,11},{11,3},{4,12},{12,4},... | collective-permute-start | bytes 786440 | tf_op jit(solution)/shard_map/ppermute | solution.py:155
  43.8 3.4 %collective-permute-start.6 = (bf16[256,512]{1,0:T(8,128)(2,1)S(1)}, bf16[256,512]{1,0:T(8,128)(2,1)S(1)}, u32[]{:S(2)}, u32[]{:S(2)}) collective-permute-start(bf16[256,512]{1,0:T(8,128)(2,1)S(1)} %collective-permute-done.5.beyond_ref), channel_id=1, source_target_pairs={{0,8},{8,0},{1,9},{9,1},{2,10},{10,2},{3,11},{11,3},{4,12},{12,4},... | collective-permute-start | bytes 786440 | tf_op jit(solution)/shard_map/ppermute | solution.py:156
  49.4 12.2 %copy-start.3 = (bf16[2,256,128]{2,1,0:T(8,128)(2,1)S(1)}, bf16[2,256,128]{2,1,0:T(8,128)(2,1)}, u32[]{:S(2)}) copy-start(bf16[2,256,128]{2,1,0:T(8,128)(2,1)} %get-tuple-element.10) | copy-start | bytes 393220
  49.4 13.5 %copy-start.2 = (bf16[2,256,128]{2,1,0:T(8,128)(2,1)S(1)}, bf16[2,256,128]{2,1,0:T(8,128)(2,1)}, u32[]{:S(2)}) copy-start(bf16[2,256,128]{2,1,0:T(8,128)(2,1)} %get-tuple-element.9) | copy-start | bytes 393220
  49.4 29.9 %copy-start.1 = (f32[2,256,128]{2,1,0:T(8,128)S(1)}, f32[2,256,128]{2,1,0:T(8,128)}, u32[]{:S(2)}) copy-start(f32[2,256,128]{2,1,0:T(8,128)} %get-tuple-element.8) | copy-start | bytes 786436
  49.4 30.6 %all-to-all-start.1 = ((bf16[16,32,512]{2,1,0:T(8,128)(2,1)}), bf16[16,32,512]{2,1,0:T(8,128)(2,1)S(1)}, u32[]{:S(2)}, u32[]{:S(2)}) async-start(bf16[16,32,512]{2,1,0:T(8,128)(2,1)} %weight_term.1), calls=%async_computation.1 | async-start | bytes 1048576 | tf_op jit(solution)/shard_map/all_to_all | solution.py:162
  61.6 15.4 %collective-permute-start.3 = (bf16[2,256,128]{2,1,0:T(8,128)(2,1)S(1)}, bf16[2,256,128]{2,1,0:T(8,128)(2,1)S(1)}, u32[]{:S(2)}, u32[]{:S(2)}) collective-permute-start(bf16[2,256,128]{2,1,0:T(8,128)(2,1)S(1)} %copy-done.3), channel_id=1, source_target_pairs={{16,0},{24,8},{32,16},{40,24},{48,32},{56,40},{64,48},{72,56},{80,... | collective-permute-start | bytes 393224 | tf_op jit(solution)/shard_map/ppermute | solution.py:22
  62.9 16.4 %collective-permute-start.2 = (bf16[2,256,128]{2,1,0:T(8,128)(2,1)S(1)}, bf16[2,256,128]{2,1,0:T(8,128)(2,1)S(1)}, u32[]{:S(2)}, u32[]{:S(2)}) collective-permute-start(bf16[2,256,128]{2,1,0:T(8,128)(2,1)S(1)} %copy-done.2), channel_id=1, source_target_pairs={{8,0},{16,8},{24,16},{32,24},{40,32},{48,40},{56,48},{64,56},{72,6... | collective-permute-start | bytes 393224 | tf_op jit(solution)/shard_map/ppermute | solution.py:22

commit v8 on v7

--- a/solution.py
+++ b/solution.py
@@ -105,31 +105,35 @@
         for owner in range(owners):
             for half in range(2):
                 for y in range(YS):
-                    out_ref[y * owners + owner, pl.ds(half * piece, piece)] = turned[half, owner]
+                    place = (owner % CS * ZL + owner // CS) * YS + y
+                    out_ref[place, pl.ds(half * piece, piece)] = turned[half, owner]
 
     shape = jax.ShapeDtypeStruct((YS * owners, 2 * piece, rows), layer_input.dtype)
     return pl.pallas_call(body, out_shape=shape, name="feature_copies")(layer_input)
 
 
 def weight_term(features, own, gathered):
-    blocks, sources, width, tokens = features.shape
+    sources, blocks, width, tokens = features.shape
     columns = own.shape[1]
 
     def body(f_ref, own_ref, beside_ref, beyond_ref, across_ref, out_ref, own_here, arrived):
         fetch = pltpu.make_async_copy(own_ref, own_here, arrived)
         fetch.start()
-        here = CS * lax.axis_index("zl") + lax.axis_index("c")
-        partner = CS * lax.axis_index("zl") + 1 - lax.axis_index("c")
+        here = ZL * lax.axis_index("c") + lax.axis_index("zl")
+        partner = ZL * (1 - lax.axis_index("c")) + lax.axis_index("zl")
 
         def term(source, rows):
-            left = f_ref[:, pl.ds(source, 1)].reshape(blocks * width, tokens)
+            left = f_ref[pl.ds(source, 1)].reshape(blocks * width, tokens)
             return dot(left, rows[...], 1, 0)
 
         total = term(partner, beside_ref) + term(sources - 1 - partner, beyond_ref)
         total += term(sources - 1 - here, across_ref)
         fetch.wait()
         total += term(here, own_here)
-        out_ref[...] = total.astype(jnp.bfloat16).reshape(out_ref.shape)
+        by_owner = total.astype(jnp.bfloat16).reshape(XS, ZH, *out_ref.shape[1:])
+        for zh in range(ZH):
+            for x in range(XS):
+                out_ref[zh * XS + x] = by_owner[x, zh]
 
     whole = pl.BlockSpec(memory_space=pltpu.VMEM)
     return pl.pallas_call(
@@ -145,8 +149,8 @@
     one = moved(key_values, SEQ, SHARDS, 1, False)
     two = moved(key_values, SEQ, SHARDS, 2, False)
     copies = feature_copies(layer_input)
-    features = lax.all_to_all(copies, ("y", "zl", "c"), split_axis=0, concat_axis=0, tiled=True)
-    features = features.reshape(YS, ZL * CS, *copies.shape[1:])
+    features = lax.all_to_all(copies, ("c", "zl", "y"), split_axis=0, concat_axis=0, tiled=True)
+    features = features.reshape(CS * ZL, YS, *copies.shape[1:])
     query_grad, own, part_one, part_two = attention_backward(
         queries, attention_out, output_grad, document_start, key_values, one, two
     )
@@ -159,7 +163,7 @@
     pair_total = own + back_one.astype(jnp.float32) + back_two.astype(jnp.float32)
     pair_total = pair_total.astype(jnp.bfloat16)
     term = weight_term(features, query_grad, (beside, beyond, across))
-    arrived = lax.all_to_all(term, ("x", "zh"), split_axis=0, concat_axis=0, tiled=True)
+    arrived = lax.all_to_all(term, ("zh", "x"), split_axis=0, concat_axis=0, tiled=True)
     return query_grad, pair_total, arrived.astype(jnp.float32).sum(axis=0)
 
 

time: 81.3 us -> 81.8 us (level)
  no operation moved by 1% of the time
where the time goes in v8:
time: 81.8 us; the launch traced here: 81.2 us
  starting transfers between devices  43.4 us (53%)
  waiting for transfers between devices  24.9 us (30%)
  Pallas kernels  10.6 us (13%)
  other arithmetic  1.41 us (2%)
    ppermute x4, waiting for transfers between devices, moved(): return lax.ppermute(shard, axis, pairs)  17.8 us
    all_to_all x1, starting transfers between devices, step(): lax.all_to_all(term, ('zh', 'x'), split_axis=0, concat_axis=0, tiled=True)  12.7 us
    ppermute x4, starting transfers between devices, moved(): return lax.ppermute(shard, axis, pairs)  12 us
    all_to_all x1, starting transfers between devices, step(): lax.all_to_all(copies, ('c', 'zl', 'y'), split_axis=0, concat_axis=0, til...  10.7 us
    pallas_call x1, Pallas kernels, attention_backward(): pl.pallas_call(body, grid=(heads,), in_specs=[pl.BlockSpec((1, rows), lam...  6.33 us
    ppermute x1, waiting for transfers between devices, step(): beyond = lax.ppermute(query_grad, 'zl', swap)  5.76 us
    ppermute x1, starting transfers between devices, step(): beyond = lax.ppermute(query_grad, 'zl', swap)  4.14 us
    pallas_call x1, Pallas kernels, weight_term(): pl.pallas_call(body, in_specs=[whole, pl.BlockSpec(memory_space=pl.ANY),...  2.25 us
  transfers between devices with their start and end apart: 9, of which 5 were waited for; matrix products, arithmetic and copies ran while one was open for 1% of the time, Pallas kernels for 8%

profile of v8, /device:TPU:1, one launch (start us, length us, event | category | flops | bytes accessed | tf_op | source)
XLA Modules:
  0.0 81.2 jit_solution(12241868049464971390)
XLA Ops:
  0.6 2.0 %feature_copies.1 = bf16[32,64,256]{2,1,0:T(8,128)(2,1)} custom-call(bf16[256,256]{1,0:T(8,128)(2,1)} %x_ref.1), custom_call_target="tpu_custom_call" | custom-call | tf_op jit(solution)/shard_map/feature_copies/pallas_call | solution.py:112
  2.6 0.0 copy-start
  2.6 10.7 %all-to-all-start = ((bf16[32,64,256]{2,1,0:T(8,128)(2,1)}), bf16[32,64,256]{2,1,0:T(8,128)(2,1)S(1)}, u32[]{:S(2)}, u32[]{:S(2)}) async-start(bf16[32,64,256]{2,1,0:T(8,128)(2,1)} %feature_copies.1), calls=%async_computation | async-start | bytes 2097152 | tf_op jit(solution)/shard_map/all_to_all | solution.py:152
  13.3 0.0 copy-done
  13.4 3.5 %collective-permute-start = (bf16[2,256,128]{2,1,0:T(8,128)(2,1)S(1)}, bf16[2,256,128]{2,1,0:T(8,128)(2,1)S(1)}, u32[]{:S(2)}, u32[]{:S(2)}) collective-permute-start(bf16[2,256,128]{2,1,0:T(8,128)(2,1)S(1)} %copy-done), channel_id=1, source_target_pairs={{0,8},{8,16},{16,24},{24,32},{32,40},{40,48},{48,56},{56,64},{64,7... | collective-permute-start | bytes 393224 | tf_op jit(solution)/shard_map/ppermute | solution.py:22
  16.9 4.6 %collective-permute-start.1 = (bf16[2,256,128]{2,1,0:T(8,128)(2,1)S(1)}, bf16[2,256,128]{2,1,0:T(8,128)(2,1)S(1)}, u32[]{:S(2)}, u32[]{:S(2)}) collective-permute-start(bf16[2,256,128]{2,1,0:T(8,128)(2,1)S(1)} %copy-done), channel_id=1, source_target_pairs={{0,16},{8,24},{16,32},{24,40},{32,48},{40,56},{48,64},{56,72},{64,... | collective-permute-start | bytes 393224 | tf_op jit(solution)/shard_map/ppermute | solution.py:22
  21.5 0.0 collective-permute-done.one_ref
  21.5 4.2 %collective-permute-done.1.two_ref = bf16[2,256,128]{2,1,0:T(8,128)(2,1)S(1)} collective-permute-done((bf16[2,256,128]{2,1,0:T(8,128)(2,1)S(1)}, bf16[2,256,128]{2,1,0:T(8,128)(2,1)S(1)}, u32[]{:S(2)}, u32[]{:S(2)}) %collective-permute-start.1) | collective-permute-done | bytes 131104 | tf_op jit(solution)/shard_map/ppermute | solution.py:22
  25.7 6.3 %attention_backward.1 = (bf16[256,512]{1,0:T(8,128)(2,1)}, f32[2,256,128]{2,1,0:T(8,128)}, bf16[2,256,128]{2,1,0:T(8,128)(2,1)}, bf16[2,256,128]{2,1,0:T(8,128)(2,1)}) custom-call(s32[1,256]{1,0:T(1,128)} %bitcast.3, bf16[256,512]{1,0:T(8,128)(2,1)} %q_ref.1, bf16[256,512]{1,0:T(8,128)(2,1)} %o_ref.1, bf16[256,512]{1,0:T(8,128)(2,1)} %g_ref.1, ...), custom_call_target="tpu_custom_call" | custom-call | tf_op jit(solution)/shard_map/attention_backward/pallas_call | solution.py:82
  32.0 4.1 %collective-permute-start.5 = (bf16[256,512]{1,0:T(8,128)(2,1)}, bf16[256,512]{1,0:T(8,128)(2,1)S(1)}, u32[]{:S(2)}, u32[]{:S(2)}) collective-permute-start(bf16[256,512]{1,0:T(8,128)(2,1)} %get-tuple-element.4.own_ref), channel_id=1, source_target_pairs={{0,16},{16,0},{1,17},{17,1},{2,18},{18,2},{3,19},{19,3},{4,20},{20... | collective-permute-start | bytes 786440 | tf_op jit(solution)/shard_map/ppermute | solution.py:158
  36.2 1.9 %collective-permute-start.4 = (bf16[256,512]{1,0:T(8,128)(2,1)}, bf16[256,512]{1,0:T(8,128)(2,1)S(1)}, u32[]{:S(2)}, u32[]{:S(2)}) collective-permute-start(bf16[256,512]{1,0:T(8,128)(2,1)} %get-tuple-element.4.own_ref), channel_id=1, source_target_pairs={{0,8},{8,0},{1,9},{9,1},{2,10},{10,2},{3,11},{11,3},{4,12},{12,4},... | collective-permute-start | bytes 786440 | tf_op jit(solution)/shard_map/ppermute | solution.py:159
  38.1 5.8 %collective-permute-done.5.beyond_ref = bf16[256,512]{1,0:T(8,128)(2,1)S(1)} collective-permute-done((bf16[256,512]{1,0:T(8,128)(2,1)}, bf16[256,512]{1,0:T(8,128)(2,1)S(1)}, u32[]{:S(2)}, u32[]{:S(2)}) %collective-permute-start.5) | collective-permute-done | bytes 262176 | tf_op jit(solution)/shard_map/ppermute | solution.py:158
  43.8 2.0 %collective-permute-start.6 = (bf16[256,512]{1,0:T(8,128)(2,1)S(1)}, bf16[256,512]{1,0:T(8,128)(2,1)S(1)}, u32[]{:S(2)}, u32[]{:S(2)}) collective-permute-start(bf16[256,512]{1,0:T(8,128)(2,1)S(1)} %collective-permute-done.5.beyond_ref), channel_id=1, source_target_pairs={{0,8},{8,0},{1,9},{9,1},{2,10},{10,2},{3,11},{11,3},{4,12},{12,4},... | collective-permute-start | bytes 786440 | tf_op jit(solution)/shard_map/ppermute | solution.py:160
  45.9 0.0 collective-permute-done.4.beside_ref
  45.9 1.4 %collective-permute-done.6.across_ref = bf16[256,512]{1,0:T(8,128)(2,1)S(1)} collective-permute-done((bf16[256,512]{1,0:T(8,128)(2,1)S(1)}, bf16[256,512]{1,0:T(8,128)(2,1)S(1)}, u32[]{:S(2)}, u32[]{:S(2)}) %collective-permute-start.6) | collective-permute-done | bytes 262176 | tf_op jit(solution)/shard_map/ppermute | solution.py:160
  47.3 0.0 all-to-all-done
  47.3 2.2 %weight_term.1 = bf16[16,32,512]{2,1,0:T(8,128)(2,1)} custom-call(bf16[4,8,64,256]{3,2,1,0:T(8,128)(2,1)S(1)} %bitcast.2, bf16[256,512]{1,0:T(8,128)(2,1)} %get-tuple-element.4.own_ref, bf16[256,512]{1,0:T(8,128)(2,1)S(1)} %collective-permute-done.4.beside_ref, bf16[256,512]{1,0:T(8,128)(2,1)S(1)} %collective-permute-done.5.beyond_ref, ...), custom_call_target="tpu_custom_call" | custom-call | tf_op jit(solution)/shard_map/weight_term/pallas_call | solution.py:139
  49.5 0.0 copy-start.3
  49.5 0.0 copy-start.2
  49.5 0.0 copy-start.1
  49.5 12.7 %all-to-all-start.1 = ((bf16[16,32,512]{2,1,0:T(8,128)(2,1)}), bf16[16,32,512]{2,1,0:T(8,128)(2,1)S(1)}, u32[]{:S(2)}, u32[]{:S(2)}) async-start(bf16[16,32,512]{2,1,0:T(8,128)(2,1)} %weight_term.1), calls=%async_computation.1 | async-start | bytes 1048576 | tf_op jit(solution)/shard_map/all_to_all | solution.py:166
  62.3 0.0 copy-done.3
  62.3 1.3 %collective-permute-start.3 = (bf16[2,256,128]{2,1,0:T(8,128)(2,1)S(1)}, bf16[2,256,128]{2,1,0:T(8,128)(2,1)S(1)}, u32[]{:S(2)}, u32[]{:S(2)}) collective-permute-start(bf16[2,256,128]{2,1,0:T(8,128)(2,1)S(1)} %copy-done.3), channel_id=1, source_target_pairs={{16,0},{24,8},{32,16},{40,24},{48,32},{56,40},{64,48},{72,56},{80,... | collective-permute-start | bytes 393224 | tf_op jit(solution)/shard_map/ppermute | solution.py:22
  63.6 0.0 copy-done.2
  63.6 2.6 %collective-permute-start.2 = (bf16[2,256,128]{2,1,0:T(8,128)(2,1)S(1)}, bf16[2,256,128]{2,1,0:T(8,128)(2,1)S(1)}, u32[]{:S(2)}, u32[]{:S(2)}) collective-permute-start(bf16[2,256,128]{2,1,0:T(8,128)(2,1)S(1)} %copy-done.2), channel_id=1, source_target_pairs={{8,0},{16,8},{24,16},{32,24},{40,32},{48,40},{56,48},{64,56},{72,6... | collective-permute-start | bytes 393224 | tf_op jit(solution)/shard_map/ppermute | solution.py:22
  66.2 11.4 %collective-permute-done.3 = bf16[2,256,128]{2,1,0:T(8,128)(2,1)S(1)} collective-permute-done((bf16[2,256,128]{2,1,0:T(8,128)(2,1)S(1)}, bf16[2,256,128]{2,1,0:T(8,128)(2,1)S(1)}, u32[]{:S(2)}, u32[]{:S(2)}) %collective-permute-start.3) | collective-permute-done | bytes 131104 | tf_op jit(solution)/shard_map/ppermute | solution.py:22
  77.5 2.2 %collective-permute-done.2 = bf16[2,256,128]{2,1,0:T(8,128)(2,1)S(1)} collective-permute-done((bf16[2,256,128]{2,1,0:T(8,128)(2,1)S(1)}, bf16[2,256,128]{2,1,0:T(8,128)(2,1)S(1)}, u32[]{:S(2)}, u32[]{:S(2)}) %collective-permute-start.2) | collective-permute-done | bytes 131104 | tf_op jit(solution)/shard_map/ppermute | solution.py:22
  79.8 0.0 copy-done.1
  79.8 0.7 add_convert_fusion
  80.5 0.0 all-to-all-done.1
  80.5 0.7 convert_reduce_fusion
Async XLA Ops:
  2.6 10.7 %copy-start = (bf16[2,256,128]{2,1,0:T(8,128)(2,1)S(1)}, bf16[2,256,128]{2,1,0:T(8,128)(2,1)}, u32[]{:S(2)}) copy-start(bf16[2,256,128]{2,1,0:T(8,128)(2,1)} %near_ref.1) | copy-start | bytes 393220
  2.6 44.6 %all-to-all-start = ((bf16[32,64,256]{2,1,0:T(8,128)(2,1)}), bf16[32,64,256]{2,1,0:T(8,128)(2,1)S(1)}, u32[]{:S(2)}, u32[]{:S(2)}) async-start(bf16[32,64,256]{2,1,0:T(8,128)(2,1)} %feature_copies.1), calls=%async_computation | async-start | bytes 2097152 | tf_op jit(solution)/shard_map/all_to_all | solution.py:152
  13.4 8.1 %collective-permute-start = (bf16[2,256,128]{2,1,0:T(8,128)(2,1)S(1)}, bf16[2,256,128]{2,1,0:T(8,128)(2,1)S(1)}, u32[]{:S(2)}, u32[]{:S(2)}) collective-permute-start(bf16[2,256,128]{2,1,0:T(8,128)(2,1)S(1)} %copy-done), channel_id=1, source_target_pairs={{0,8},{8,16},{16,24},{24,32},{32,40},{40,48},{48,56},{56,64},{64,7... | collective-permute-start | bytes 393224 | tf_op jit(solution)/shard_map/ppermute | solution.py:22
  16.9 8.8 %collective-permute-start.1 = (bf16[2,256,128]{2,1,0:T(8,128)(2,1)S(1)}, bf16[2,256,128]{2,1,0:T(8,128)(2,1)S(1)}, u32[]{:S(2)}, u32[]{:S(2)}) collective-permute-start(bf16[2,256,128]{2,1,0:T(8,128)(2,1)S(1)} %copy-done), channel_id=1, source_target_pairs={{0,16},{8,24},{16,32},{24,40},{32,48},{40,56},{48,64},{56,72},{64,... | collective-permute-start | bytes 393224 | tf_op jit(solution)/shard_map/ppermute | solution.py:22
  32.0 11.8 %collective-permute-start.5 = (bf16[256,512]{1,0:T(8,128)(2,1)}, bf16[256,512]{1,0:T(8,128)(2,1)S(1)}, u32[]{:S(2)}, u32[]{:S(2)}) collective-permute-start(bf16[256,512]{1,0:T(8,128)(2,1)} %get-tuple-element.4.own_ref), channel_id=1, source_target_pairs={{0,16},{16,0},{1,17},{17,1},{2,18},{18,2},{3,19},{19,3},{4,20},{20... | collective-permute-start | bytes 786440 | tf_op jit(solution)/shard_map/ppermute | solution.py:158
  36.2 9.7 %collective-permute-start.4 = (bf16[256,512]{1,0:T(8,128)(2,1)}, bf16[256,512]{1,0:T(8,128)(2,1)S(1)}, u32[]{:S(2)}, u32[]{:S(2)}) collective-permute-start(bf16[256,512]{1,0:T(8,128)(2,1)} %get-tuple-element.4.own_ref), channel_id=1, source_target_pairs={{0,8},{8,0},{1,9},{9,1},{2,10},{10,2},{3,11},{11,3},{4,12},{12,4},... | collective-permute-start | bytes 786440 | tf_op jit(solution)/shard_map/ppermute | solution.py:159
  43.8 3.4 %collective-permute-start.6 = (bf16[256,512]{1,0:T(8,128)(2,1)S(1)}, bf16[256,512]{1,0:T(8,128)(2,1)S(1)}, u32[]{:S(2)}, u32[]{:S(2)}) collective-permute-start(bf16[256,512]{1,0:T(8,128)(2,1)S(1)} %collective-permute-done.5.beyond_ref), channel_id=1, source_target_pairs={{0,8},{8,0},{1,9},{9,1},{2,10},{10,2},{3,11},{11,3},{4,12},{12,4},... | collective-permute-start | bytes 786440 | tf_op jit(solution)/shard_map/ppermute | solution.py:160
  49.5 12.8 %copy-start.3 = (bf16[2,256,128]{2,1,0:T(8,128)(2,1)S(1)}, bf16[2,256,128]{2,1,0:T(8,128)(2,1)}, u32[]{:S(2)}) copy-start(bf16[2,256,128]{2,1,0:T(8,128)(2,1)} %get-tuple-element.10) | copy-start | bytes 393220
  49.5 14.1 %copy-start.2 = (bf16[2,256,128]{2,1,0:T(8,128)(2,1)S(1)}, bf16[2,256,128]{2,1,0:T(8,128)(2,1)}, u32[]{:S(2)}) copy-start(bf16[2,256,128]{2,1,0:T(8,128)(2,1)} %get-tuple-element.9) | copy-start | bytes 393220
  49.5 30.2 %copy-start.1 = (f32[2,256,128]{2,1,0:T(8,128)S(1)}, f32[2,256,128]{2,1,0:T(8,128)}, u32[]{:S(2)}) copy-start(f32[2,256,128]{2,1,0:T(8,128)} %get-tuple-element.8) | copy-start | bytes 786436
  49.5 30.9 %all-to-all-start.1 = ((bf16[16,32,512]{2,1,0:T(8,128)(2,1)}), bf16[16,32,512]{2,1,0:T(8,128)(2,1)S(1)}, u32[]{:S(2)}, u32[]{:S(2)}) async-start(bf16[16,32,512]{2,1,0:T(8,128)(2,1)} %weight_term.1), calls=%async_computation.1 | async-start | bytes 1048576 | tf_op jit(solution)/shard_map/all_to_all | solution.py:166
  62.3 15.2 %collective-permute-start.3 = (bf16[2,256,128]{2,1,0:T(8,128)(2,1)S(1)}, bf16[2,256,128]{2,1,0:T(8,128)(2,1)S(1)}, u32[]{:S(2)}, u32[]{:S(2)}) collective-permute-start(bf16[2,256,128]{2,1,0:T(8,128)(2,1)S(1)} %copy-done.3), channel_id=1, source_target_pairs={{16,0},{24,8},{32,16},{40,24},{48,32},{56,40},{64,48},{72,56},{80,... | collective-permute-start | bytes 393224 | tf_op jit(solution)/shard_map/ppermute | solution.py:22
  63.6 16.2 %collective-permute-start.2 = (bf16[2,256,128]{2,1,0:T(8,128)(2,1)S(1)}, bf16[2,256,128]{2,1,0:T(8,128)(2,1)S(1)}, u32[]{:S(2)}, u32[]{:S(2)}) collective-permute-start(bf16[2,256,128]{2,1,0:T(8,128)(2,1)S(1)} %copy-done.2), channel_id=1, source_target_pairs={{8,0},{16,8},{24,16},{32,24},{40,32},{48,40},{56,48},{64,56},{72,6... | collective-permute-start | bytes 393224 | tf_op jit(solution)/shard_map/ppermute | solution.py:22
